TPU v7x, 32 devices: a whole 2x2x4 slice. The times are simulated.
32 devices in a mesh: field: 2 (over x), gx: 4 (over z), gy: 4 (over y, core).
Axes of the slice: x: 2, y: 2, z: 4, core: 2. Of those that a mesh axis runs over, the one named last changes fastest.
Arguments:
- concentrations: float32 [2, 16, 16, 32, 128], P('field', None, 'gx', 'gy'), may hold values from 0 to 2
- velocity: float32 [3, 16, 32, 128], P(None, 'gx', 'gy'), may hold values from -0.3 to 0.3
- diffusivity: float32 [16, 32, 128], P('gx', 'gy'), may hold values from 0.02 to 0.12
- wiener: float32 [2, 3, 2, 16, 32, 128], P(None, None, 'field', 'gx', 'gy'), may hold values from -1.8 to 1.8
- mix_rate: float32 [16, 32, 128], P('gx', 'gy'), may hold values from 0.2 to 2
- rate_constants: float32 [64], replicated, may hold values from 0.1 to 1
- reactions: int32 [64, 4], replicated, may hold values from 0 to 15
Outputs:
- advanced: float32 [2, 16, 16, 32, 128], P('field', None, 'gx', 'gy')
Inputs may be any that keep to these rules, and one draw needn't show every extreme that they name: `reactions`: each row names two reactant and two product scalars.
All inputs are finite; a program needn't handle non-finite values.
Results may differ from a plain program's by a relative error of at most 0.0001.
Values sent between devices are 32-bit elements; how exact they have to be, the bound alone decides.
No kernel may reach another device: no remote copies, remote signals or barrier semaphores. Data moves between devices by JAX's collectives and lax.ppermute only.
A program may use at most 64 MiB of HBM per device.

v0:
```python
import jax
import jax.numpy as jnp
from jax import lax
from jax.sharding import PartitionSpec as P

SUBSTEPS = 12
STEPS = 2


chem_step = 0.04
highest = lax.Precision.HIGHEST


def padded_2(block, sides, width):
    for axis, dim in sides:
        count = lax.axis_size(axis)
        forward = [(i, i + 1) for i in range(count - 1)]
        backward = [(target, source) for source, target in forward]
        low = lax.ppermute(
            lax.slice_in_dim(block, block.shape[dim] - width, None, axis=dim), axis, forward
        )
        high = lax.ppermute(lax.slice_in_dim(block, 0, width, axis=dim), axis, backward)
        block = jnp.concatenate([low, block, high], axis=dim)
    return block


def tables(reactions, count):
    scalar_ids = jnp.arange(count, dtype=jnp.int32)[None, :]
    react = (reactions[:, 0:1] == scalar_ids).astype(jnp.float32) + (
        reactions[:, 1:2] == scalar_ids
    ).astype(jnp.float32)
    produce = (reactions[:, 2:3] == scalar_ids).astype(jnp.float32) + (
        reactions[:, 3:4] == scalar_ids
    ).astype(jnp.float32)
    return (react, (produce - react).T)


def neighbours(values):
    middle = (slice(1, -1), slice(1, -1), slice(1, -1))
    leading = (slice(None),) * (values.ndim - 3)
    result = []
    for dim_index in range(3):
        upper_cut = list(middle)
        upper_cut[dim_index] = slice(2, None)
        lower_cut = list(middle)
        lower_cut[dim_index] = slice(0, -2)
        result.append((values[leading + tuple(upper_cut)], values[leading + tuple(lower_cut)]))
    return result


def transport(padded, gamma_pad, gamma, velocity, increments):
    centre = padded[:, 1:-1, 1:-1, 1:-1]
    pairs = neighbours(padded)
    gamma_pairs = neighbours(gamma_pad)
    noise_amp = jnp.sqrt(2.0 * gamma)
    change = jnp.zeros_like(centre)
    for dim_index in range(3):
        upward, downward = pairs[dim_index]
        gamma_up, gamma_down = gamma_pairs[dim_index]
        change = (
            change
            + 0.5 * (gamma + gamma_up) * (upward - centre)
            + 0.5 * (gamma + gamma_down) * (downward - centre)
        )
        change = change + (noise_amp * increments[dim_index] - velocity[dim_index]) * (
            0.5 * (upward - downward)
        )
    return centre + change


def chemistry(values, react, net_t, rate_constants):

    def substep(index, conc):
        logs = jnp.log(jax.nn.softplus(conc))
        flux = rate_constants[:, None] * jnp.exp(jnp.dot(react, logs, precision=highest))
        return conc + chem_step * jnp.dot(net_t, flux, precision=highest)

    return lax.fori_loop(0, SUBSTEPS, substep, values)


def closure(first, second, count, mix_rate):
    mean = first / count
    meansq = second / count
    spread = jnp.sum(meansq - mean * mean, axis=0)
    energy = jnp.sum(meansq, axis=0)
    omega = mix_rate * (1.0 + spread / (1.0 + energy))
    return (mean, jnp.exp(-0.5 * omega))


def on_device(concentrations, velocity, diffusivity, wiener, mix_rate, rate_constants, reactions):
    conc = concentrations[0]
    scalars = conc.shape[0]
    react, net_t = tables(reactions, scalars)
    count = lax.axis_size("field")
    gamma_rim = padded_2(diffusivity, (("gx", 0), ("gy", 1)), 1)
    gamma_pad = jnp.pad(gamma_rim, ((0, 0), (0, 0), (1, 1)))
    for step_index in range(STEPS):
        rimmed = padded_2(conc, (("gx", 1), ("gy", 2)), 1)
        padded = jnp.pad(rimmed, ((0, 0), (0, 0), (0, 0), (1, 1)))
        moved = transport(padded, gamma_pad, diffusivity, velocity, wiener[step_index, :, 0])
        conc = chemistry(moved.reshape(scalars, -1), react, net_t, rate_constants).reshape(
            moved.shape
        )
        every = lax.all_gather(conc[None], "field", axis=0, tiled=True)
        first = jnp.sum(every, axis=0)
        second = jnp.sum(every * every, axis=0)
        mean, decay = closure(first, second, count, mix_rate)
        conc = mean + (conc - mean) * decay
    return conc[None]


def solution(mesh):
    return jax.shard_map(
        on_device,
        mesh=mesh,
        in_specs=(
            P("field", None, "gx", "gy", None),
            P(None, "gx", "gy", None),
            P("gx", "gy", None),
            P(None, None, "field", "gx", "gy", None),
            P("gx", "gy", None),
            P(),
            P(),
        ),
        out_specs=P("field", None, "gx", "gy", None),
        check_vma=False,
    )
```

profile of v0, /device:TPU:0, one launch (start us, length us, event | category | flops | bytes accessed | tf_op | source)
XLA Modules:
  0.0 195.9 jit_solution(17820845344473216672)
XLA Ops:
  2.0 5.6 %collective-permute-start.2 = (f32[1,8,128]{2,1,0:T(8,128)S(1)}, f32[1,8,128]{2,1,0:T(8,128)S(1)}, u32[]{:S(2)}, u32[]{:S(2)}) collective-permute-start(f32[1,8,128]{2,1,0:T(8,128)S(1)} %get-tuple-element.219), channel_id=1, source_target_pairs={{0,4},{4,8},{8,12},{1,5},{5,9},{9,13},{2,6},{6,10},{10,14},{3,7},{... | collective-permute-start | bytes 12296 | tf_op jit(solution)/shard_map/ppermute | solution.py:19
  9.8 4.6 %collective-permute-start.3 = (f32[16,1,8,128]{3,2,1,0:T(8,128)S(1)}, f32[16,1,8,128]{3,2,1,0:T(8,128)S(1)}, u32[]{:S(2)}, u32[]{:S(2)}) collective-permute-start(f32[16,1,8,128]{3,2,1,0:T(8,128)S(1)} %get-tuple-element.200), channel_id=1, source_target_pairs={{0,4},{4,8},{8,12},{1,5},{5,9},{9,13},{2,6},{6,10},{10,14},{3,7},{... | collective-permute-start | bytes 196616 | tf_op jit(solution)/shard_map/ppermute | solution.py:19
  23.1 4.3 %collective-permute-start.7 = (f32[16,6,1,128]{3,2,1,0:T(1,128)S(1)}, f32[16,6,1,128]{3,2,1,0:T(1,128)S(1)}, u32[]{:S(2)}, u32[]{:S(2)}) collective-permute-start(f32[16,6,1,128]{3,2,1,0:T(1,128)S(1)} %get-tuple-element.195), channel_id=1, source_target_pairs={{0,1},{1,2},{2,3},{4,5},{5,6},{6,7},{8,9},{9,10},{10,11},{12,13},{... | collective-permute-start | bytes 147464 | tf_op jit(solution)/shard_map/ppermute | solution.py:19
  32.0 65.5 %while.24 = (s32[]{:T(128)}, f32[16,4096]{1,0:T(8,128)S(1)}, f32[64]{0:T(128)S(1)}, s32[64]{0:T(128)S(1)}, s32[64]{0:T(128)S(1)}, /*index=5*/s32[64]{0:T(128)S(1)}, s32[64]{0:T(128)S(1)}, s32[]{:T(128)}) while((s32[]{:T(128)}, f32[16,4096]{1,0:T(8,128)S(1)}, f32[64]{0:T(128)S(1)}, s32[64]{0:T(128)S(1)}, ...), condition=%wide.region_1.2_spmd.clone.clone, body=%wide.region_0.1_spmd.clone.clone.sunk | while | flops 101466112 | bytes 2885461 | solution.py:78
  32.0 3.5 %fusion.140 = f32[4096,64]{1,0:T(8,128)S(1)} fusion(f32[64]{0:T(128)S(1)} %get-tuple-element.328, f32[16,4096]{1,0:T(8,128)S(1)} %get-tuple-element.319, s32[64]{0:T(128)S(1)} %get-tuple-element.330, s32[64]{0:T(128)S(1)} %get-tuple-element.329), kind=kOutput, calls=%fused_computation.5.clone.1 | convolution fusion | flops 50992128 | bytes 1311488 | tf_op jit(solution)/shard_map/while/body/eval_jaxpr/dot_general | solution.py:75
  37.5 3.5 %fusion.140 = f32[4096,64]{1,0:T(8,128)S(1)} fusion(f32[64]{0:T(128)S(1)} %get-tuple-element.328, f32[16,4096]{1,0:T(8,128)S(1)} %get-tuple-element.319, s32[64]{0:T(128)S(1)} %get-tuple-element.330, s32[64]{0:T(128)S(1)} %get-tuple-element.329), kind=kOutput, calls=%fused_computation.5.clone.1 | convolution fusion | flops 50992128 | bytes 1311488 | tf_op jit(solution)/shard_map/while/body/eval_jaxpr/dot_general | solution.py:75
  42.9 3.5 %fusion.140 = f32[4096,64]{1,0:T(8,128)S(1)} fusion(f32[64]{0:T(128)S(1)} %get-tuple-element.328, f32[16,4096]{1,0:T(8,128)S(1)} %get-tuple-element.319, s32[64]{0:T(128)S(1)} %get-tuple-element.330, s32[64]{0:T(128)S(1)} %get-tuple-element.329), kind=kOutput, calls=%fused_computation.5.clone.1 | convolution fusion | flops 50992128 | bytes 1311488 | tf_op jit(solution)/shard_map/while/body/eval_jaxpr/dot_general | solution.py:75
  48.4 3.5 %fusion.140 = f32[4096,64]{1,0:T(8,128)S(1)} fusion(f32[64]{0:T(128)S(1)} %get-tuple-element.328, f32[16,4096]{1,0:T(8,128)S(1)} %get-tuple-element.319, s32[64]{0:T(128)S(1)} %get-tuple-element.330, s32[64]{0:T(128)S(1)} %get-tuple-element.329), kind=kOutput, calls=%fused_computation.5.clone.1 | convolution fusion | flops 50992128 | bytes 1311488 | tf_op jit(solution)/shard_map/while/body/eval_jaxpr/dot_general | solution.py:75
  53.9 3.5 %fusion.140 = f32[4096,64]{1,0:T(8,128)S(1)} fusion(f32[64]{0:T(128)S(1)} %get-tuple-element.328, f32[16,4096]{1,0:T(8,128)S(1)} %get-tuple-element.319, s32[64]{0:T(128)S(1)} %get-tuple-element.330, s32[64]{0:T(128)S(1)} %get-tuple-element.329), kind=kOutput, calls=%fused_computation.5.clone.1 | convolution fusion | flops 50992128 | bytes 1311488 | tf_op jit(solution)/shard_map/while/body/eval_jaxpr/dot_general | solution.py:75
  59.3 3.5 %fusion.140 = f32[4096,64]{1,0:T(8,128)S(1)} fusion(f32[64]{0:T(128)S(1)} %get-tuple-element.328, f32[16,4096]{1,0:T(8,128)S(1)} %get-tuple-element.319, s32[64]{0:T(128)S(1)} %get-tuple-element.330, s32[64]{0:T(128)S(1)} %get-tuple-element.329), kind=kOutput, calls=%fused_computation.5.clone.1 | convolution fusion | flops 50992128 | bytes 1311488 | tf_op jit(solution)/shard_map/while/body/eval_jaxpr/dot_general | solution.py:75
  64.8 3.5 %fusion.140 = f32[4096,64]{1,0:T(8,128)S(1)} fusion(f32[64]{0:T(128)S(1)} %get-tuple-element.328, f32[16,4096]{1,0:T(8,128)S(1)} %get-tuple-element.319, s32[64]{0:T(128)S(1)} %get-tuple-element.330, s32[64]{0:T(128)S(1)} %get-tuple-element.329), kind=kOutput, calls=%fused_computation.5.clone.1 | convolution fusion | flops 50992128 | bytes 1311488 | tf_op jit(solution)/shard_map/while/body/eval_jaxpr/dot_general | solution.py:75
  70.2 3.5 %fusion.140 = f32[4096,64]{1,0:T(8,128)S(1)} fusion(f32[64]{0:T(128)S(1)} %get-tuple-element.328, f32[16,4096]{1,0:T(8,128)S(1)} %get-tuple-element.319, s32[64]{0:T(128)S(1)} %get-tuple-element.330, s32[64]{0:T(128)S(1)} %get-tuple-element.329), kind=kOutput, calls=%fused_computation.5.clone.1 | convolution fusion | flops 50992128 | bytes 1311488 | tf_op jit(solution)/shard_map/while/body/eval_jaxpr/dot_general | solution.py:75
  75.7 3.5 %fusion.140 = f32[4096,64]{1,0:T(8,128)S(1)} fusion(f32[64]{0:T(128)S(1)} %get-tuple-element.328, f32[16,4096]{1,0:T(8,128)S(1)} %get-tuple-element.319, s32[64]{0:T(128)S(1)} %get-tuple-element.330, s32[64]{0:T(128)S(1)} %get-tuple-element.329), kind=kOutput, calls=%fused_computation.5.clone.1 | convolution fusion | flops 50992128 | bytes 1311488 | tf_op jit(solution)/shard_map/while/body/eval_jaxpr/dot_general | solution.py:75
  81.2 3.5 %fusion.140 = f32[4096,64]{1,0:T(8,128)S(1)} fusion(f32[64]{0:T(128)S(1)} %get-tuple-element.328, f32[16,4096]{1,0:T(8,128)S(1)} %get-tuple-element.319, s32[64]{0:T(128)S(1)} %get-tuple-element.330, s32[64]{0:T(128)S(1)} %get-tuple-element.329), kind=kOutput, calls=%fused_computation.5.clone.1 | convolution fusion | flops 50992128 | bytes 1311488 | tf_op jit(solution)/shard_map/while/body/eval_jaxpr/dot_general | solution.py:75
  86.6 3.5 %fusion.140 = f32[4096,64]{1,0:T(8,128)S(1)} fusion(f32[64]{0:T(128)S(1)} %get-tuple-element.328, f32[16,4096]{1,0:T(8,128)S(1)} %get-tuple-element.319, s32[64]{0:T(128)S(1)} %get-tuple-element.330, s32[64]{0:T(128)S(1)} %get-tuple-element.329), kind=kOutput, calls=%fused_computation.5.clone.1 | convolution fusion | flops 50992128 | bytes 1311488 | tf_op jit(solution)/shard_map/while/body/eval_jaxpr/dot_general | solution.py:75
  92.1 3.5 %fusion.140 = f32[4096,64]{1,0:T(8,128)S(1)} fusion(f32[64]{0:T(128)S(1)} %get-tuple-element.328, f32[16,4096]{1,0:T(8,128)S(1)} %get-tuple-element.319, s32[64]{0:T(128)S(1)} %get-tuple-element.330, s32[64]{0:T(128)S(1)} %get-tuple-element.329), kind=kOutput, calls=%fused_computation.5.clone.1 | convolution fusion | flops 50992128 | bytes 1311488 | tf_op jit(solution)/shard_map/while/body/eval_jaxpr/dot_general | solution.py:75
  97.6 8.5 %all_gather.6 = f32[2,16,4,8,128]{4,3,2,1,0:T(8,128)S(1)} all-gather(f32[1,16,4,8,128]{4,3,2,1,0:T(8,128)S(1)} %bitcast.106), channel_id=1, replica_groups=mesh['field'=2,'gx'=4,'gy'=4] {'field'}, dimensions={0}, use_global_device_ids=true | all-gather | bytes 786432 | tf_op jit(solution)/shard_map/all_gather | solution.py:104
  107.7 4.5 %collective-permute-start.9 = (f32[16,1,8,128]{3,2,1,0:T(8,128)S(1)}, f32[16,1,8,128]{3,2,1,0:T(8,128)S(1)}, u32[]{:S(2)}, u32[]{:S(2)}) collective-permute-start(f32[16,1,8,128]{3,2,1,0:T(8,128)S(1)} %get-tuple-element.198), channel_id=1, source_target_pairs={{0,4},{4,8},{8,12},{1,5},{5,9},{9,13},{2,6},{6,10},{10,14},{3,7},{... | collective-permute-start | bytes 196616 | tf_op jit(solution)/shard_map/ppermute | solution.py:19
  121.2 65.5 %while.25 = (s32[]{:T(128)}, f32[16,4096]{1,0:T(8,128)S(1)}, f32[64]{0:T(128)S(1)}, s32[64]{0:T(128)S(1)}, s32[64]{0:T(128)S(1)}, /*index=5*/s32[64]{0:T(128)S(1)}, s32[64]{0:T(128)S(1)}, s32[]{:T(128)}) while((s32[]{:T(128)}, f32[16,4096]{1,0:T(8,128)S(1)}, f32[64]{0:T(128)S(1)}, s32[64]{0:T(128)S(1)}, ...), condition=%wide.region_7.8_spmd.clone.clone, body=%wide.region_6.7_spmd.clone.clone.sunk | while | flops 101466112 | bytes 2885461 | solution.py:78
  126.7 3.5 %fusion.146 = f32[4096,64]{1,0:T(8,128)S(1)} fusion(f32[64]{0:T(128)S(1)} %get-tuple-element.352, f32[16,4096]{1,0:T(8,128)S(1)} %get-tuple-element.343, s32[64]{0:T(128)S(1)} %get-tuple-element.354, s32[64]{0:T(128)S(1)} %get-tuple-element.353), kind=kOutput, calls=%fused_computation.42.clone.1 | convolution fusion | flops 50992128 | bytes 1311488 | tf_op jit(solution)/shard_map/while/body/eval_jaxpr/dot_general | solution.py:75
  143.1 3.5 %fusion.146 = f32[4096,64]{1,0:T(8,128)S(1)} fusion(f32[64]{0:T(128)S(1)} %get-tuple-element.352, f32[16,4096]{1,0:T(8,128)S(1)} %get-tuple-element.343, s32[64]{0:T(128)S(1)} %get-tuple-element.354, s32[64]{0:T(128)S(1)} %get-tuple-element.353), kind=kOutput, calls=%fused_computation.42.clone.1 | convolution fusion | flops 50992128 | bytes 1311488 | tf_op jit(solution)/shard_map/while/body/eval_jaxpr/dot_general | solution.py:75
  159.4 3.5 %fusion.146 = f32[4096,64]{1,0:T(8,128)S(1)} fusion(f32[64]{0:T(128)S(1)} %get-tuple-element.352, f32[16,4096]{1,0:T(8,128)S(1)} %get-tuple-element.343, s32[64]{0:T(128)S(1)} %get-tuple-element.354, s32[64]{0:T(128)S(1)} %get-tuple-element.353), kind=kOutput, calls=%fused_computation.42.clone.1 | convolution fusion | flops 50992128 | bytes 1311488 | tf_op jit(solution)/shard_map/while/body/eval_jaxpr/dot_general | solution.py:75
  175.8 3.5 %fusion.146 = f32[4096,64]{1,0:T(8,128)S(1)} fusion(f32[64]{0:T(128)S(1)} %get-tuple-element.352, f32[16,4096]{1,0:T(8,128)S(1)} %get-tuple-element.343, s32[64]{0:T(128)S(1)} %get-tuple-element.354, s32[64]{0:T(128)S(1)} %get-tuple-element.353), kind=kOutput, calls=%fused_computation.42.clone.1 | convolution fusion | flops 50992128 | bytes 1311488 | tf_op jit(solution)/shard_map/while/body/eval_jaxpr/dot_general | solution.py:75
  186.8 8.2 %all_gather.7 = f32[2,16,4,8,128]{4,3,2,1,0:T(8,128)S(1)} all-gather(f32[1,16,4,8,128]{4,3,2,1,0:T(8,128)S(1)} %bitcast.108), channel_id=1, replica_groups=mesh['field'=2,'gx'=4,'gy'=4] {'field'}, dimensions={0}, use_global_device_ids=true | all-gather | bytes 786432 | tf_op jit(solution)/shard_map/all_gather | solution.py:104
  (86 shorter events, 103.5 us)
Async XLA Ops:
  0.0 30.5 %copy-start = (f32[1,16,4,8,128]{4,3,2,1,0:T(8,128)S(1)}, f32[1,16,4,8,128]{4,3,2,1,0:T(8,128)}, u32[]{:S(2)}) copy-start(f32[1,16,4,8,128]{4,3,2,1,0:T(8,128)} %param.11) | copy-start | bytes 786436
  0.8 13.7 %collective-permute-start = (f32[1,8,128]{2,1,0:T(8,128)S(1)}, f32[1,8,128]{2,1,0:T(8,128)S(1)}, u32[]{:S(2)}, u32[]{:S(2)}) collective-permute-start(f32[1,8,128]{2,1,0:T(8,128)S(1)} %get-tuple-element.218), channel_id=1, source_target_pairs={{4,0},{8,4},{12,8},{5,1},{9,5},{13,9},{6,2},{10,6},{14,10},{7,3},{... | collective-permute-start | bytes 12296 | tf_op jit(solution)/shard_map/ppermute | solution.py:22
  2.0 12.3 %collective-permute-start.2 = (f32[1,8,128]{2,1,0:T(8,128)S(1)}, f32[1,8,128]{2,1,0:T(8,128)S(1)}, u32[]{:S(2)}, u32[]{:S(2)}) collective-permute-start(f32[1,8,128]{2,1,0:T(8,128)S(1)} %get-tuple-element.219), channel_id=1, source_target_pairs={{0,4},{4,8},{8,12},{1,5},{5,9},{9,13},{2,6},{6,10},{10,14},{3,7},{... | collective-permute-start | bytes 12296 | tf_op jit(solution)/shard_map/ppermute | solution.py:19
  8.5 13.5 %collective-permute-start.1 = (f32[16,1,8,128]{3,2,1,0:T(8,128)S(1)}, f32[16,1,8,128]{3,2,1,0:T(8,128)S(1)}, u32[]{:S(2)}, u32[]{:S(2)}) collective-permute-start(f32[16,1,8,128]{3,2,1,0:T(8,128)S(1)} %get-tuple-element.199), channel_id=1, source_target_pairs={{4,0},{8,4},{12,8},{5,1},{9,5},{13,9},{6,2},{10,6},{14,10},{7,3},{... | collective-permute-start | bytes 196616 | tf_op jit(solution)/shard_map/ppermute | solution.py:22
  9.8 12.2 %collective-permute-start.3 = (f32[16,1,8,128]{3,2,1,0:T(8,128)S(1)}, f32[16,1,8,128]{3,2,1,0:T(8,128)S(1)}, u32[]{:S(2)}, u32[]{:S(2)}) collective-permute-start(f32[16,1,8,128]{3,2,1,0:T(8,128)S(1)} %get-tuple-element.200), channel_id=1, source_target_pairs={{0,4},{4,8},{8,12},{1,5},{5,9},{9,13},{2,6},{6,10},{10,14},{3,7},{... | collective-permute-start | bytes 196616 | tf_op jit(solution)/shard_map/ppermute | solution.py:19
  15.3 3.4 %collective-permute-start.6 = (f32[6,1,128]{2,1,0:T(1,128)S(1)}, f32[6,1,128]{2,1,0:T(1,128)S(1)}, u32[]{:S(2)}, u32[]{:S(2)}) collective-permute-start(f32[6,1,128]{2,1,0:T(1,128)S(1)} %get-tuple-element.211), channel_id=1, source_target_pairs={{0,1},{1,2},{2,3},{4,5},{5,6},{6,7},{8,9},{9,10},{10,11},{12,13},{... | collective-permute-start | bytes 9224 | tf_op jit(solution)/shard_map/ppermute | solution.py:19
  16.6 5.2 %collective-permute-start.4 = (f32[6,1,128]{2,1,0:T(1,128)S(1)}, f32[6,1,128]{2,1,0:T(1,128)S(1)}, u32[]{:S(2)}, u32[]{:S(2)}) collective-permute-start(f32[6,1,128]{2,1,0:T(1,128)S(1)} %get-tuple-element.212), channel_id=1, source_target_pairs={{1,0},{2,1},{3,2},{5,4},{6,5},{7,6},{9,8},{10,9},{11,10},{13,12},{... | collective-permute-start | bytes 9224 | tf_op jit(solution)/shard_map/ppermute | solution.py:22
  23.1 6.4 %collective-permute-start.7 = (f32[16,6,1,128]{3,2,1,0:T(1,128)S(1)}, f32[16,6,1,128]{3,2,1,0:T(1,128)S(1)}, u32[]{:S(2)}, u32[]{:S(2)}) collective-permute-start(f32[16,6,1,128]{3,2,1,0:T(1,128)S(1)} %get-tuple-element.195), channel_id=1, source_target_pairs={{0,1},{1,2},{2,3},{4,5},{5,6},{6,7},{8,9},{9,10},{10,11},{12,13},{... | collective-permute-start | bytes 147464 | tf_op jit(solution)/shard_map/ppermute | solution.py:19
  27.4 3.1 %collective-permute-start.5 = (f32[16,6,1,128]{3,2,1,0:T(1,128)S(1)}, f32[16,6,1,128]{3,2,1,0:T(1,128)S(1)}, u32[]{:S(2)}, u32[]{:S(2)}) collective-permute-start(f32[16,6,1,128]{3,2,1,0:T(1,128)S(1)} %get-tuple-element.196), channel_id=1, source_target_pairs={{1,0},{2,1},{3,2},{5,4},{6,5},{7,6},{9,8},{10,9},{11,10},{13,12},{... | collective-permute-start | bytes 147464 | tf_op jit(solution)/shard_map/ppermute | solution.py:22
  29.5 2.5 %copy-start.2 = (f32[64]{0:T(128)S(1)}, f32[64]{0:T(128)}, u32[]{:S(2)}) copy-start(f32[64]{0:T(128)} %param.16) | copy-start | bytes 772
  97.5 8.7 %copy-start.1 = (f32[4,8,128]{2,1,0:T(8,128)S(1)}, f32[4,8,128]{2,1,0:T(8,128)}, u32[]{:S(2)}) copy-start(f32[4,8,128]{2,1,0:T(8,128)} %param.15) | copy-start | bytes 49156
  106.4 6.7 %collective-permute-start.8 = (f32[16,1,8,128]{3,2,1,0:T(8,128)S(1)}, f32[16,1,8,128]{3,2,1,0:T(8,128)S(1)}, u32[]{:S(2)}, u32[]{:S(2)}) collective-permute-start(f32[16,1,8,128]{3,2,1,0:T(8,128)S(1)} %get-tuple-element.197), channel_id=1, source_target_pairs={{4,0},{8,4},{12,8},{5,1},{9,5},{13,9},{6,2},{10,6},{14,10},{7,3},{... | collective-permute-start | bytes 196616 | tf_op jit(solution)/shard_map/ppermute | solution.py:22
  107.7 7.0 %collective-permute-start.9 = (f32[16,1,8,128]{3,2,1,0:T(8,128)S(1)}, f32[16,1,8,128]{3,2,1,0:T(8,128)S(1)}, u32[]{:S(2)}, u32[]{:S(2)}) collective-permute-start(f32[16,1,8,128]{3,2,1,0:T(8,128)S(1)} %get-tuple-element.198), channel_id=1, source_target_pairs={{0,4},{4,8},{8,12},{1,5},{5,9},{9,13},{2,6},{6,10},{10,14},{3,7},{... | collective-permute-start | bytes 196616 | tf_op jit(solution)/shard_map/ppermute | solution.py:19
  114.7 3.4 %collective-permute-start.11 = (f32[16,6,1,128]{3,2,1,0:T(1,128)S(1)}, f32[16,6,1,128]{3,2,1,0:T(1,128)S(1)}, u32[]{:S(2)}, u32[]{:S(2)}) collective-permute-start(f32[16,6,1,128]{3,2,1,0:T(1,128)S(1)} %get-tuple-element.193), channel_id=1, source_target_pairs={{0,1},{1,2},{2,3},{4,5},{5,6},{6,7},{8,9},{9,10},{10,11},{12,13},{... | collective-permute-start | bytes 147464 | tf_op jit(solution)/shard_map/ppermute | solution.py:19
  116.6 3.1 %collective-permute-start.10 = (f32[16,6,1,128]{3,2,1,0:T(1,128)S(1)}, f32[16,6,1,128]{3,2,1,0:T(1,128)S(1)}, u32[]{:S(2)}, u32[]{:S(2)}) collective-permute-start(f32[16,6,1,128]{3,2,1,0:T(1,128)S(1)} %get-tuple-element.194), channel_id=1, source_target_pairs={{1,0},{2,1},{3,2},{5,4},{6,5},{7,6},{9,8},{10,9},{11,10},{13,12},{... | collective-permute-start | bytes 147464 | tf_op jit(solution)/shard_map/ppermute | solution.py:22
where the time goes:
time: 198 us; the launch traced here: 196 us
  matrix products  130 us (66%)
  starting transfers between devices  30.1 us (15%)
  blocking collectives  16.7 us (8%)
  waiting for transfers between devices  8.18 us (4%)
  other arithmetic  6.65 us (3%)
  local copies, waits for them, and re-layouts  2.92 us (1%)
    dot_general x24, matrix products, substep(): jnp.dot(react, logs, precision=highest)  83.5 us
    dot_general x24, matrix products, substep(): return conc + chem_step * jnp.dot(net_t, flux, precision=highest)  46.8 us
    ppermute x6, starting transfers between devices, padded_2(): lax.ppermute(lax.slice_in_dim(block, block.shape[dim] - width, None, axis...  22.2 us
    all_gather x2, blocking collectives, on_device(): every = lax.all_gather(conc[None], 'field', axis=0, tiled=True)  16.7 us
    ppermute x6, starting transfers between devices, padded_2(): lax.ppermute(lax.slice_in_dim(block, 0, width, axis=dim), axis, backward)  7.92 us
    ppermute x6, waiting for transfers between devices, padded_2(): lax.ppermute(lax.slice_in_dim(block, 0, width, axis=dim), axis, backward)  6.56 us
  transfers between devices with their start and end apart: 12, of which 5 were waited for; matrix products, arithmetic and copies ran while one was open for 2% of the time, Pallas kernels for 0%

commit v1 on v0

v1 whole, which is shorter than its diff:
```python
import functools

import jax
import jax.numpy as jnp
from jax import lax
from jax.experimental import pallas as pl
from jax.experimental.pallas import tpu as pltpu
from jax.sharding import PartitionSpec as P

SUBSTEPS = 12
STEPS = 2
CHEM_STEP = 0.04
LOG2E = 1.4426950408889634
LN2 = 0.6931471805599453
TILE = 256
VMEM = pl.BlockSpec(memory_space=pltpu.VMEM)


def roundup(n, m):
    return (n + m - 1) // m * m


def split(x):
    hi = x.astype(jnp.bfloat16)
    lo = (x - hi.astype(jnp.float32)).astype(jnp.bfloat16)
    return hi, lo


def faces_kernel(conc, gamma, reactions, rates, xlo, xhi, ylo, yhi, gather, scatter):
    ns, nx, ny, nz = conc.shape
    nr = reactions.shape[0]
    for s in range(ns):
        xlo[s] = conc[s, 0]
        xhi[s] = conc[s, nx - 1]
        ylo[s] = conc[s, :, 0, :]
        yhi[s] = conc[s, :, ny - 1, :]
    xlo[ns] = gamma[0]
    xhi[ns] = gamma[nx - 1]
    ylo[ns] = gamma[:, 0, :]
    yhi[ns] = gamma[:, ny - 1, :]
    lane = lax.broadcasted_iota(jnp.int32, (nr, 128), 1)
    scalar = lax.rem(lane, ns)
    part = lax.div(lane, ns)
    k = rates[...] * (CHEM_STEP * LN2)
    k_hi = k.astype(jnp.bfloat16).astype(jnp.float32)
    k_lo = k - k_hi
    first = jnp.where(scalar == reactions[:, 0:1], 1.0, 0.0)
    second = jnp.where(scalar == reactions[:, 1:2], 1.0, 0.0)
    weight = jnp.where(part < 2, k_hi, jnp.where(part == 2, k_lo, 0.0))
    gather[:nr, :] = (first * weight).astype(jnp.bfloat16)
    gather[nr:, :] = (second * jnp.where(part < 2, 1.0, 0.0)).astype(jnp.bfloat16)
    third = jnp.where(scalar == reactions[:, 2:3], 1.0, 0.0)
    fourth = jnp.where(scalar == reactions[:, 3:4], 1.0, 0.0)
    net = third + fourth - first - second
    scatter[...] = jnp.concatenate([net, net], axis=0).T[:ns].astype(jnp.bfloat16)


def step_kernel(
    conc, xlo, xhi, ylo, yhi, gamma, glox, ghix, gloy, ghiy, velocity, wiener, gather, scatter,
    out, rows, state
):
    ns, nx, ny, nz = conc.shape
    stride = rows.shape[0] // ns
    chunks = nx * ny
    lane = lax.broadcasted_iota(jnp.int32, (ny, nz), 1)
    sub = lax.broadcasted_iota(jnp.int32, (ny, nz), 0)
    is_top, is_bottom = sub == ny - 1, sub == 0

    def shifted(value, low, high):
        up = jnp.where(is_top, high, pltpu.roll(value, ny - 1, 0))
        down = jnp.where(is_bottom, low, pltpu.roll(value, 1, 0))
        return up, down

    for x in range(nx):
        g = gamma[x]
        amp = jnp.sqrt(2.0 * g)
        gx_up = ghix[ns] if x == nx - 1 else gamma[x + 1]
        gx_down = glox[ns] if x == 0 else gamma[x - 1]
        gy_up, gy_down = shifted(g, gloy[ns, x : x + 1, :], ghiy[ns, x : x + 1, :])
        gz_up = jnp.where(lane == nz - 1, 0.0, pltpu.roll(g, nz - 1, 1))
        gz_down = jnp.where(lane == 0, 0.0, pltpu.roll(g, 1, 1))
        coef = []
        total = jnp.zeros_like(g)
        for d, (gu, gd) in enumerate(((gx_up, gx_down), (gy_up, gy_down), (gz_up, gz_down))):
            drift = 0.5 * (amp * wiener[d, x] - velocity[d, x])
            cu = 0.5 * (g + gu) + drift
            cd = 0.5 * (g + gd) - drift
            total = total + 0.5 * (g + gu) + 0.5 * (g + gd)
            coef.append((cu, cd))
        centre = (1.0 - total) * LOG2E
        (xu, xd), (yu, yd), (zu, zd) = [(a * LOG2E, b * LOG2E) for a, b in coef]
        zu = jnp.where(lane == nz - 1, 0.0, zu)
        zd = jnp.where(lane == 0, 0.0, zd)
        for s in range(ns):
            p = conc[s, x]
            px_up = xhi[s] if x == nx - 1 else conc[s, x + 1]
            px_down = xlo[s] if x == 0 else conc[s, x - 1]
            py_up, py_down = shifted(p, ylo[s, x : x + 1, :], yhi[s, x : x + 1, :])
            pz_up = pltpu.roll(p, nz - 1, 1)
            pz_down = pltpu.roll(p, 1, 1)
            moved = (centre * p + (xu * px_up + xd * px_down)) + (
                (yu * py_up + yd * py_down) + (zu * pz_up + zd * pz_down)
            )
            rows[s * stride + x * ny : s * stride + (x + 1) * ny, :] = moved

    for j in range(chunks):
        state[:, j * nz : (j + 1) * nz] = rows[pl.ds(j, ns, stride=stride), :]

    table = gather[...]
    net = scatter[...]
    nr = table.shape[0] // 2
    depth = 3 * ns
    table = table[:, :depth]

    def substep(i, carry):
        for t in range(chunks * nz // TILE):
            u = state[:, t * TILE : (t + 1) * TILE]
            sp = jnp.maximum(u, jnp.log2(1.0 + jnp.exp2(jnp.minimum(u, 120.0))))
            hi, lo = split(sp)
            both = jnp.dot(
                table,
                jnp.concatenate([hi, lo, hi], axis=0),
                preferred_element_type=jnp.float32,
            )
            rate = both[:nr] * both[nr:]
            hi, lo = split(rate)
            change = jnp.dot(
                net, jnp.concatenate([hi, lo], axis=0), preferred_element_type=jnp.float32
            )
            state[:, t * TILE : (t + 1) * TILE] = u + change
        return carry

    lax.fori_loop(0, SUBSTEPS, substep, 0)

    for j in range(chunks):
        rows[pl.ds(j, ns, stride=stride), :] = state[:, j * nz : (j + 1) * nz] * LN2
    for s in range(ns):
        for x in range(nx):
            out[s, x] = rows[s * stride + x * ny : s * stride + (x + 1) * ny, :]


def mix_kernel(count, mine, other, mix_rate, out, *faces):
    ns, nx, ny, nz = mine.shape
    for x in range(nx):
        spread = jnp.zeros((ny, nz), jnp.float32)
        energy = jnp.zeros((ny, nz), jnp.float32)
        for s in range(ns):
            a, b = mine[s, x], other[s, x]
            mean = (a + b) * (1.0 / count)
            meansq = (a * a + b * b) * (1.0 / count)
            spread = spread + (meansq - mean * mean)
            energy = energy + meansq
        omega = mix_rate[x] * (1.0 + spread / (1.0 + energy))
        decay = jnp.exp(-0.5 * omega)
        for s in range(ns):
            a, b = mine[s, x], other[s, x]
            mean = (a + b) * (1.0 / count)
            new = mean + (a - mean) * decay
            out[s, x] = new
            if faces:
                xlo, xhi, ylo, yhi = faces
                if x == 0:
                    xlo[s] = new
                if x == nx - 1:
                    xhi[s] = new
                ylo[s, x : x + 1] = new[0:1]
                yhi[s, x : x + 1] = new[ny - 1 : ny]


def closure(first, second, count, mix_rate):
    mean = first / count
    meansq = second / count
    spread = jnp.sum(meansq - mean * mean, axis=0)
    energy = jnp.sum(meansq, axis=0)
    omega = mix_rate * (1.0 + spread / (1.0 + energy))
    return (mean, jnp.exp(-0.5 * omega))


def shape_of(*dims, dtype=jnp.float32):
    return jax.ShapeDtypeStruct(dims, dtype)


def exchange(xlo, xhi, ylo, yhi):
    nx, ny = lax.axis_size("gx"), lax.axis_size("gy")
    up = lambda n: [(i, i + 1) for i in range(n - 1)]
    down = lambda n: [(i + 1, i) for i in range(n - 1)]
    from_below = lax.ppermute(xhi, "gx", up(nx))
    from_above = lax.ppermute(xlo, "gx", down(nx))
    from_left = lax.ppermute(yhi, "gy", up(ny))
    from_right = lax.ppermute(ylo, "gy", down(ny))
    return from_below, from_above, from_left, from_right


def on_device(concentrations, velocity, diffusivity, wiener, mix_rate, rate_constants, reactions):
    conc = concentrations[0]
    ns, nx, ny, nz = conc.shape
    nr = reactions.shape[0]
    count = lax.axis_size("field")
    faces = [shape_of(ns, ny, nz), shape_of(ns, ny, nz), shape_of(ns, nx, nz), shape_of(ns, nx, nz)]
    first_faces = [shape_of(ns + 1, *f.shape[1:]) for f in faces]
    *sent, gather, scatter = pl.pallas_call(
        faces_kernel,
        out_shape=first_faces
        + [shape_of(2 * nr, 128, dtype=jnp.bfloat16), shape_of(ns, 2 * nr, dtype=jnp.bfloat16)],
        in_specs=[VMEM] * 4,
        out_specs=[VMEM] * 6,
    )(conc, diffusivity, reactions, rate_constants.reshape(nr, 1))
    stride = roundup(nx * ny, 32) + 1
    halos = exchange(*sent)
    gamma_halos = halos
    for step_index in range(STEPS):
        reacted = pl.pallas_call(
            step_kernel,
            out_shape=shape_of(ns, nx, ny, nz),
            in_specs=[VMEM] * 14,
            out_specs=VMEM,
            scratch_shapes=[
                pltpu.VMEM((ns * stride, nz), jnp.float32),
                pltpu.VMEM((ns, nx * ny * nz), jnp.float32),
            ],
        )(
            conc, *halos, diffusivity, *gamma_halos, velocity, wiener[step_index, :, 0],
            gather, scatter,
        )
        last = step_index == STEPS - 1
        if count == 2:
            other = lax.ppermute(reacted, "field", [(0, 1), (1, 0)])
            mixed = pl.pallas_call(
                functools.partial(mix_kernel, count),
                out_shape=[shape_of(ns, nx, ny, nz)] + ([] if last else faces),
                in_specs=[VMEM] * 3,
                out_specs=[VMEM] * (1 if last else 5),
            )(reacted, other, mix_rate)
            conc, sent = mixed[0], mixed[1:]
        else:
            first = lax.psum(reacted, "field")
            second = lax.psum(reacted * reacted, "field")
            mean, decay = closure(first, second, count, mix_rate)
            conc = mean + (reacted - mean) * decay
            sent = (conc[:, 0], conc[:, -1], conc[:, :, 0], conc[:, :, -1])
        if not last:
            halos = exchange(*sent)
    return conc[None]


def solution(mesh):
    return jax.shard_map(
        on_device,
        mesh=mesh,
        in_specs=(
            P("field", None, "gx", "gy", None),
            P(None, "gx", "gy", None),
            P("gx", "gy", None),
            P(None, None, "field", "gx", "gy", None),
            P("gx", "gy", None),
            P(),
            P(),
        ),
        out_specs=P("field", None, "gx", "gy", None),
        check_vma=False,
    )
```

time: 198 us -> 125 us (0.63)
  matrix products: 130 us -> 0 us
  Pallas kernels: 0 us -> 76 us
  blocking collectives: 16.7 us -> 0 us
  waiting for transfers between devices: 8.18 us -> 21.6 us
  starting transfers between devices: 30.1 us -> 20.1 us
  other arithmetic: 6.65 us -> 0 us
  local copies, waits for them, and re-layouts: 2.92 us -> 5.36 us
    dot_general x48 -> x0, matrix products: 130 us -> none  [the longest x24 83.5 us: substep(): jnp.dot(react, logs, precision=highest)]
    pallas_call x0 -> x5, Pallas kernels: none -> 76 us  [the longest x2 70.4 us: on_device(): pl.pallas_call(step_kernel, out_shape=shape_of(ns, nx, ny, nz), in_specs=...]
    all_gather x2 -> x0, blocking collectives: 16.7 us -> none  [on_device(): every = lax.all_gather(conc[None], 'field', axis=0, tiled=True)]
    ppermute x12 -> x10, waiting for transfers between devices: 8.18 us -> 21.6 us  [the longest x2 14.1 us: on_device(): other = lax.ppermute(reacted, 'field', [(0, 1), (1, 0)])]
    ppermute x12 -> x10, starting transfers between devices: 30.1 us -> 20.1 us  [the longest x2 7.77 us: exchange(): from_below = lax.ppermute(xhi, 'gx', up(nx))]
    unnamed x11 -> x27, local copies, waits for them, and re-layouts: 0.44 us -> 4.02 us
    concatenate x5 -> x0, other arithmetic: 3.04 us -> none  [padded_2(): block = jnp.concatenate([low, block, high], axis=dim)]
  transfers between devices with their start and end apart: 12 -> 10, of which waited for: 5 -> 5; matrix products, arithmetic and copies ran while one was open for 2% -> 1% of each run, Pallas kernels for 0% -> 0%
where the time goes in v1:
time: 125 us; the launch traced here: 123 us
  Pallas kernels  76 us (61%)
  waiting for transfers between devices  21.6 us (17%)
  starting transfers between devices  20.1 us (16%)
  local copies, waits for them, and re-layouts  5.36 us (4%)
    pallas_call x2, Pallas kernels, on_device(): pl.pallas_call(step_kernel, out_shape=shape_of(ns, nx, ny, nz), in_specs=...  70.4 us
    ppermute x2, waiting for transfers between devices, on_device(): other = lax.ppermute(reacted, 'field', [(0, 1), (1, 0)])  14.1 us
    ppermute x2, starting transfers between devices, exchange(): from_below = lax.ppermute(xhi, 'gx', up(nx))  7.77 us
    ppermute x2, waiting for transfers between devices, exchange(): from_above = lax.ppermute(xlo, 'gx', down(nx))  4.17 us
    ppermute x2, starting transfers between devices, exchange(): from_left = lax.ppermute(yhi, 'gy', up(ny))  4.13 us
    unnamed x27, local copies, waits for them, and re-layouts  4.02 us
    pallas_call x2, Pallas kernels, on_device(): pl.pallas_call(functools.partial(mix_kernel, count), out_shape=[shape_of(...  3.85 us
    ppermute x2, waiting for transfers between devices, exchange(): from_right = lax.ppermute(ylo, 'gy', down(ny))  3.05 us
  transfers between devices with their start and end apart: 10, of which 5 were waited for; matrix products, arithmetic and copies ran while one was open for 1% of the time, Pallas kernels for 0%

profile of v1, /device:TPU:0, one launch (start us, length us, event | category | flops | bytes accessed | tf_op | source)
XLA Modules:
  0.0 123.2 jit_solution(3166769508394876412)
XLA Ops:
  0.0 0.7 copy-done.12
  0.7 0.7 copy.9.rates
  1.4 0.7 copy.8.reactions
  2.1 1.8 %shard_map.73 = (f32[17,8,128]{2,1,0:T(8,128)}, f32[17,8,128]{2,1,0:T(8,128)}, f32[17,4,128]{2,1,0:T(4,128)}, f32[17,4,128]{2,1,0:T(4,128)}, bf16[128,128]{1,0:T(8,128)(2,1)}, /*index=5*/bf16[16,128]{1,0:T(8,128)(2,1)}) custom-call(f32[16,4,8,128]{3,2,1,0:T(8,128)} %bitcast.8, f32[4,8,128]{2,1,0:T(8,128)} %gamma.5, s32[64,4]{1,0:T(8,128)} %copy.8.reactions, ...), custom_call_target="tpu_custom_call" | custom-call | tf_op jit(solution)/shard_map/pallas_call | solution.py:201
  3.9 2.4 %collective-permute-start.2 = (f32[17,4,128]{2,1,0:T(4,128)}, f32[17,4,128]{2,1,0:T(4,128)S(1)}, u32[]{:S(2)}, u32[]{:S(2)}) collective-permute-start(f32[17,4,128]{2,1,0:T(4,128)} %get-tuple-element.18), channel_id=1, source_target_pairs={{0,1},{1,2},{2,3},{4,5},{5,6},{6,7},{8,9},{9,10},{10,11},{12,13},{... | collective-permute-start | bytes 104456 | tf_op jit(solution)/shard_map/ppermute | solution.py:189
  6.3 1.3 %collective-permute-start.3 = (f32[17,4,128]{2,1,0:T(4,128)}, f32[17,4,128]{2,1,0:T(4,128)S(1)}, u32[]{:S(2)}, u32[]{:S(2)}) collective-permute-start(f32[17,4,128]{2,1,0:T(4,128)} %get-tuple-element.19), channel_id=1, source_target_pairs={{1,0},{2,1},{3,2},{5,4},{6,5},{7,6},{9,8},{10,9},{11,10},{13,12},{... | collective-permute-start | bytes 104456 | tf_op jit(solution)/shard_map/ppermute | solution.py:190
  7.6 4.3 %collective-permute-start = (f32[17,8,128]{2,1,0:T(8,128)}, f32[17,8,128]{2,1,0:T(8,128)S(1)}, u32[]{:S(2)}, u32[]{:S(2)}) collective-permute-start(f32[17,8,128]{2,1,0:T(8,128)} %get-tuple-element.16), channel_id=1, source_target_pairs={{0,4},{4,8},{8,12},{1,5},{5,9},{9,13},{2,6},{6,10},{10,14},{3,7},{... | collective-permute-start | bytes 208904 | tf_op jit(solution)/shard_map/ppermute | solution.py:187
  11.9 1.3 %collective-permute-start.1 = (f32[17,8,128]{2,1,0:T(8,128)}, f32[17,8,128]{2,1,0:T(8,128)S(1)}, u32[]{:S(2)}, u32[]{:S(2)}) collective-permute-start(f32[17,8,128]{2,1,0:T(8,128)} %get-tuple-element.17), channel_id=1, source_target_pairs={{4,0},{8,4},{12,8},{5,1},{9,5},{13,9},{6,2},{10,6},{14,10},{7,3},{... | collective-permute-start | bytes 208904 | tf_op jit(solution)/shard_map/ppermute | solution.py:188
  14.1 4.2 %collective-permute-done.1.xhi.ghix = f32[17,8,128]{2,1,0:T(8,128)S(1)} collective-permute-done((f32[17,8,128]{2,1,0:T(8,128)}, f32[17,8,128]{2,1,0:T(8,128)S(1)}, u32[]{:S(2)}, u32[]{:S(2)}) %collective-permute-start.1) | collective-permute-done | bytes 69664 | tf_op jit(solution)/shard_map/ppermute | solution.py:188
  18.9 35.2 %shard_map.74.mine = f32[16,4,8,128]{3,2,1,0:T(8,128)} custom-call(f32[16,4,8,128]{3,2,1,0:T(8,128)} %bitcast.9, f32[17,8,128]{2,1,0:T(8,128)} %copy-done, f32[17,8,128]{2,1,0:T(8,128)} %copy-done.1, f32[17,4,128]{2,1,0:T(4,128)} %copy-done.2, f32[17,4,128]{2,1,0:T(4,128)} %copy-done.3, f32[4,8,128]{2,1,0:T(8,128)} %gamma.5, f32[17,8,128]{2,1,0:T(8,128)} %copy-done, ...), custom_call_target="tpu_custom_call" | custom-call | tf_op jit(solution)/shard_map/pallas_call | solution.py:212
  54.1 1.5 %collective-permute-start.4 = (f32[16,4,8,128]{3,2,1,0:T(8,128)}, f32[16,4,8,128]{3,2,1,0:T(8,128)S(1)}, u32[]{:S(2)}, u32[]{:S(2)}) collective-permute-start(f32[16,4,8,128]{3,2,1,0:T(8,128)} %shard_map.74.mine), channel_id=1, source_target_pairs={{0,16},{16,0},{1,17},{17,1},{2,18},{18,2},{3,19},{19,3},{4,20},{20... | collective-permute-start | bytes 786440 | tf_op jit(solution)/shard_map/ppermute | solution.py:227
  55.6 7.9 %collective-permute-done.4.other = f32[16,4,8,128]{3,2,1,0:T(8,128)S(1)} collective-permute-done((f32[16,4,8,128]{3,2,1,0:T(8,128)}, f32[16,4,8,128]{3,2,1,0:T(8,128)S(1)}, u32[]{:S(2)}, u32[]{:S(2)}) %collective-permute-start.4) | collective-permute-done | bytes 262176 | tf_op jit(solution)/shard_map/ppermute | solution.py:227
  63.5 0.7 copy-done.5
  64.2 2.0 %shard_map.75 = (f32[16,4,8,128]{3,2,1,0:T(8,128)}, f32[16,8,128]{2,1,0:T(8,128)}, f32[16,8,128]{2,1,0:T(8,128)}, f32[16,4,128]{2,1,0:T(4,128)}, f32[16,4,128]{2,1,0:T(4,128)}) custom-call(f32[16,4,8,128]{3,2,1,0:T(8,128)} %shard_map.74.mine, f32[16,4,8,128]{3,2,1,0:T(8,128)} %copy-done.5, f32[4,8,128]{2,1,0:T(8,128)} %mix_rate.3), custom_call_target="tpu_custom_call" | custom-call | tf_op jit(solution)/shard_map/pallas_call | solution.py:228
  66.1 3.5 %collective-permute-start.5 = (f32[16,8,128]{2,1,0:T(8,128)}, f32[16,8,128]{2,1,0:T(8,128)S(1)}, u32[]{:S(2)}, u32[]{:S(2)}) collective-permute-start(f32[16,8,128]{2,1,0:T(8,128)} %get-tuple-element.23), channel_id=1, source_target_pairs={{0,4},{4,8},{8,12},{1,5},{5,9},{9,13},{2,6},{6,10},{10,14},{3,7},{... | collective-permute-start | bytes 196616 | tf_op jit(solution)/shard_map/ppermute | solution.py:187
  69.6 1.3 %collective-permute-start.6 = (f32[16,8,128]{2,1,0:T(8,128)}, f32[16,8,128]{2,1,0:T(8,128)S(1)}, u32[]{:S(2)}, u32[]{:S(2)}) collective-permute-start(f32[16,8,128]{2,1,0:T(8,128)} %get-tuple-element.24), channel_id=1, source_target_pairs={{4,0},{8,4},{12,8},{5,1},{9,5},{13,9},{6,2},{10,6},{14,10},{7,3},{... | collective-permute-start | bytes 196616 | tf_op jit(solution)/shard_map/ppermute | solution.py:188
  70.9 1.7 %collective-permute-start.7 = (f32[16,4,128]{2,1,0:T(4,128)}, f32[16,4,128]{2,1,0:T(4,128)S(1)}, u32[]{:S(2)}, u32[]{:S(2)}) collective-permute-start(f32[16,4,128]{2,1,0:T(4,128)} %get-tuple-element.25), channel_id=1, source_target_pairs={{0,1},{1,2},{2,3},{4,5},{5,6},{6,7},{8,9},{9,10},{10,11},{12,13},{... | collective-permute-start | bytes 98312 | tf_op jit(solution)/shard_map/ppermute | solution.py:189
  72.7 1.3 %collective-permute-start.8 = (f32[16,4,128]{2,1,0:T(4,128)}, f32[16,4,128]{2,1,0:T(4,128)S(1)}, u32[]{:S(2)}, u32[]{:S(2)}) collective-permute-start(f32[16,4,128]{2,1,0:T(4,128)} %get-tuple-element.26), channel_id=1, source_target_pairs={{1,0},{2,1},{3,2},{5,4},{6,5},{7,6},{9,8},{10,9},{11,10},{13,12},{... | collective-permute-start | bytes 98312 | tf_op jit(solution)/shard_map/ppermute | solution.py:190
  74.0 3.0 %collective-permute-done.8.yhi = f32[16,4,128]{2,1,0:T(4,128)S(1)} collective-permute-done((f32[16,4,128]{2,1,0:T(4,128)}, f32[16,4,128]{2,1,0:T(4,128)S(1)}, u32[]{:S(2)}, u32[]{:S(2)}) %collective-permute-start.8) | collective-permute-done | bytes 32800 | tf_op jit(solution)/shard_map/ppermute | solution.py:190
  77.7 35.2 %shard_map.76.mine = f32[16,4,8,128]{3,2,1,0:T(8,128)} custom-call(f32[16,4,8,128]{3,2,1,0:T(8,128)} %get-tuple-element.22.conc, f32[16,8,128]{2,1,0:T(8,128)} %copy-done.7, f32[16,8,128]{2,1,0:T(8,128)} %copy-done.8, f32[16,4,128]{2,1,0:T(4,128)} %copy-done.9, f32[16,4,128]{2,1,0:T(4,128)} %copy-done.10, f32[4,8,128]{2,1,0:T(8,128)} %gamma.5, ...), custom_call_target="tpu_custom_call" | custom-call | tf_op jit(solution)/shard_map/pallas_call | solution.py:212
  112.9 1.5 %collective-permute-start.9 = (f32[16,4,8,128]{3,2,1,0:T(8,128)}, f32[16,4,8,128]{3,2,1,0:T(8,128)S(1)}, u32[]{:S(2)}, u32[]{:S(2)}) collective-permute-start(f32[16,4,8,128]{3,2,1,0:T(8,128)} %shard_map.76.mine), channel_id=1, source_target_pairs={{0,16},{16,0},{1,17},{17,1},{2,18},{18,2},{3,19},{19,3},{4,20},{20... | collective-permute-start | bytes 786440 | tf_op jit(solution)/shard_map/ppermute | solution.py:227
  114.4 6.2 %collective-permute-done.9.other = f32[16,4,8,128]{3,2,1,0:T(8,128)S(1)} collective-permute-done((f32[16,4,8,128]{3,2,1,0:T(8,128)}, f32[16,4,8,128]{3,2,1,0:T(8,128)S(1)}, u32[]{:S(2)}, u32[]{:S(2)}) %collective-permute-start.9) | collective-permute-done | bytes 262176 | tf_op jit(solution)/shard_map/ppermute | solution.py:227
  120.6 0.7 copy-done.4
  121.3 1.9 %shard_map.77 = f32[16,4,8,128]{3,2,1,0:T(8,128)} custom-call(f32[16,4,8,128]{3,2,1,0:T(8,128)} %shard_map.76.mine, f32[16,4,8,128]{3,2,1,0:T(8,128)} %copy-done.4, f32[4,8,128]{2,1,0:T(8,128)} %mix_rate.3), custom_call_target="tpu_custom_call" | custom-call | tf_op jit(solution)/shard_map/pallas_call | solution.py:228
  (30 shorter events, 2.2 us)
Async XLA Ops:
  0.0 0.7 copy-start.12
  0.7 0.7 copy-start.11
  2.1 11.1 %copy-start.6 = (f32[2,3,1,4,8,128]{5,4,3,2,1,0:T(8,128)S(1)}, f32[2,3,1,4,8,128]{5,4,3,2,1,0:T(8,128)}, u32[]{:S(2)}) copy-start(f32[2,3,1,4,8,128]{5,4,3,2,1,0:T(8,128)} %param.10) | copy-start | bytes 294916
  3.9 10.0 %collective-permute-start.2 = (f32[17,4,128]{2,1,0:T(4,128)}, f32[17,4,128]{2,1,0:T(4,128)S(1)}, u32[]{:S(2)}, u32[]{:S(2)}) collective-permute-start(f32[17,4,128]{2,1,0:T(4,128)} %get-tuple-element.18), channel_id=1, source_target_pairs={{0,1},{1,2},{2,3},{4,5},{5,6},{6,7},{8,9},{9,10},{10,11},{12,13},{... | collective-permute-start | bytes 104456 | tf_op jit(solution)/shard_map/ppermute | solution.py:189
  6.3 7.6 %collective-permute-start.3 = (f32[17,4,128]{2,1,0:T(4,128)}, f32[17,4,128]{2,1,0:T(4,128)S(1)}, u32[]{:S(2)}, u32[]{:S(2)}) collective-permute-start(f32[17,4,128]{2,1,0:T(4,128)} %get-tuple-element.19), channel_id=1, source_target_pairs={{1,0},{2,1},{3,2},{5,4},{6,5},{7,6},{9,8},{10,9},{11,10},{13,12},{... | collective-permute-start | bytes 104456 | tf_op jit(solution)/shard_map/ppermute | solution.py:190
  7.6 6.5 %collective-permute-start = (f32[17,8,128]{2,1,0:T(8,128)}, f32[17,8,128]{2,1,0:T(8,128)S(1)}, u32[]{:S(2)}, u32[]{:S(2)}) collective-permute-start(f32[17,8,128]{2,1,0:T(8,128)} %get-tuple-element.16), channel_id=1, source_target_pairs={{0,4},{4,8},{8,12},{1,5},{5,9},{9,13},{2,6},{6,10},{10,14},{3,7},{... | collective-permute-start | bytes 208904 | tf_op jit(solution)/shard_map/ppermute | solution.py:187
  11.9 6.4 %collective-permute-start.1 = (f32[17,8,128]{2,1,0:T(8,128)}, f32[17,8,128]{2,1,0:T(8,128)S(1)}, u32[]{:S(2)}, u32[]{:S(2)}) collective-permute-start(f32[17,8,128]{2,1,0:T(8,128)} %get-tuple-element.17), channel_id=1, source_target_pairs={{4,0},{8,4},{12,8},{5,1},{9,5},{13,9},{6,2},{10,6},{14,10},{7,3},{... | collective-permute-start | bytes 208904 | tf_op jit(solution)/shard_map/ppermute | solution.py:188
  13.8 4.5 %copy-start.2 = (f32[17,4,128]{2,1,0:T(4,128)}, f32[17,4,128]{2,1,0:T(4,128)S(1)}, u32[]{:S(2)}) copy-start(f32[17,4,128]{2,1,0:T(4,128)S(1)} %collective-permute-done.2.ylo.gloy) | copy-start | bytes 104452
  13.8 4.4 %copy-start.3 = (f32[17,4,128]{2,1,0:T(4,128)}, f32[17,4,128]{2,1,0:T(4,128)S(1)}, u32[]{:S(2)}) copy-start(f32[17,4,128]{2,1,0:T(4,128)S(1)} %collective-permute-done.3.yhi.ghiy) | copy-start | bytes 104452
  14.1 4.2 %copy-start = (f32[17,8,128]{2,1,0:T(8,128)}, f32[17,8,128]{2,1,0:T(8,128)S(1)}, u32[]{:S(2)}) copy-start(f32[17,8,128]{2,1,0:T(8,128)S(1)} %collective-permute-done.xlo.glox) | copy-start | bytes 208900
  18.3 0.6 copy-start.1
  54.1 9.4 %collective-permute-start.4 = (f32[16,4,8,128]{3,2,1,0:T(8,128)}, f32[16,4,8,128]{3,2,1,0:T(8,128)S(1)}, u32[]{:S(2)}, u32[]{:S(2)}) collective-permute-start(f32[16,4,8,128]{3,2,1,0:T(8,128)} %shard_map.74.mine), channel_id=1, source_target_pairs={{0,16},{16,0},{1,17},{17,1},{2,18},{18,2},{3,19},{19,3},{4,20},{20... | collective-permute-start | bytes 786440 | tf_op jit(solution)/shard_map/ppermute | solution.py:227
  63.5 0.7 copy-start.5
  66.1 10.9 %collective-permute-start.5 = (f32[16,8,128]{2,1,0:T(8,128)}, f32[16,8,128]{2,1,0:T(8,128)S(1)}, u32[]{:S(2)}, u32[]{:S(2)}) collective-permute-start(f32[16,8,128]{2,1,0:T(8,128)} %get-tuple-element.23), channel_id=1, source_target_pairs={{0,4},{4,8},{8,12},{1,5},{5,9},{9,13},{2,6},{6,10},{10,14},{3,7},{... | collective-permute-start | bytes 196616 | tf_op jit(solution)/shard_map/ppermute | solution.py:187
  69.6 7.4 %collective-permute-start.6 = (f32[16,8,128]{2,1,0:T(8,128)}, f32[16,8,128]{2,1,0:T(8,128)S(1)}, u32[]{:S(2)}, u32[]{:S(2)}) collective-permute-start(f32[16,8,128]{2,1,0:T(8,128)} %get-tuple-element.24), channel_id=1, source_target_pairs={{4,0},{8,4},{12,8},{5,1},{9,5},{13,9},{6,2},{10,6},{14,10},{7,3},{... | collective-permute-start | bytes 196616 | tf_op jit(solution)/shard_map/ppermute | solution.py:188
  70.9 3.1 %collective-permute-start.7 = (f32[16,4,128]{2,1,0:T(4,128)}, f32[16,4,128]{2,1,0:T(4,128)S(1)}, u32[]{:S(2)}, u32[]{:S(2)}) collective-permute-start(f32[16,4,128]{2,1,0:T(4,128)} %get-tuple-element.25), channel_id=1, source_target_pairs={{0,1},{1,2},{2,3},{4,5},{5,6},{6,7},{8,9},{9,10},{10,11},{12,13},{... | collective-permute-start | bytes 98312 | tf_op jit(solution)/shard_map/ppermute | solution.py:189
  72.7 4.4 %collective-permute-start.8 = (f32[16,4,128]{2,1,0:T(4,128)}, f32[16,4,128]{2,1,0:T(4,128)S(1)}, u32[]{:S(2)}, u32[]{:S(2)}) collective-permute-start(f32[16,4,128]{2,1,0:T(4,128)} %get-tuple-element.26), channel_id=1, source_target_pairs={{1,0},{2,1},{3,2},{5,4},{6,5},{7,6},{9,8},{10,9},{11,10},{13,12},{... | collective-permute-start | bytes 98312 | tf_op jit(solution)/shard_map/ppermute | solution.py:190
  74.0 3.1 %copy-start.9 = (f32[16,4,128]{2,1,0:T(4,128)}, f32[16,4,128]{2,1,0:T(4,128)S(1)}, u32[]{:S(2)}) copy-start(f32[16,4,128]{2,1,0:T(4,128)S(1)} %collective-permute-done.7.ylo) | copy-start | bytes 98308
  77.0 0.6 copy-start.10
  77.0 0.6 copy-start.7
  77.0 0.6 copy-start.8
  112.9 7.7 %collective-permute-start.9 = (f32[16,4,8,128]{3,2,1,0:T(8,128)}, f32[16,4,8,128]{3,2,1,0:T(8,128)S(1)}, u32[]{:S(2)}, u32[]{:S(2)}) collective-permute-start(f32[16,4,8,128]{3,2,1,0:T(8,128)} %shard_map.76.mine), channel_id=1, source_target_pairs={{0,16},{16,0},{1,17},{17,1},{2,18},{18,2},{3,19},{19,3},{4,20},{20... | collective-permute-start | bytes 786440 | tf_op jit(solution)/shard_map/ppermute | solution.py:227
  120.6 0.7 copy-start.4

commit v2 on v1

v2 whole, which is shorter than its diff:
```python
import functools

import jax
import jax.numpy as jnp
from jax import lax
from jax.experimental import pallas as pl
from jax.experimental.pallas import tpu as pltpu
from jax.sharding import PartitionSpec as P

SUBSTEPS = 12
STEPS = 2
CHEM_STEP = 0.04
LOG2E = 1.4426950408889634
LN2 = 0.6931471805599453
TILE = 256
VMEM = pl.BlockSpec(memory_space=pltpu.VMEM)


def roundup(n, m):
    return (n + m - 1) // m * m


def split(x):
    hi = x.astype(jnp.bfloat16)
    lo = (x - hi.astype(jnp.float32)).astype(jnp.bfloat16)
    return hi, lo


def params(mib):
    return pltpu.CompilerParams(vmem_limit_bytes=mib * 2**20)


def sides(axis):
    here, count = lax.axis_index(axis), lax.axis_size(axis)
    even = lax.rem(here, 2) == 0
    return even, here == 0, here == count - 1


def picked(even, low, high):
    return jnp.where(even, high, low), jnp.where(even, low, high)


def send_faces(conc, s, x1, x2, y1, y2, row):
    nx, ny = conc.shape[-3], conc.shape[-2]
    even, _, _ = sides("gx")
    for ref, x in zip((x1, x2), picked(even, 0, nx - 1)):
        ref[row] = conc[s, x]
    even, _, _ = sides("gy")
    y1[row], y2[row] = picked(even, conc[s, :, 0, :], conc[s, :, ny - 1, :])


def halo(axis, first, second):
    even, lowest, highest = sides(axis)
    above = jnp.where(highest, 0.0, jnp.where(even, first, second))
    below = jnp.where(lowest, 0.0, jnp.where(even, second, first))
    return above, below


def faces_kernel(conc, gamma, x1, x2, y1, y2):
    ns = conc.shape[0]
    for s in range(ns):
        send_faces(conc, s, x1, x2, y1, y2, s)
    send_faces(gamma, 0, x1, x2, y1, y2, ns)


def tables_kernel(ns, reactions, rates, gather, scatter):
    nr = reactions.shape[1]
    depth = gather.shape[1]
    row = lax.broadcasted_iota(jnp.int32, (depth, nr), 0)
    scalar, part = lax.rem(row, ns), lax.div(row, ns)
    k = rates[...] * (CHEM_STEP * LN2)
    k_hi = k.astype(jnp.bfloat16).astype(jnp.float32)
    k_lo = k - k_hi

    def column(c):
        return jnp.where(scalar == reactions[c : c + 1, :], 1.0, 0.0)

    first, second, third, fourth = (column(c) for c in range(4))
    weight = jnp.where(part < 2, k_hi, jnp.where(part == 2, k_lo, 0.0))
    both = jnp.concatenate(
        [first * weight, second * jnp.where(part < 2, 1.0, 0.0)], axis=1
    ).T
    for j in range(nr // 8):
        block = [both[c + 8 * j : c + 8 * j + 8, :] for c in (0, nr)]
        gather[16 * j : 16 * j + 16, :] = jnp.concatenate(block, axis=0).astype(jnp.bfloat16)
    net = (third + fourth - first - second)[:ns].astype(jnp.bfloat16)
    scatter[...] = jnp.concatenate([net, net], axis=1)


def step_kernel(
    step, conc, x1, x2, y1, y2, gamma, gx1, gx2, gy1, gy2, velocity, wiener, gather, scatter,
    out, rows, state
):
    ns, nx, ny, nz = conc.shape
    stride = rows.shape[0] // ns
    chunks = nx * ny
    lane = lax.broadcasted_iota(jnp.int32, (ny, nz), 1)
    sub = lax.broadcasted_iota(jnp.int32, (ny, nz), 0)
    is_top, is_bottom = sub == ny - 1, sub == 0

    def shifted(value, above, below):
        up = jnp.where(is_top, above, pltpu.roll(value, ny - 1, 0))
        down = jnp.where(is_bottom, below, pltpu.roll(value, 1, 0))
        return up, down

    gx_above, gx_below = halo("gx", gx1[ns], gx2[ns])
    gy_above, gy_below = halo("gy", gy1[ns], gy2[ns])
    coefs = []
    for x in range(nx):
        g = gamma[0, x]
        amp = jnp.sqrt(2.0 * g)
        gx_up = gx_above if x == nx - 1 else gamma[0, x + 1]
        gx_down = gx_below if x == 0 else gamma[0, x - 1]
        gy_up, gy_down = shifted(g, gy_above[x : x + 1], gy_below[x : x + 1])
        gz_up = jnp.where(lane == nz - 1, 0.0, pltpu.roll(g, nz - 1, 1))
        gz_down = jnp.where(lane == 0, 0.0, pltpu.roll(g, 1, 1))
        total = jnp.zeros_like(g)
        coef = []
        for d, (gu, gd) in enumerate(((gx_up, gx_down), (gy_up, gy_down), (gz_up, gz_down))):
            drift = 0.5 * (amp * wiener[step, d, 0, x] - velocity[d, x])
            up, down = 0.5 * (g + gu), 0.5 * (g + gd)
            total = total + (up + down)
            coef += [(up + drift) * LOG2E, (down - drift) * LOG2E]
        coef[4] = jnp.where(lane == nz - 1, 0.0, coef[4])
        coef[5] = jnp.where(lane == 0, 0.0, coef[5])
        coefs.append([(1.0 - total) * LOG2E] + coef)
    for s in range(ns):
        x_above, x_below = halo("gx", x1[s], x2[s])
        y_above, y_below = halo("gy", y1[s], y2[s])
        for x in range(nx):
            centre, xu, xd, yu, yd, zu, zd = coefs[x]
            p = conc[s, x]
            px_up = x_above if x == nx - 1 else conc[s, x + 1]
            px_down = x_below if x == 0 else conc[s, x - 1]
            py_up, py_down = shifted(p, y_above[x : x + 1], y_below[x : x + 1])
            pz_up = pltpu.roll(p, nz - 1, 1)
            pz_down = pltpu.roll(p, 1, 1)
            moved = (centre * p + (xu * px_up + xd * px_down)) + (
                (yu * py_up + yd * py_down) + (zu * pz_up + zd * pz_down)
            )
            rows[s * stride + x * ny : s * stride + (x + 1) * ny, :] = moved

    for j in range(chunks):
        state[:, j * nz : (j + 1) * nz] = rows[pl.ds(j, ns, stride=stride), :]
    chemistry(state, gather, scatter)
    for j in range(chunks):
        rows[pl.ds(j, ns, stride=stride), :] = state[:, j * nz : (j + 1) * nz] * LN2
    for s in range(ns):
        for x in range(nx):
            out[s, x] = rows[s * stride + x * ny : s * stride + (x + 1) * ny, :]


def chemistry(state, gather, scatter):
    ns, cells = state.shape
    tiles = cells // TILE
    table, net = gather[...][:, : 3 * ns], scatter[...]
    nr = table.shape[0] // 2
    steps = SUBSTEPS * tiles
    lag = tiles // 2
    both, change = {}, {}

    def cut(t):
        return slice(t % tiles * TILE, (t % tiles + 1) * TILE)

    for t in range(steps + 2 * lag):
        done = t - 2 * lag
        if done >= 0:
            state[:, cut(done)] += change.pop(done)
        if t < steps:
            u = state[:, cut(t)]
            sp = jnp.maximum(u, jnp.log2(1.0 + jnp.exp2(jnp.minimum(u, 120.0))))
            hi, lo = split(sp)
            both[t] = jnp.dot(
                table,
                jnp.concatenate([hi, lo, hi], axis=0),
                preferred_element_type=jnp.float32,
            )
        ready = t - lag
        if 0 <= ready < steps:
            pair = both.pop(ready).reshape(nr // 8, 2, 8, TILE)
            hi, lo = split((pair[:, 0] * pair[:, 1]).reshape(nr, TILE))
            change[ready] = jnp.dot(
                net, jnp.concatenate([hi, lo], axis=0), preferred_element_type=jnp.float32
            )


def mix_kernel(count, mine, other, mix_rate, out, *faces):
    ns, nx, ny, nz = mine.shape
    for x in range(nx):
        spread = jnp.zeros((ny, nz), jnp.float32)
        energy = jnp.zeros((ny, nz), jnp.float32)
        for s in range(ns):
            a, b = mine[s, x], other[s, x]
            mean = (a + b) * (1.0 / count)
            meansq = (a * a + b * b) * (1.0 / count)
            spread = spread + (meansq - mean * mean)
            energy = energy + meansq
        omega = mix_rate[x] * (1.0 + spread / (1.0 + energy))
        decay = jnp.exp(-0.5 * omega)
        for s in range(ns):
            a, b = mine[s, x], other[s, x]
            mean = (a + b) * (1.0 / count)
            new = mean + (a - mean) * decay
            out[s, x] = new
    if faces:
        for s in range(ns):
            send_faces(out, s, *faces, s)


def closure(first, second, count, mix_rate):
    mean = first / count
    meansq = second / count
    spread = jnp.sum(meansq - mean * mean, axis=0)
    energy = jnp.sum(meansq, axis=0)
    omega = mix_rate * (1.0 + spread / (1.0 + energy))
    return (mean, jnp.exp(-0.5 * omega))


def shape_of(*dims, dtype=jnp.float32):
    return jax.ShapeDtypeStruct(dims, dtype)


def swaps(count):
    pairs = [[(i, i + 1) for i in range(start, count - 1, 2)] for start in (0, 1)]
    return [(p, sorted(set(range(count)) - {i for q in p for i in q})) for p in pairs]


def swap(value, axis, pairs, rest, other=None):
    both = pairs + [(j, i) for i, j in pairs]
    if other is not None and rest and lax.axis_size(other) % 2 == 0:
        n = lax.axis_size(other)
        joint = [(i * n + k, j * n + k) for i, j in both for k in range(n)]
        joint += [(i * n + k, i * n + k + 1 - 2 * (k % 2)) for i in rest for k in range(n)]
        return lax.ppermute(value, (axis, other), joint)
    if len(rest) == 2:
        both = both + [tuple(rest), tuple(rest[::-1])]
    else:
        both = both + [(i, i) for i in rest]
    return lax.ppermute(value, axis, both)


def exchange(x1, x2, y1, y2):
    (a, rest_a), (b, rest_b) = swaps(lax.axis_size("gx"))
    (c, rest_c), (d, rest_d) = swaps(lax.axis_size("gy"))
    return (
        swap(x1, "gx", a, rest_a, "gy"),
        swap(x2, "gx", b, rest_b, "gy"),
        swap(y1, "gy", c, rest_c),
        swap(y2, "gy", d, rest_d),
    )


def on_device(concentrations, velocity, diffusivity, wiener, mix_rate, rate_constants, reactions):
    conc = concentrations[0]
    ns, nx, ny, nz = conc.shape
    nr = reactions.shape[0]
    count = lax.axis_size("field")
    gamma = diffusivity[None]
    face_dims = [(ny, nz), (ny, nz), (nx, nz), (nx, nz)]
    sent = pl.pallas_call(
        faces_kernel,
        out_shape=[shape_of(ns + 1, *d) for d in face_dims],
        in_specs=[VMEM] * 2,
        out_specs=[VMEM] * 4,
        compiler_params=params(4),
        name="faces",
    )(conc, gamma)
    gather, scatter = pl.pallas_call(
        functools.partial(tables_kernel, ns),
        out_shape=[
            shape_of(2 * nr, 128, dtype=jnp.bfloat16), shape_of(ns, 2 * nr, dtype=jnp.bfloat16)
        ],
        in_specs=[VMEM] * 2,
        out_specs=[VMEM] * 2,
        compiler_params=params(2),
        name="tables",
    )(reactions.T, rate_constants.reshape(1, nr))
    stride = roundup(nx * ny, 32) + 1
    halos = exchange(*sent)
    gamma_halos = halos
    for step_index in range(STEPS):
        reacted = pl.pallas_call(
            functools.partial(step_kernel, step_index),
            out_shape=shape_of(ns, nx, ny, nz),
            in_specs=[VMEM] * 14,
            out_specs=VMEM,
            scratch_shapes=[
                pltpu.VMEM((ns * stride, nz), jnp.float32),
                pltpu.VMEM((ns, nx * ny * nz), jnp.float32),
            ],
            compiler_params=params(8),
            name="step",
        )(
            conc, *halos, gamma, *gamma_halos, velocity, wiener, gather, scatter,
        )
        last = step_index == STEPS - 1
        if count == 2:
            other = lax.ppermute(reacted, "field", [(0, 1), (1, 0)])
            mixed = pl.pallas_call(
                functools.partial(mix_kernel, count),
                out_shape=[shape_of(ns, nx, ny, nz)]
                + ([] if last else [shape_of(ns, *d) for d in face_dims]),
                in_specs=[VMEM] * 3,
                out_specs=[VMEM] * (1 if last else 5),
                compiler_params=params(4),
                name="mix",
            )(reacted, other, mix_rate)
            conc, sent = mixed[0], mixed[1:]
        else:
            first = lax.psum(reacted, "field")
            second = lax.psum(reacted * reacted, "field")
            mean, decay = closure(first, second, count, mix_rate)
            conc = mean + (reacted - mean) * decay
            if not last:
                x_even, y_even = sides("gx")[0], sides("gy")[0]
                sent = picked(x_even, conc[:, 0], conc[:, -1]) + picked(
                    y_even, conc[:, :, 0], conc[:, :, -1]
                )
        if not last:
            halos = exchange(*sent)
    return conc[None]


def solution(mesh):
    return jax.shard_map(
        on_device,
        mesh=mesh,
        in_specs=(
            P("field", None, "gx", "gy", None),
            P(None, "gx", "gy", None),
            P("gx", "gy", None),
            P(None, None, "field", "gx", "gy", None),
            P("gx", "gy", None),
            P(),
            P(),
        ),
        out_specs=P("field", None, "gx", "gy", None),
        check_vma=False,
    )
```

time: 125 us -> 44.5 us (0.36); the launches traced: 123 us -> 44.2 us
  Pallas kernels: 76 us -> 10 us
  starting transfers between devices: 20.1 us -> 12.4 us
  waiting for transfers between devices: 21.6 us -> 18.3 us
  local copies, waits for them, and re-layouts: 5.36 us -> 3.39 us
    pallas_call x3 -> x4, Pallas kernels: 72.2 us -> 8.96 us  [the longest x2 8.73 us: on_device(): pl.pallas_call(functools.partial(step_kernel, step_index), out_shape=shap...]
    ppermute x8, starting transfers between devices: 17.1 us -> 9.31 us  [the longest x6 9.3 us: swap(): return lax.ppermute(value, axis, both)]
    ppermute x8, waiting for transfers between devices: 7.48 us -> 4.62 us  [the longest x6 4.62 us: swap(): return lax.ppermute(value, axis, both)]
    pallas_call x2, Pallas kernels: 3.85 us -> 1.05 us  [on_device(): pl.pallas_call(functools.partial(mix_kernel, count), out_shape=[shape_of(...]
    unnamed x27 -> x22, local copies, waits for them, and re-layouts: 4.02 us -> 3.39 us
  transfers between devices with their start and end apart: 10 -> 10, of which waited for: 5 -> 4; matrix products, arithmetic and copies ran while one was open for 1% -> 0% of each run, Pallas kernels for 0% -> 0%
where the time goes in v2:
time: 44.5 us; the launch traced here: 44.2 us
  waiting for transfers between devices  18.3 us (41%)
  starting transfers between devices  12.4 us (28%)
  Pallas kernels  10 us (22%)
  local copies, waits for them, and re-layouts  3.39 us (8%)
    ppermute x2, waiting for transfers between devices, on_device(): other = lax.ppermute(reacted, 'field', [(0, 1), (1, 0)])  13.7 us
    ppermute x6, starting transfers between devices, swap(): return lax.ppermute(value, axis, both)  9.3 us
    pallas_call x2, Pallas kernels, on_device(): pl.pallas_call(functools.partial(step_kernel, step_index), out_shape=shap...  8.73 us
    ppermute x6, waiting for transfers between devices, swap(): return lax.ppermute(value, axis, both)  4.62 us
    unnamed x22, local copies, waits for them, and re-layouts  3.39 us
    ppermute x2, starting transfers between devices, on_device(): other = lax.ppermute(reacted, 'field', [(0, 1), (1, 0)])  3.11 us
    pallas_call x2, Pallas kernels, on_device(): pl.pallas_call(functools.partial(mix_kernel, count), out_shape=[shape_of(...  1.05 us
  transfers between devices with their start and end apart: 10, of which 4 were waited for; matrix products, arithmetic and copies ran while one was open for 0% of the time, Pallas kernels for 0%

profile of v2, /device:TPU:0, one launch (start us, length us, event | category | flops | bytes accessed | tf_op | source)
XLA Modules:
  0.0 44.2 jit_solution(7595118333005717625)
XLA Ops:
  0.0 0.9 %copy-done = f32[1,16,4,8,128]{4,3,2,1,0:T(8,128)S(1)} copy-done((f32[1,16,4,8,128]{4,3,2,1,0:T(8,128)S(1)}, f32[1,16,4,8,128]{4,3,2,1,0:T(8,128)}, u32[]{:S(2)}) %copy-start) | copy-done | bytes 262168
  1.0 0.7 %copy-done.6 = f32[4,8,128]{2,1,0:T(8,128)S(1)} copy-done((f32[4,8,128]{2,1,0:T(8,128)S(1)}, f32[4,8,128]{2,1,0:T(8,128)}, u32[]{:S(2)}) %copy-start.6) | copy-done | bytes 16408
  1.7 0.1 faces.1
  1.7 0.0 copy-start.7
  1.8 3.1 %collective-permute-start = (f32[17,8,128]{2,1,0:T(8,128)S(1)}, f32[17,8,128]{2,1,0:T(8,128)S(1)}, u32[]{:S(2)}, u32[]{:S(2)}) collective-permute-start(f32[17,8,128]{2,1,0:T(8,128)S(1)} %get-tuple-element.16), channel_id=1, source_target_pairs={{0,4},{8,12},{4,0},{12,8},{1,5},{9,13},{5,1},{13,9},{2,6},{10,14},... | collective-permute-start | bytes 208904 | tf_op jit(solution)/shard_map/ppermute | solution.py:239
  4.9 0.5 %collective-permute-start.2 = (f32[17,4,128]{2,1,0:T(4,128)S(1)}, f32[17,4,128]{2,1,0:T(4,128)S(1)}, u32[]{:S(2)}, u32[]{:S(2)}) collective-permute-start(f32[17,4,128]{2,1,0:T(4,128)S(1)} %get-tuple-element.18), channel_id=1, source_target_pairs={{0,1},{2,3},{1,0},{3,2},{4,5},{6,7},{5,4},{7,6},{8,9},{10,11},{9,8... | collective-permute-start | bytes 104456 | tf_op jit(solution)/shard_map/ppermute | solution.py:239
  5.4 1.1 %collective-permute-start.3 = (f32[17,4,128]{2,1,0:T(4,128)S(1)}, f32[17,4,128]{2,1,0:T(4,128)S(1)}, u32[]{:S(2)}, u32[]{:S(2)}) collective-permute-start(f32[17,4,128]{2,1,0:T(4,128)S(1)} %get-tuple-element.19), channel_id=1, source_target_pairs={{1,2},{2,1},{0,3},{3,0},{5,6},{6,5},{4,7},{7,4},{9,10},{10,9},{8,1... | collective-permute-start | bytes 104456 | tf_op jit(solution)/shard_map/ppermute | solution.py:239
  6.5 0.2 tables.1
  6.7 2.2 %collective-permute-done.3.y2.gy2 = f32[17,4,128]{2,1,0:T(4,128)S(1)} collective-permute-done((f32[17,4,128]{2,1,0:T(4,128)S(1)}, f32[17,4,128]{2,1,0:T(4,128)S(1)}, u32[]{:S(2)}, u32[]{:S(2)}) %collective-permute-start.3) | collective-permute-done | bytes 34848 | tf_op jit(solution)/shard_map/ppermute | solution.py:239
  9.0 0.9 %copy-done.2 = f32[2,3,1,4,8,128]{5,4,3,2,1,0:T(8,128)S(1)} copy-done((f32[2,3,1,4,8,128]{5,4,3,2,1,0:T(8,128)S(1)}, f32[2,3,1,4,8,128]{5,4,3,2,1,0:T(8,128)}, u32[]{:S(2)}) %copy-start.2) | copy-done | bytes 98328
  9.9 0.8 %copy-done.4 = f32[3,4,8,128]{3,2,1,0:T(8,128)S(1)} copy-done((f32[3,4,8,128]{3,2,1,0:T(8,128)S(1)}, f32[3,4,8,128]{3,2,1,0:T(8,128)}, u32[]{:S(2)}) %copy-start.4) | copy-done | bytes 49176
  10.7 4.4 %step.2.mine = f32[16,4,8,128]{3,2,1,0:T(8,128)S(1)} custom-call(f32[16,4,8,128]{3,2,1,0:T(8,128)S(1)} %bitcast.6, f32[17,8,128]{2,1,0:T(8,128)S(1)} %collective-permute-done.x1.gx1, f32[17,8,128]{2,1,0:T(8,128)S(1)} %collective-permute-done.1.x2.gx2, f32[17,4,128]{2,1,0:T(4,128)S(1)} %collective-permute-done.2.y1.gy1, ...), custom_call_target="tpu_custom_call" | custom-call | tf_op jit(solution)/shard_map/step/pallas_call | solution.py:282
  15.0 0.0 copy-start.3
  15.0 1.6 %collective-permute-start.4 = (f32[16,4,8,128]{3,2,1,0:T(8,128)S(1)}, f32[16,4,8,128]{3,2,1,0:T(8,128)S(1)}, u32[]{:S(2)}, u32[]{:S(2)}) collective-permute-start(f32[16,4,8,128]{3,2,1,0:T(8,128)S(1)} %step.2.mine), channel_id=1, source_target_pairs={{0,16},{16,0},{1,17},{17,1},{2,18},{18,2},{3,19},{19,3},{4,20},{20... | collective-permute-start | bytes 786440 | tf_op jit(solution)/shard_map/ppermute | solution.py:298
  16.6 6.8 %collective-permute-done.4.other = f32[16,4,8,128]{3,2,1,0:T(8,128)S(1)} collective-permute-done((f32[16,4,8,128]{3,2,1,0:T(8,128)S(1)}, f32[16,4,8,128]{3,2,1,0:T(8,128)S(1)}, u32[]{:S(2)}, u32[]{:S(2)}) %collective-permute-start.4) | collective-permute-done | bytes 262176 | tf_op jit(solution)/shard_map/ppermute | solution.py:298
  23.4 0.2 mix.2
  23.6 2.9 %collective-permute-start.5 = (f32[16,8,128]{2,1,0:T(8,128)S(1)}, f32[16,8,128]{2,1,0:T(8,128)S(1)}, u32[]{:S(2)}, u32[]{:S(2)}) collective-permute-start(f32[16,8,128]{2,1,0:T(8,128)S(1)} %get-tuple-element.23), channel_id=1, source_target_pairs={{0,4},{8,12},{4,0},{12,8},{1,5},{9,13},{5,1},{13,9},{2,6},{10,14},... | collective-permute-start | bytes 196616 | tf_op jit(solution)/shard_map/ppermute | solution.py:239
  26.6 0.5 %collective-permute-start.7 = (f32[16,4,128]{2,1,0:T(4,128)S(1)}, f32[16,4,128]{2,1,0:T(4,128)S(1)}, u32[]{:S(2)}, u32[]{:S(2)}) collective-permute-start(f32[16,4,128]{2,1,0:T(4,128)S(1)} %get-tuple-element.25), channel_id=1, source_target_pairs={{0,1},{2,3},{1,0},{3,2},{4,5},{6,7},{5,4},{7,6},{8,9},{10,11},{9,8... | collective-permute-start | bytes 98312 | tf_op jit(solution)/shard_map/ppermute | solution.py:239
  27.1 1.1 %collective-permute-start.8 = (f32[16,4,128]{2,1,0:T(4,128)S(1)}, f32[16,4,128]{2,1,0:T(4,128)S(1)}, u32[]{:S(2)}, u32[]{:S(2)}) collective-permute-start(f32[16,4,128]{2,1,0:T(4,128)S(1)} %get-tuple-element.26), channel_id=1, source_target_pairs={{1,2},{2,1},{0,3},{3,0},{5,6},{6,5},{4,7},{7,4},{9,10},{10,9},{8,1... | collective-permute-start | bytes 98312 | tf_op jit(solution)/shard_map/ppermute | solution.py:239
  28.2 2.4 %collective-permute-done.8.y2 = f32[16,4,128]{2,1,0:T(4,128)S(1)} collective-permute-done((f32[16,4,128]{2,1,0:T(4,128)S(1)}, f32[16,4,128]{2,1,0:T(4,128)S(1)}, u32[]{:S(2)}, u32[]{:S(2)}) %collective-permute-start.8) | collective-permute-done | bytes 32800 | tf_op jit(solution)/shard_map/ppermute | solution.py:239
  30.6 4.4 %step.3.mine = f32[16,4,8,128]{3,2,1,0:T(8,128)S(1)} custom-call(f32[16,4,8,128]{3,2,1,0:T(8,128)S(1)} %get-tuple-element.22.conc, f32[16,8,128]{2,1,0:T(8,128)S(1)} %collective-permute-done.5.x1, f32[16,8,128]{2,1,0:T(8,128)S(1)} %collective-permute-done.6.x2, f32[16,4,128]{2,1,0:T(4,128)S(1)} %collective-permute-done.7.y1, ...), custom_call_target="tpu_custom_call" | custom-call | tf_op jit(solution)/shard_map/step/pallas_call | solution.py:282
  35.0 1.6 %collective-permute-start.9 = (f32[16,4,8,128]{3,2,1,0:T(8,128)S(1)}, f32[16,4,8,128]{3,2,1,0:T(8,128)S(1)}, u32[]{:S(2)}, u32[]{:S(2)}) collective-permute-start(f32[16,4,8,128]{3,2,1,0:T(8,128)S(1)} %step.3.mine), channel_id=1, source_target_pairs={{0,16},{16,0},{1,17},{17,1},{2,18},{18,2},{3,19},{19,3},{4,20},{20... | collective-permute-start | bytes 786440 | tf_op jit(solution)/shard_map/ppermute | solution.py:298
  36.5 6.8 %collective-permute-done.9.other = f32[16,4,8,128]{3,2,1,0:T(8,128)S(1)} collective-permute-done((f32[16,4,8,128]{3,2,1,0:T(8,128)S(1)}, f32[16,4,8,128]{3,2,1,0:T(8,128)S(1)}, u32[]{:S(2)}, u32[]{:S(2)}) %collective-permute-start.9) | collective-permute-done | bytes 262176 | tf_op jit(solution)/shard_map/ppermute | solution.py:298
  43.4 0.9 %mix.3 = f32[16,4,8,128]{3,2,1,0:T(8,128)} custom-call(f32[16,4,8,128]{3,2,1,0:T(8,128)S(1)} %step.3.mine, f32[16,4,8,128]{3,2,1,0:T(8,128)S(1)} %collective-permute-done.9.other, f32[4,8,128]{2,1,0:T(8,128)S(1)} %copy-done.8), custom_call_target="tpu_custom_call" | custom-call | tf_op jit(solution)/shard_map/mix/pallas_call | solution.py:299
  (24 shorter events, 0.1 us)
Async XLA Ops:
  0.0 0.9 %copy-start = (f32[1,16,4,8,128]{4,3,2,1,0:T(8,128)S(1)}, f32[1,16,4,8,128]{4,3,2,1,0:T(8,128)}, u32[]{:S(2)}) copy-start(f32[1,16,4,8,128]{4,3,2,1,0:T(8,128)} %param.7) | copy-start | bytes 786436
  1.0 0.7 %copy-start.6 = (f32[4,8,128]{2,1,0:T(8,128)S(1)}, f32[4,8,128]{2,1,0:T(8,128)}, u32[]{:S(2)}) copy-start(f32[4,8,128]{2,1,0:T(8,128)} %param.9) | copy-start | bytes 49156
  1.7 4.8 %copy-start.9 = (s32[64,4]{0,1:T(4,128)S(1)}, s32[64,4]{0,1:T(4,128)}, u32[]{:S(2)}) copy-start(s32[64,4]{0,1:T(4,128)} %param.13) | copy-start | bytes 3076
  1.7 4.8 %copy-start.10 = (f32[64]{0:T(128)S(1)}, f32[64]{0:T(128)}, u32[]{:S(2)}) copy-start(f32[64]{0:T(128)} %param.12) | copy-start | bytes 772
  1.7 7.3 %copy-start.1 = (f32[1,16,4,8,128]{4,3,2,1,0:T(8,128)S(1)}, f32[1,16,4,8,128]{4,3,2,1,0:T(8,128)}, u32[]{:S(2)}) copy-start(f32[1,16,4,8,128]{4,3,2,1,0:T(8,128)} %param.7) | copy-start | bytes 786436
  1.7 7.2 %copy-start.7 = (f32[4,8,128]{2,1,0:T(8,128)S(1)}, f32[4,8,128]{2,1,0:T(8,128)}, u32[]{:S(2)}) copy-start(f32[4,8,128]{2,1,0:T(8,128)} %param.9) | copy-start | bytes 49156
  1.8 7.2 %collective-permute-start = (f32[17,8,128]{2,1,0:T(8,128)S(1)}, f32[17,8,128]{2,1,0:T(8,128)S(1)}, u32[]{:S(2)}, u32[]{:S(2)}) collective-permute-start(f32[17,8,128]{2,1,0:T(8,128)S(1)} %get-tuple-element.16), channel_id=1, source_target_pairs={{0,4},{8,12},{4,0},{12,8},{1,5},{9,13},{5,1},{13,9},{2,6},{10,14},... | collective-permute-start | bytes 208904 | tf_op jit(solution)/shard_map/ppermute | solution.py:239
  4.9 4.1 %collective-permute-start.1 = (f32[17,8,128]{2,1,0:T(8,128)S(1)}, f32[17,8,128]{2,1,0:T(8,128)S(1)}, u32[]{:S(2)}, u32[]{:S(2)}) collective-permute-start(f32[17,8,128]{2,1,0:T(8,128)S(1)} %get-tuple-element.17), channel_id=1, source_target_pairs={{4,8},{5,9},{6,10},{7,11},{8,4},{9,5},{10,6},{11,7},{0,1},{1,0},{2... | collective-permute-start | bytes 208904 | tf_op jit(solution)/shard_map/ppermute | solution.py:234
  4.9 1.8 %collective-permute-start.2 = (f32[17,4,128]{2,1,0:T(4,128)S(1)}, f32[17,4,128]{2,1,0:T(4,128)S(1)}, u32[]{:S(2)}, u32[]{:S(2)}) collective-permute-start(f32[17,4,128]{2,1,0:T(4,128)S(1)} %get-tuple-element.18), channel_id=1, source_target_pairs={{0,1},{2,3},{1,0},{3,2},{4,5},{6,7},{5,4},{7,6},{8,9},{10,11},{9,8... | collective-permute-start | bytes 104456 | tf_op jit(solution)/shard_map/ppermute | solution.py:239
  5.4 3.5 %collective-permute-start.3 = (f32[17,4,128]{2,1,0:T(4,128)S(1)}, f32[17,4,128]{2,1,0:T(4,128)S(1)}, u32[]{:S(2)}, u32[]{:S(2)}) collective-permute-start(f32[17,4,128]{2,1,0:T(4,128)S(1)} %get-tuple-element.19), channel_id=1, source_target_pairs={{1,2},{2,1},{0,3},{3,0},{5,6},{6,5},{4,7},{7,4},{9,10},{10,9},{8,1... | collective-permute-start | bytes 104456 | tf_op jit(solution)/shard_map/ppermute | solution.py:239
  9.0 0.9 %copy-start.2 = (f32[2,3,1,4,8,128]{5,4,3,2,1,0:T(8,128)S(1)}, f32[2,3,1,4,8,128]{5,4,3,2,1,0:T(8,128)}, u32[]{:S(2)}) copy-start(f32[2,3,1,4,8,128]{5,4,3,2,1,0:T(8,128)} %wiener.3) | copy-start | bytes 294916
  9.9 0.8 %copy-start.4 = (f32[3,4,8,128]{3,2,1,0:T(8,128)S(1)}, f32[3,4,8,128]{3,2,1,0:T(8,128)}, u32[]{:S(2)}) copy-start(f32[3,4,8,128]{3,2,1,0:T(8,128)} %velocity.3) | copy-start | bytes 147460
  10.7 12.8 %copy-start.8 = (f32[4,8,128]{2,1,0:T(8,128)S(1)}, f32[4,8,128]{2,1,0:T(8,128)}, u32[]{:S(2)}) copy-start(f32[4,8,128]{2,1,0:T(8,128)} %mix_rate.3) | copy-start | bytes 49156
  15.0 15.6 %copy-start.3 = (f32[2,3,1,4,8,128]{5,4,3,2,1,0:T(8,128)S(1)}, f32[2,3,1,4,8,128]{5,4,3,2,1,0:T(8,128)}, u32[]{:S(2)}) copy-start(f32[2,3,1,4,8,128]{5,4,3,2,1,0:T(8,128)} %wiener.3) | copy-start | bytes 294916
  15.0 15.6 %copy-start.5 = (f32[3,4,8,128]{3,2,1,0:T(8,128)S(1)}, f32[3,4,8,128]{3,2,1,0:T(8,128)}, u32[]{:S(2)}) copy-start(f32[3,4,8,128]{3,2,1,0:T(8,128)} %velocity.3) | copy-start | bytes 147460
  15.0 8.4 %collective-permute-start.4 = (f32[16,4,8,128]{3,2,1,0:T(8,128)S(1)}, f32[16,4,8,128]{3,2,1,0:T(8,128)S(1)}, u32[]{:S(2)}, u32[]{:S(2)}) collective-permute-start(f32[16,4,8,128]{3,2,1,0:T(8,128)S(1)} %step.2.mine), channel_id=1, source_target_pairs={{0,16},{16,0},{1,17},{17,1},{2,18},{18,2},{3,19},{19,3},{4,20},{20... | collective-permute-start | bytes 786440 | tf_op jit(solution)/shard_map/ppermute | solution.py:298
  23.6 6.9 %collective-permute-start.5 = (f32[16,8,128]{2,1,0:T(8,128)S(1)}, f32[16,8,128]{2,1,0:T(8,128)S(1)}, u32[]{:S(2)}, u32[]{:S(2)}) collective-permute-start(f32[16,8,128]{2,1,0:T(8,128)S(1)} %get-tuple-element.23), channel_id=1, source_target_pairs={{0,4},{8,12},{4,0},{12,8},{1,5},{9,13},{5,1},{13,9},{2,6},{10,14},... | collective-permute-start | bytes 196616 | tf_op jit(solution)/shard_map/ppermute | solution.py:239
  26.6 4.0 %collective-permute-start.6 = (f32[16,8,128]{2,1,0:T(8,128)S(1)}, f32[16,8,128]{2,1,0:T(8,128)S(1)}, u32[]{:S(2)}, u32[]{:S(2)}) collective-permute-start(f32[16,8,128]{2,1,0:T(8,128)S(1)} %get-tuple-element.24), channel_id=1, source_target_pairs={{4,8},{5,9},{6,10},{7,11},{8,4},{9,5},{10,6},{11,7},{0,1},{1,0},{2... | collective-permute-start | bytes 196616 | tf_op jit(solution)/shard_map/ppermute | solution.py:234
  26.6 1.6 %collective-permute-start.7 = (f32[16,4,128]{2,1,0:T(4,128)S(1)}, f32[16,4,128]{2,1,0:T(4,128)S(1)}, u32[]{:S(2)}, u32[]{:S(2)}) collective-permute-start(f32[16,4,128]{2,1,0:T(4,128)S(1)} %get-tuple-element.25), channel_id=1, source_target_pairs={{0,1},{2,3},{1,0},{3,2},{4,5},{6,7},{5,4},{7,6},{8,9},{10,11},{9,8... | collective-permute-start | bytes 98312 | tf_op jit(solution)/shard_map/ppermute | solution.py:239
  27.1 3.5 %collective-permute-start.8 = (f32[16,4,128]{2,1,0:T(4,128)S(1)}, f32[16,4,128]{2,1,0:T(4,128)S(1)}, u32[]{:S(2)}, u32[]{:S(2)}) collective-permute-start(f32[16,4,128]{2,1,0:T(4,128)S(1)} %get-tuple-element.26), channel_id=1, source_target_pairs={{1,2},{2,1},{0,3},{3,0},{5,6},{6,5},{4,7},{7,4},{9,10},{10,9},{8,1... | collective-permute-start | bytes 98312 | tf_op jit(solution)/shard_map/ppermute | solution.py:239
  35.0 8.4 %collective-permute-start.9 = (f32[16,4,8,128]{3,2,1,0:T(8,128)S(1)}, f32[16,4,8,128]{3,2,1,0:T(8,128)S(1)}, u32[]{:S(2)}, u32[]{:S(2)}) collective-permute-start(f32[16,4,8,128]{3,2,1,0:T(8,128)S(1)} %step.3.mine), channel_id=1, source_target_pairs={{0,16},{16,0},{1,17},{17,1},{2,18},{18,2},{3,19},{19,3},{4,20},{20... | collective-permute-start | bytes 786440 | tf_op jit(solution)/shard_map/ppermute | solution.py:298

commit v3 on v0

v3 whole, which is shorter than its diff:
```python
import functools

import jax
import jax.numpy as jnp
from jax import lax
from jax.experimental import pallas as pl
from jax.experimental.pallas import tpu as pltpu
from jax.sharding import PartitionSpec as P

SUBSTEPS = 12
STEPS = 2
CHEM_STEP = 0.04
LOG2E = 1.4426950408889634
LN2 = 0.6931471805599453
TILE = 256
VMEM = pl.BlockSpec(memory_space=pltpu.VMEM)
HBM = pl.BlockSpec(memory_space=pltpu.HBM)


def roundup(n, m):
    return (n + m - 1) // m * m


def split(x):
    hi = x.astype(jnp.bfloat16)
    lo = (x - hi.astype(jnp.float32)).astype(jnp.bfloat16)
    return hi, lo


def shape_of(*dims, dtype=jnp.float32):
    return jax.ShapeDtypeStruct(dims, dtype)


def call(kernel, name, mib, out_shape, *args, in_specs=None, scratch_shapes=()):
    return pl.pallas_call(
        kernel,
        out_shape=out_shape,
        in_specs=in_specs or [VMEM] * len(args),
        out_specs=[VMEM] * len(out_shape),
        scratch_shapes=scratch_shapes,
        compiler_params=pltpu.CompilerParams(vmem_limit_bytes=mib * 2**20),
        name=name,
    )(*args)


def swaps(count):
    pairs = [[(i, i + 1) for i in range(start, count - 1, 2)] for start in (0, 1)]
    return [(p, sorted(set(range(count)) - {i for q in p for i in q})) for p in pairs]


def swap(value, axis, pairs, rest, other=None):
    both = pairs + [(j, i) for i, j in pairs]
    if other is not None and rest and lax.axis_size(other) % 2 == 0:
        n = lax.axis_size(other)
        joint = [(i * n + k, j * n + k) for i, j in both for k in range(n)]
        joint += [(i * n + k, i * n + k + 1 - 2 * (k % 2)) for i in rest for k in range(n)]
        return lax.ppermute(value, (axis, other), joint)
    if len(rest) == 2:
        both = both + [tuple(rest), tuple(rest[::-1])]
    else:
        both = both + [(i, i) for i in rest]
    return lax.ppermute(value, axis, both)


def exchange(x1, x2, y1, y2):
    (a, rest_a), (b, rest_b) = swaps(lax.axis_size("gx"))
    (c, rest_c), (d, rest_d) = swaps(lax.axis_size("gy"))
    return (
        swap(x1, "gx", a, rest_a, "gy"),
        swap(x2, "gx", b, rest_b, "gy"),
        swap(y1, "gy", c, rest_c),
        swap(y2, "gy", d, rest_d),
    )


def sides(axis):
    here, count = lax.axis_index(axis), lax.axis_size(axis)
    even = lax.rem(here, 2) == 0
    return even, here == 0, here == count - 1


def picked(even, low, high):
    return jnp.where(even, high, low), jnp.where(even, low, high)


def send_faces(conc, s, x1, x2, y1, y2, row):
    nx, ny = conc.shape[-3], conc.shape[-2]
    even, _, _ = sides("gx")
    for ref, x in zip((x1, x2), picked(even, 0, nx - 1)):
        ref[row] = conc[s, x]
    even, _, _ = sides("gy")
    y1[row], y2[row] = picked(even, conc[s, :, 0, :], conc[s, :, ny - 1, :])


def halo(axis, first, second):
    even, lowest, highest = sides(axis)
    above = jnp.where(highest, 0.0, jnp.where(even, first, second))
    below = jnp.where(lowest, 0.0, jnp.where(even, second, first))
    return above, below


def lanes(like):
    return lax.broadcasted_iota(jnp.int32, like, len(like) - 1)


def kept(dims):
    half = dims[-1] // 2
    return (lanes(dims) >= half) == (lax.axis_index("field") == 1)


def turned(value):
    return pltpu.roll(value, value.shape[-1] // 2, value.ndim - 1)


def doubled(value):
    return jnp.where(kept(value.shape), value, turned(value))


def packed(low, high, mask):
    return jnp.where(mask, low, turned(high))


def shifted(value, above, below):
    ny = value.shape[0]
    sub = lax.broadcasted_iota(jnp.int32, value.shape, 0)
    up = jnp.where(sub == ny - 1, above, pltpu.roll(value, ny - 1, 0))
    down = jnp.where(sub == 0, below, pltpu.roll(value, 1, 0))
    return up, down


def means(gamma, x1, x2, y1, y2):
    nx, ny, nz = gamma.shape
    last = x1.shape[0] - 1
    lane = lanes((ny, nz))
    x_above, x_below = halo("gx", x1[last], x2[last])
    y_above, y_below = halo("gy", y1[last], y2[last])
    result = []
    for x in range(nx):
        g = gamma[x]
        pairs = [
            (
                x_above if x == nx - 1 else gamma[x + 1],
                x_below if x == 0 else gamma[x - 1],
            ),
            shifted(g, y_above[x : x + 1], y_below[x : x + 1]),
            (
                jnp.where(lane == nz - 1, 0.0, pltpu.roll(g, nz - 1, 1)),
                jnp.where(lane == 0, 0.0, pltpu.roll(g, 1, 1)),
            ),
        ]
        result.append([(0.5 * (g + up), 0.5 * (g + down)) for up, down in pairs])
    return result


def stencil(pairs, drifts, top, bottom):
    total = sum(up + down for up, down in pairs)
    coef = [(1.0 - total) * LOG2E]
    for (up, down), drift in zip(pairs, drifts):
        coef += [(up + drift) * LOG2E, (down - drift) * LOG2E]
    coef[5] = jnp.where(top, 0.0, coef[5])
    coef[6] = jnp.where(bottom, 0.0, coef[6])
    return coef


def move(conc, s, coefs, x1, x2, y1, y2, along_z):
    nx = conc.shape[1]
    x_above, x_below = halo("gx", x1[s], x2[s])
    y_above, y_below = halo("gy", y1[s], y2[s])
    for x in range(nx):
        centre, xu, xd, yu, yd, zu, zd = coefs[x]
        p = conc[s, x]
        px_up = x_above if x == nx - 1 else conc[s, x + 1]
        px_down = x_below if x == 0 else conc[s, x - 1]
        py_up, py_down = shifted(p, y_above[x : x + 1], y_below[x : x + 1])
        pz_up, pz_down = along_z(p, s * nx + x)
        yield (centre * p + (xu * px_up + xd * px_down)) + (
            (yu * py_up + yd * py_down) + (zu * pz_up + zd * pz_down)
        )


def whole_z(p, item):
    nz = p.shape[1]
    return pltpu.roll(p, nz - 1, 1), pltpu.roll(p, 1, 1)


def chemistry(state, gather, scatter):
    ns, cells = state.shape
    tiles = cells // TILE
    table, net = gather[...][:, : 3 * ns], scatter[...]
    nr = table.shape[0] // 2
    steps = SUBSTEPS * tiles
    lag = tiles // 2
    both, change = {}, {}

    def cut(t):
        return slice(t % tiles * TILE, (t % tiles + 1) * TILE)

    for t in range(steps + 2 * lag):
        done = t - 2 * lag
        if done >= 0:
            state[:, cut(done)] += change.pop(done)
        if t < steps:
            u = state[:, cut(t)]
            sp = jnp.maximum(u, jnp.log2(1.0 + jnp.exp2(jnp.minimum(u, 120.0))))
            hi, lo = split(sp)
            both[t] = jnp.dot(
                table,
                jnp.concatenate([hi, lo, hi], axis=0),
                preferred_element_type=jnp.float32,
            )
        ready = t - lag
        if 0 <= ready < steps:
            pair = both.pop(ready).reshape(nr // 8, 2, 8, TILE)
            hi, lo = split((pair[:, 0] * pair[:, 1]).reshape(nr, TILE))
            change[ready] = jnp.dot(
                net, jnp.concatenate([hi, lo], axis=0), preferred_element_type=jnp.float32
            )


def react(rows, state, gather, scatter):
    ns = state.shape[0]
    nz = rows.shape[1]
    stride = rows.shape[0] // ns
    chunks = state.shape[1] // nz
    for j in range(chunks):
        state[:, j * nz : (j + 1) * nz] = rows[pl.ds(j, ns, stride=stride), :]
    chemistry(state, gather, scatter)
    for j in range(chunks):
        rows[pl.ds(j, ns, stride=stride), :] = state[:, j * nz : (j + 1) * nz] * LN2


def scratch(ns, nx, ny, nz):
    stride = roundup(nx * ny, 32) + 1
    return [
        pltpu.VMEM((ns * stride, nz), jnp.float32),
        pltpu.VMEM((ns, nx * ny * nz), jnp.float32),
    ]


def mixing(pairs, count, mix_rate):
    ns, get = pairs
    spread, energy = jnp.zeros_like(mix_rate), jnp.zeros_like(mix_rate)
    for s in range(ns):
        a, b = get(s)
        mean = (a + b) * (1.0 / count)
        meansq = (a * a + b * b) * (1.0 / count)
        spread = spread + (meansq - mean * mean)
        energy = energy + meansq
    decay = jnp.exp(-0.5 * (mix_rate * (1.0 + spread / (1.0 + energy))))
    for s in range(ns):
        a, b = get(s)
        mean = (a + b) * (1.0 / count)
        yield mean + (a - mean) * decay, mean + (b - mean) * decay


def faces_kernel(conc_in, gamma_in, x1, x2, y1, y2, conc, gamma, sems):
    ns = conc.shape[0]
    copies = [
        pltpu.make_async_copy(conc_in, conc, sems.at[0]),
        pltpu.make_async_copy(gamma_in, gamma, sems.at[1]),
    ]
    for copy in copies:
        copy.start()
    for copy in copies:
        copy.wait()
    for s in range(ns):
        send_faces(conc, s, x1, x2, y1, y2, s)
    send_faces(gamma, 0, x1, x2, y1, y2, ns)


def tables_kernel(ns, reactions, rates, gather, scatter):
    nr = reactions.shape[1]
    depth = gather.shape[1]
    row = lax.broadcasted_iota(jnp.int32, (depth, nr), 0)
    scalar, part = lax.rem(row, ns), lax.div(row, ns)
    k = rates[...] * (CHEM_STEP * LN2)
    k_hi = k.astype(jnp.bfloat16).astype(jnp.float32)
    k_lo = k - k_hi

    def column(c):
        return jnp.where(scalar == reactions[c : c + 1, :], 1.0, 0.0)

    first, second, third, fourth = (column(c) for c in range(4))
    weight = jnp.where(part < 2, k_hi, jnp.where(part == 2, k_lo, 0.0))
    both = jnp.concatenate(
        [first * weight, second * jnp.where(part < 2, 1.0, 0.0)], axis=1
    ).T
    for j in range(nr // 8):
        block = [both[c + 8 * j : c + 8 * j + 8, :] for c in (0, nr)]
        gather[16 * j : 16 * j + 16, :] = jnp.concatenate(block, axis=0).astype(jnp.bfloat16)
    net = (third + fourth - first - second)[:ns].astype(jnp.bfloat16)
    scatter[...] = jnp.concatenate([net, net], axis=1)


def prepare_kernel(
    ns, reactions, rates, gamma, velocity, wiener, mix_rate,
    gather, scatter, drift, amp, speed, noise, noise_out, mix_packed, mix_doubled
):
    tables_kernel(ns, reactions, rates, gather, scatter)
    nx = gamma.shape[1]
    own = kept(gamma.shape[2:])
    for x in range(nx):
        root = jnp.sqrt(2.0 * gamma[0, x])
        amp[x] = doubled(root)
        mix_doubled[x] = doubled(mix_rate[x])
        for d in range(3):
            drift[d, x] = 0.5 * (root * wiener[0, d, 0, x] - velocity[d, x])
            speed[d, x] = doubled(velocity[d, x])
            noise[d, x] = wiener[1, d, 0, x]
    for x in range(nx // 2):
        mix_packed[x] = packed(mix_rate[x], mix_rate[x + nx // 2], own)
        for d in range(3):
            noise_out[d * (nx // 2) + x] = packed(
                wiener[1, d, 0, x], wiener[1, d, 0, x + nx // 2], jnp.logical_not(own)
            )


def leave_kernel(conc, x1, x2, y1, y2, gamma, drift, mine, theirs):
    ns, nx, ny, nz = conc.shape
    own = kept((ny, nz))
    lane = lanes((ny, nz))
    pairs = means(gamma.at[0], x1, x2, y1, y2)
    coefs = [
        stencil(pairs[x], [drift[d, x] for d in range(3)], lane == nz - 1, lane == 0)
        for x in range(nx)
    ]
    for s in range(ns):
        moved = list(move(conc, s, coefs, x1, x2, y1, y2, whole_z))
        for x in range(nx // 2):
            mine[s, x] = packed(moved[x], moved[x + nx // 2], own)
            theirs[s, x] = packed(moved[x], moved[x + nx // 2], jnp.logical_not(own))


def coefs_kernel(gamma, x1, x2, y1, y2, ups, downs):
    pairs = means(gamma.at[0], x1, x2, y1, y2)
    for x, plane in enumerate(pairs):
        for d, (up, down) in enumerate(plane):
            ups[d, x] = doubled(up)
            downs[d, x] = doubled(down)


def first_kernel(
    count, mine, theirs, gather, scatter, mix_rate, noise_out,
    conc, x1, x2, y1, y2, side, rows, state
):
    ns, nx, ny, nz = conc.shape
    half = nx // 2
    stride = rows.shape[0] // ns
    own = kept((ny, nz))
    is_first = lax.axis_index("field") == 0

    def place(s, field, x):
        start = s * stride + (field * half + x) * ny
        return slice(start, start + ny)

    for s in range(ns):
        for x in range(half):
            rows[place(s, 0, x), :] = mine[s, x]
            rows[place(s, 1, x), :] = theirs[s, x]
    react(rows, state, gather, scatter)
    for x in range(half):
        mixed = mixing(
            (ns, lambda s: (rows[place(s, 0, x), :], rows[place(s, 1, x), :])),
            count,
            mix_rate[x],
        )
        for s, (a, b) in enumerate(mixed):
            conc[s, x] = packed(a, b, own)
            conc[s, x + half] = jnp.where(own, turned(a), b)
    per = nz // 2
    lane = lax.rem(lanes((ny, nz)), per)
    parts = side.shape[0] - noise_out.shape[0]
    for part in range(parts):
        column = jnp.zeros((ny, nz), jnp.float32)
        for item in range(part * per, min(ns * nx, (part + 1) * per)):
            j = item % per
            shift = jnp.where(is_first, (j + per + 1) % nz, j)
            value = pltpu.roll(conc[item // nx, item % nx], shift, 1)
            column = jnp.where(lane == j, value, column)
        side[part] = column
    side[parts:] = noise_out[...]
    for s in range(ns):
        send_faces(conc, s, x1, x2, y1, y2, s)


def second_kernel(
    count, conc, x1, x2, y1, y2, side, ups, downs, amp, speed, noise, gather, scatter, mix_rate,
    mine, theirs, rows, state
):
    ns, nx, ny, nz = conc.shape
    half, per = nx // 2, nz // 2
    stride = rows.shape[0] // ns
    own = kept((ny, nz))
    is_first = lax.axis_index("field") == 0
    lane = lax.rem(lanes((ny, nz)), per)
    at_top, at_bottom = lane == per - 1, lane == 0
    top = jnp.logical_and(at_top, jnp.logical_not(is_first))
    bottom = jnp.logical_and(at_bottom, is_first)
    parts = side.shape[0] - 3 * half

    def half_z(p, item):
        j = item % per
        shift = jnp.where(is_first, per - 1 - j, (nz - j) % nz)
        edge = pltpu.roll(side[item // per], shift, 1)
        up, down = whole_z(p, item)
        return jnp.where(at_top, edge, up), jnp.where(at_bottom, edge, down)

    coefs = []
    for x in range(nx):
        drifts = []
        for d in range(3):
            got = side[parts + d * half + x % half]
            other = turned(got) if x < half else got
            drifts.append(0.5 * (amp[x] * jnp.where(own, noise[d, x], other) - speed[d, x]))
        pairs = [(ups[d, x], downs[d, x]) for d in range(3)]
        coefs.append(stencil(pairs, drifts, top, bottom))
    for s in range(ns):
        for x, moved in enumerate(move(conc, s, coefs, x1, x2, y1, y2, half_z)):
            rows[s * stride + x * ny : s * stride + (x + 1) * ny, :] = moved
    react(rows, state, gather, scatter)

    def field_pair(x):
        def get(s):
            a = rows[s * stride + x * ny : s * stride + (x + 1) * ny, :]
            return a, turned(a)

        return get

    for x in range(half):
        low = mixing((ns, field_pair(x)), count, mix_rate[x])
        high = mixing((ns, field_pair(x + half)), count, mix_rate[x + half])
        for s, ((a, _), (b, _)) in enumerate(zip(low, high)):
            mine[s, x] = a
            mine[s, x + half] = b
            theirs[s, x] = packed(a, b, jnp.logical_not(own))


def join_kernel(mine, theirs, out):
    ns, nx, ny, nz = mine.shape
    half = nx // 2
    own = kept((ny, nz))
    for s in range(ns):
        for x in range(half):
            out[s, x] = packed(mine[s, x], theirs[s, x], own)
            out[s, x + half] = jnp.where(own, mine[s, x + half], theirs[s, x])


def step_kernel(
    step, conc, x1, x2, y1, y2, gamma, gx1, gx2, gy1, gy2, velocity, wiener, gather, scatter,
    out, rows, state
):
    ns, nx, ny, nz = conc.shape
    stride = rows.shape[0] // ns
    lane = lanes((ny, nz))
    pairs = means(gamma.at[0], gx1, gx2, gy1, gy2)
    coefs = []
    for x in range(nx):
        amp = jnp.sqrt(2.0 * gamma[0, x])
        drifts = [0.5 * (amp * wiener[step, d, 0, x] - velocity[d, x]) for d in range(3)]
        coefs.append(stencil(pairs[x], drifts, lane == nz - 1, lane == 0))
    for s in range(ns):
        for x, moved in enumerate(move(conc, s, coefs, x1, x2, y1, y2, whole_z)):
            rows[s * stride + x * ny : s * stride + (x + 1) * ny, :] = moved
    react(rows, state, gather, scatter)
    for s in range(ns):
        for x in range(nx):
            out[s, x] = rows[s * stride + x * ny : s * stride + (x + 1) * ny, :]


def closure(first, second, count, mix_rate):
    mean = first / count
    meansq = second / count
    spread = jnp.sum(meansq - mean * mean, axis=0)
    energy = jnp.sum(meansq, axis=0)
    omega = mix_rate * (1.0 + spread / (1.0 + energy))
    return (mean, jnp.exp(-0.5 * omega))


def on_device(concentrations, velocity, diffusivity, wiener, mix_rate, rate_constants, reactions):
    ns, nx, ny, nz = concentrations.shape[1:]
    nr = reactions.shape[0]
    count = lax.axis_size("field")
    rates = rate_constants.reshape(1, nr)
    table_shapes = [
        shape_of(2 * nr, 128, dtype=jnp.bfloat16), shape_of(ns, 2 * nr, dtype=jnp.bfloat16)
    ]
    face_dims = [(ny, nz), (ny, nz), (nx, nz), (nx, nz)]
    faces = [shape_of(ns, *d) for d in face_dims]
    block = shape_of(ns, nx, ny, nz)
    *sent, conc, gamma = call(
        faces_kernel, "faces", 4,
        [shape_of(ns + 1, *d) for d in face_dims] + [block, shape_of(1, nx, ny, nz)],
        concentrations[0], diffusivity[None],
        in_specs=[HBM] * 2, scratch_shapes=[pltpu.SemaphoreType.DMA((2,))],
    )
    halos = exchange(*sent)
    if count == 2 and STEPS == 2 and nx % 2 == 0 and nz == 128:
        half = shape_of(ns, nx // 2, ny, nz)
        partner = [(0, 1), (1, 0)]
        vectors, planes = shape_of(3, nx, ny, nz), shape_of(nx, ny, nz)
        noise_dims = 3 * (nx // 2)
        gather, scatter, drift, amp, speed, noise, noise_out, mix_packed, mix_doubled = call(
            functools.partial(prepare_kernel, ns), "prepare", 4,
            table_shapes
            + [vectors, planes, vectors, vectors, shape_of(noise_dims, ny, nz)]
            + [shape_of(nx // 2, ny, nz), planes],
            reactions.T, rates, gamma, velocity, wiener, mix_rate,
        )
        mine, theirs = call(
            leave_kernel, "leave", 4, [half, half], conc, *halos, gamma, drift
        )
        theirs = lax.ppermute(theirs, "field", partner)
        ups, downs = call(coefs_kernel, "coefs", 4, [vectors, vectors], gamma, *halos)
        parts = -(-ns * nx // (nz // 2))
        conc, *sent, side = call(
            functools.partial(first_kernel, count), "first", 8,
            [block] + faces + [shape_of(parts + noise_dims, ny, nz)],
            mine, theirs, gather, scatter, mix_packed, noise_out,
            scratch_shapes=scratch(ns, nx, ny, nz),
        )
        halos = exchange(*sent)
        side = lax.ppermute(side, "field", partner)
        mine, theirs = call(
            functools.partial(second_kernel, count), "second", 8, [block, half],
            conc, *halos, side, ups, downs, amp, speed, noise, gather, scatter, mix_doubled,
            scratch_shapes=scratch(ns, nx, ny, nz),
        )
        theirs = lax.ppermute(theirs, "field", partner)
        (out,) = call(join_kernel, "join", 4, [block], mine, theirs)
        return out[None]
    gather, scatter = call(
        functools.partial(tables_kernel, ns), "tables", 2, table_shapes, reactions.T, rates
    )
    gamma_halos = halos
    for step_index in range(STEPS):
        (reacted,) = call(
            functools.partial(step_kernel, step_index), "step", 8, [block],
            conc, *halos, gamma, *gamma_halos, velocity, wiener, gather, scatter,
            scratch_shapes=scratch(ns, nx, ny, nz),
        )
        first = lax.psum(reacted, "field")
        second = lax.psum(reacted * reacted, "field")
        mean, decay = closure(first, second, count, mix_rate)
        conc = mean + (reacted - mean) * decay
        if step_index < STEPS - 1:
            sent = picked(sides("gx")[0], conc[:, 0], conc[:, -1])
            sent += picked(sides("gy")[0], conc[:, :, 0], conc[:, :, -1])
            halos = exchange(*sent)
    return conc[None]


def solution(mesh):
    return jax.shard_map(
        on_device,
        mesh=mesh,
        in_specs=(
            P("field", None, "gx", "gy", None),
            P(None, "gx", "gy", None),
            P("gx", "gy", None),
            P(None, None, "field", "gx", "gy", None),
            P("gx", "gy", None),
            P(),
            P(),
        ),
        out_specs=P("field", None, "gx", "gy", None),
        check_vma=False,
    )
```

time: 198 us -> 38.7 us (0.20)
  matrix products: 130 us -> 0 us
  blocking collectives: 16.7 us -> 0 us
  starting transfers between devices: 30.1 us -> 13.9 us
  Pallas kernels: 0 us -> 10.9 us
  other arithmetic: 6.65 us -> 0 us
  waiting for transfers between devices: 8.18 us -> 11.3 us
    dot_general x48 -> x0, matrix products: 130 us -> none  [the longest x24 83.5 us: substep(): jnp.dot(react, logs, precision=highest)]
    all_gather x2 -> x0, blocking collectives: 16.7 us -> none  [on_device(): every = lax.all_gather(conc[None], 'field', axis=0, tiled=True)]
    ppermute x12 -> x11, starting transfers between devices: 30.1 us -> 13.9 us  [the longest x6 9.3 us: swap(): return lax.ppermute(value, axis, both)]
    pallas_call x0 -> x7, Pallas kernels: none -> 10.9 us  [call(): pl.pallas_call(kernel, out_shape=out_shape, in_specs=in_specs or [VMEM] *...]
    ppermute x12 -> x11, waiting for transfers between devices: 8.18 us -> 11.3 us  [the longest x2 7.5 us: on_device(): theirs = lax.ppermute(theirs, 'field', partner)]
    concatenate x5 -> x0, other arithmetic: 3.04 us -> none  [padded_2(): block = jnp.concatenate([low, block, high], axis=dim)]
  transfers between devices with their start and end apart: 12 -> 11, of which waited for: 5 -> 4; matrix products, arithmetic and copies ran while one was open for 2% -> 0% of each run, Pallas kernels for 0% -> 1%
where the time goes in v3:
time: 38.7 us; the launch traced here: 38.5 us
  starting transfers between devices  13.9 us (36%)
  waiting for transfers between devices  11.3 us (29%)
  Pallas kernels  10.9 us (28%)
  local copies, waits for them, and re-layouts  2.34 us (6%)
    pallas_call x7, Pallas kernels, call(): pl.pallas_call(kernel, out_shape=out_shape, in_specs=in_specs or [VMEM] *...  10.9 us
    ppermute x6, starting transfers between devices, swap(): return lax.ppermute(value, axis, both)  9.3 us
    ppermute x2, waiting for transfers between devices, on_device(): theirs = lax.ppermute(theirs, 'field', partner)  7.5 us
    ppermute x2, starting transfers between devices, on_device(): theirs = lax.ppermute(theirs, 'field', partner)  3.11 us
    unnamed x14, local copies, waits for them, and re-layouts  2.34 us
    ppermute x1, waiting for transfers between devices, on_device(): side = lax.ppermute(side, 'field', partner)  2.24 us
    ppermute x6, waiting for transfers between devices, swap(): return lax.ppermute(value, axis, both)  1.56 us
    ppermute x1, starting transfers between devices, on_device(): side = lax.ppermute(side, 'field', partner)  1.49 us
  transfers between devices with their start and end apart: 11, of which 4 were waited for; matrix products, arithmetic and copies ran while one was open for 0% of the time, Pallas kernels for 1%

profile of v3, /device:TPU:0, one launch (start us, length us, event | category | flops | bytes accessed | tf_op | source)
XLA Modules:
  0.0 38.5 jit_solution(1710153015558766853)
XLA Ops:
  0.0 0.9 %copy-done = f32[1,16,4,8,128]{4,3,2,1,0:T(8,128)S(1)} copy-done((f32[1,16,4,8,128]{4,3,2,1,0:T(8,128)S(1)}, f32[1,16,4,8,128]{4,3,2,1,0:T(8,128)}, u32[]{:S(2)}) %copy-start) | copy-done | bytes 262168
  1.0 0.7 %copy-done.3 = f32[4,8,128]{2,1,0:T(8,128)S(1)} copy-done((f32[4,8,128]{2,1,0:T(8,128)S(1)}, f32[4,8,128]{2,1,0:T(8,128)}, u32[]{:S(2)}) %copy-start.3) | copy-done | bytes 16408
  1.7 0.1 faces.1
  1.8 3.1 %collective-permute-start = (f32[17,8,128]{2,1,0:T(8,128)S(1)}, f32[17,8,128]{2,1,0:T(8,128)S(1)}, u32[]{:S(2)}, u32[]{:S(2)}) collective-permute-start(f32[17,8,128]{2,1,0:T(8,128)S(1)} %get-tuple-element.33), channel_id=1, source_target_pairs={{0,4},{8,12},{4,0},{12,8},{1,5},{9,13},{5,1},{13,9},{2,6},{10,14},... | collective-permute-start | bytes 208904 | tf_op jit(solution)/shard_map/ppermute | solution.py:62
  4.9 0.0 collective-permute-start.1
  4.9 0.5 %collective-permute-start.2 = (f32[17,4,128]{2,1,0:T(4,128)S(1)}, f32[17,4,128]{2,1,0:T(4,128)S(1)}, u32[]{:S(2)}, u32[]{:S(2)}) collective-permute-start(f32[17,4,128]{2,1,0:T(4,128)S(1)} %get-tuple-element.35), channel_id=1, source_target_pairs={{0,1},{2,3},{1,0},{3,2},{4,5},{6,7},{5,4},{7,6},{8,9},{10,11},{9,8... | collective-permute-start | bytes 104456 | tf_op jit(solution)/shard_map/ppermute | solution.py:62
  5.4 1.1 %collective-permute-start.3 = (f32[17,4,128]{2,1,0:T(4,128)S(1)}, f32[17,4,128]{2,1,0:T(4,128)S(1)}, u32[]{:S(2)}, u32[]{:S(2)}) collective-permute-start(f32[17,4,128]{2,1,0:T(4,128)S(1)} %get-tuple-element.36), channel_id=1, source_target_pairs={{1,2},{2,1},{0,3},{3,0},{5,6},{6,5},{4,7},{7,4},{9,10},{10,9},{8,1... | collective-permute-start | bytes 104456 | tf_op jit(solution)/shard_map/ppermute | solution.py:62
  6.6 0.7 %copy-done.5 = s32[64,4]{0,1:T(4,128)S(1)} copy-done((s32[64,4]{0,1:T(4,128)S(1)}, s32[64,4]{0,1:T(4,128)}, u32[]{:S(2)}) %copy-start.5) | copy-done | bytes 1048
  7.2 0.2 prepare.1
  7.4 1.5 %collective-permute-done.3.y2 = f32[17,4,128]{2,1,0:T(4,128)S(1)} collective-permute-done((f32[17,4,128]{2,1,0:T(4,128)S(1)}, f32[17,4,128]{2,1,0:T(4,128)S(1)}, u32[]{:S(2)}, u32[]{:S(2)}) %collective-permute-start.3) | collective-permute-done | bytes 34848 | tf_op jit(solution)/shard_map/ppermute | solution.py:62
  9.0 0.5 %leave.1 = (f32[16,2,8,128]{3,2,1,0:T(8,128)S(1)}, f32[16,2,8,128]{3,2,1,0:T(8,128)S(1)}) custom-call(f32[16,4,8,128]{3,2,1,0:T(8,128)S(1)} %get-tuple-element.32.conc, f32[17,8,128]{2,1,0:T(8,128)S(1)} %collective-permute-done.x1, f32[17,8,128]{2,1,0:T(8,128)S(1)} %collective-permute-done.1.x2, f32[17,4,128]{2,1,0:T(4,128)S(1)} %collective-permute-done.2.y1, ...), custom_call_target="tpu_custom_call" | custom-call | tf_op jit(solution)/shard_map/leave/pallas_call | solution.py:35
  9.5 1.6 %collective-permute-start.4 = (f32[16,2,8,128]{3,2,1,0:T(8,128)S(1)}, f32[16,2,8,128]{3,2,1,0:T(8,128)S(1)}, u32[]{:S(2)}, u32[]{:S(2)}) collective-permute-start(f32[16,2,8,128]{3,2,1,0:T(8,128)S(1)} %get-tuple-element.40), channel_id=1, source_target_pairs={{0,16},{16,0},{1,17},{17,1},{2,18},{18,2},{3,19},{19,3},{4,20},{20... | collective-permute-start | bytes 393224 | tf_op jit(solution)/shard_map/ppermute | solution.py:512
  11.0 4.0 %collective-permute-done.4.theirs = f32[16,2,8,128]{3,2,1,0:T(8,128)S(1)} collective-permute-done((f32[16,2,8,128]{3,2,1,0:T(8,128)S(1)}, f32[16,2,8,128]{3,2,1,0:T(8,128)S(1)}, u32[]{:S(2)}, u32[]{:S(2)}) %collective-permute-start.4) | collective-permute-done | bytes 131104 | tf_op jit(solution)/shard_map/ppermute | solution.py:512
  15.1 4.5 %first.1 = (f32[16,4,8,128]{3,2,1,0:T(8,128)S(1)}, f32[16,8,128]{2,1,0:T(8,128)S(1)}, f32[16,8,128]{2,1,0:T(8,128)S(1)}, f32[16,4,128]{2,1,0:T(4,128)S(1)}, f32[...) custom-call(f32[16,2,8,128]{3,2,1,0:T(8,128)S(1)} %get-tuple-element.39.mine, ...), custom_call_target="tpu_custom_call" | custom-call | tf_op jit(solution)/shard_map/first/pallas_call | solution.py:35
  19.6 2.9 %collective-permute-start.5 = (f32[16,8,128]{2,1,0:T(8,128)S(1)}, f32[16,8,128]{2,1,0:T(8,128)S(1)}, u32[]{:S(2)}, u32[]{:S(2)}) collective-permute-start(f32[16,8,128]{2,1,0:T(8,128)S(1)} %get-tuple-element.46), channel_id=1, source_target_pairs={{0,4},{8,12},{4,0},{12,8},{1,5},{9,13},{5,1},{13,9},{2,6},{10,14},... | collective-permute-start | bytes 196616 | tf_op jit(solution)/shard_map/ppermute | solution.py:62
  22.5 0.5 %collective-permute-start.7 = (f32[16,4,128]{2,1,0:T(4,128)S(1)}, f32[16,4,128]{2,1,0:T(4,128)S(1)}, u32[]{:S(2)}, u32[]{:S(2)}) collective-permute-start(f32[16,4,128]{2,1,0:T(4,128)S(1)} %get-tuple-element.48), channel_id=1, source_target_pairs={{0,1},{2,3},{1,0},{3,2},{4,5},{6,7},{5,4},{7,6},{8,9},{10,11},{9,8... | collective-permute-start | bytes 98312 | tf_op jit(solution)/shard_map/ppermute | solution.py:62
  23.0 1.1 %collective-permute-start.8 = (f32[16,4,128]{2,1,0:T(4,128)S(1)}, f32[16,4,128]{2,1,0:T(4,128)S(1)}, u32[]{:S(2)}, u32[]{:S(2)}) collective-permute-start(f32[16,4,128]{2,1,0:T(4,128)S(1)} %get-tuple-element.49), channel_id=1, source_target_pairs={{1,2},{2,1},{0,3},{3,0},{5,6},{6,5},{4,7},{7,4},{9,10},{10,9},{8,1... | collective-permute-start | bytes 98312 | tf_op jit(solution)/shard_map/ppermute | solution.py:62
  24.2 1.5 %collective-permute-start.9 = (f32[7,8,128]{2,1,0:T(8,128)S(1)}, f32[7,8,128]{2,1,0:T(8,128)S(1)}, u32[]{:S(2)}, u32[]{:S(2)}) collective-permute-start(f32[7,8,128]{2,1,0:T(8,128)S(1)} %get-tuple-element.50), channel_id=1, source_target_pairs={{0,16},{16,0},{1,17},{17,1},{2,18},{18,2},{3,19},{19,3},{4,20},{20... | collective-permute-start | bytes 86024 | tf_op jit(solution)/shard_map/ppermute | solution.py:522
  25.7 0.1 coefs.1
  25.8 2.2 %collective-permute-done.9.side = f32[7,8,128]{2,1,0:T(8,128)S(1)} collective-permute-done((f32[7,8,128]{2,1,0:T(8,128)S(1)}, f32[7,8,128]{2,1,0:T(8,128)S(1)}, u32[]{:S(2)}, u32[]{:S(2)}) %collective-permute-start.9) | collective-permute-done | bytes 28704 | tf_op jit(solution)/shard_map/ppermute | solution.py:522
  28.1 4.6 %second.1 = (f32[16,4,8,128]{3,2,1,0:T(8,128)S(1)}, f32[16,2,8,128]{3,2,1,0:T(8,128)S(1)}) custom-call(f32[16,4,8,128]{3,2,1,0:T(8,128)S(1)} %get-tuple-element.45.conc, f32[16,8,128]{2,1,0:T(8,128)S(1)} %collective-permute-done.5.x1, f32[16,8,128]{2,1,0:T(8,128)S(1)} %collective-permute-done.6.x2, f32[16,4,128]{2,1,0:T(4,128)S(1)} %collective-permute-done.7.y1, ...), custom_call_target="tpu_custom_call" | custom-call | tf_op jit(solution)/shard_map/second/pallas_call | solution.py:35
  32.6 1.6 %collective-permute-start.10 = (f32[16,2,8,128]{3,2,1,0:T(8,128)S(1)}, f32[16,2,8,128]{3,2,1,0:T(8,128)S(1)}, u32[]{:S(2)}, u32[]{:S(2)}) collective-permute-start(f32[16,2,8,128]{3,2,1,0:T(8,128)S(1)} %get-tuple-element.58), channel_id=1, source_target_pairs={{0,16},{16,0},{1,17},{17,1},{2,18},{18,2},{3,19},{19,3},{4,20},{20... | collective-permute-start | bytes 393224 | tf_op jit(solution)/shard_map/ppermute | solution.py:528
  34.2 3.5 %collective-permute-done.10.theirs = f32[16,2,8,128]{3,2,1,0:T(8,128)S(1)} collective-permute-done((f32[16,2,8,128]{3,2,1,0:T(8,128)S(1)}, f32[16,2,8,128]{3,2,1,0:T(8,128)S(1)}, u32[]{:S(2)}, u32[]{:S(2)}) %collective-permute-start.10) | collective-permute-done | bytes 131104 | tf_op jit(solution)/shard_map/ppermute | solution.py:528
  37.7 0.8 %join.1 = f32[16,4,8,128]{3,2,1,0:T(8,128)} custom-call(f32[16,4,8,128]{3,2,1,0:T(8,128)S(1)} %get-tuple-element.57.mine, f32[16,2,8,128]{3,2,1,0:T(8,128)S(1)} %collective-permute-done.10.theirs), custom_call_target="tpu_custom_call" | custom-call | tf_op jit(solution)/shard_map/join/pallas_call | solution.py:35
  (19 shorter events, 0.0 us)
Async XLA Ops:
  0.0 0.9 %copy-start = (f32[1,16,4,8,128]{4,3,2,1,0:T(8,128)S(1)}, f32[1,16,4,8,128]{4,3,2,1,0:T(8,128)}, u32[]{:S(2)}) copy-start(f32[1,16,4,8,128]{4,3,2,1,0:T(8,128)} %param.7) | copy-start | bytes 786436
  1.0 0.7 %copy-start.3 = (f32[4,8,128]{2,1,0:T(8,128)S(1)}, f32[4,8,128]{2,1,0:T(8,128)}, u32[]{:S(2)}) copy-start(f32[4,8,128]{2,1,0:T(8,128)} %param.9) | copy-start | bytes 49156
  1.7 4.9 %copy-start.1 = (f32[2,3,1,4,8,128]{5,4,3,2,1,0:T(8,128)S(1)}, f32[2,3,1,4,8,128]{5,4,3,2,1,0:T(8,128)}, u32[]{:S(2)}) copy-start(f32[2,3,1,4,8,128]{5,4,3,2,1,0:T(8,128)} %wiener.1) | copy-start | bytes 294916
  1.7 4.9 %copy-start.2 = (f32[3,4,8,128]{3,2,1,0:T(8,128)S(1)}, f32[3,4,8,128]{3,2,1,0:T(8,128)}, u32[]{:S(2)}) copy-start(f32[3,4,8,128]{3,2,1,0:T(8,128)} %velocity.1) | copy-start | bytes 147460
  1.7 4.9 %copy-start.4 = (f32[4,8,128]{2,1,0:T(8,128)S(1)}, f32[4,8,128]{2,1,0:T(8,128)}, u32[]{:S(2)}) copy-start(f32[4,8,128]{2,1,0:T(8,128)} %mix_rate.1) | copy-start | bytes 49156
  1.8 7.2 %collective-permute-start = (f32[17,8,128]{2,1,0:T(8,128)S(1)}, f32[17,8,128]{2,1,0:T(8,128)S(1)}, u32[]{:S(2)}, u32[]{:S(2)}) collective-permute-start(f32[17,8,128]{2,1,0:T(8,128)S(1)} %get-tuple-element.33), channel_id=1, source_target_pairs={{0,4},{8,12},{4,0},{12,8},{1,5},{9,13},{5,1},{13,9},{2,6},{10,14},... | collective-permute-start | bytes 208904 | tf_op jit(solution)/shard_map/ppermute | solution.py:62
  4.9 4.1 %collective-permute-start.1 = (f32[17,8,128]{2,1,0:T(8,128)S(1)}, f32[17,8,128]{2,1,0:T(8,128)S(1)}, u32[]{:S(2)}, u32[]{:S(2)}) collective-permute-start(f32[17,8,128]{2,1,0:T(8,128)S(1)} %get-tuple-element.34), channel_id=1, source_target_pairs={{4,8},{5,9},{6,10},{7,11},{8,4},{9,5},{10,6},{11,7},{0,1},{1,0},{2... | collective-permute-start | bytes 208904 | tf_op jit(solution)/shard_map/ppermute | solution.py:57
  4.9 2.5 %collective-permute-start.2 = (f32[17,4,128]{2,1,0:T(4,128)S(1)}, f32[17,4,128]{2,1,0:T(4,128)S(1)}, u32[]{:S(2)}, u32[]{:S(2)}) collective-permute-start(f32[17,4,128]{2,1,0:T(4,128)S(1)} %get-tuple-element.35), channel_id=1, source_target_pairs={{0,1},{2,3},{1,0},{3,2},{4,5},{6,7},{5,4},{7,6},{8,9},{10,11},{9,8... | collective-permute-start | bytes 104456 | tf_op jit(solution)/shard_map/ppermute | solution.py:62
  5.4 3.5 %collective-permute-start.3 = (f32[17,4,128]{2,1,0:T(4,128)S(1)}, f32[17,4,128]{2,1,0:T(4,128)S(1)}, u32[]{:S(2)}, u32[]{:S(2)}) collective-permute-start(f32[17,4,128]{2,1,0:T(4,128)S(1)} %get-tuple-element.36), channel_id=1, source_target_pairs={{1,2},{2,1},{0,3},{3,0},{5,6},{6,5},{4,7},{7,4},{9,10},{10,9},{8,1... | collective-permute-start | bytes 104456 | tf_op jit(solution)/shard_map/ppermute | solution.py:62
  6.6 0.7 %copy-start.5 = (s32[64,4]{0,1:T(4,128)S(1)}, s32[64,4]{0,1:T(4,128)}, u32[]{:S(2)}) copy-start(s32[64,4]{0,1:T(4,128)} %param.13) | copy-start | bytes 3076
  6.6 0.7 %copy-start.6 = (f32[64]{0:T(128)S(1)}, f32[64]{0:T(128)}, u32[]{:S(2)}) copy-start(f32[64]{0:T(128)} %param.12) | copy-start | bytes 772
  9.5 5.6 %collective-permute-start.4 = (f32[16,2,8,128]{3,2,1,0:T(8,128)S(1)}, f32[16,2,8,128]{3,2,1,0:T(8,128)S(1)}, u32[]{:S(2)}, u32[]{:S(2)}) collective-permute-start(f32[16,2,8,128]{3,2,1,0:T(8,128)S(1)} %get-tuple-element.40), channel_id=1, source_target_pairs={{0,16},{16,0},{1,17},{17,1},{2,18},{18,2},{3,19},{19,3},{4,20},{20... | collective-permute-start | bytes 393224 | tf_op jit(solution)/shard_map/ppermute | solution.py:512
  19.6 8.4 %collective-permute-start.5 = (f32[16,8,128]{2,1,0:T(8,128)S(1)}, f32[16,8,128]{2,1,0:T(8,128)S(1)}, u32[]{:S(2)}, u32[]{:S(2)}) collective-permute-start(f32[16,8,128]{2,1,0:T(8,128)S(1)} %get-tuple-element.46), channel_id=1, source_target_pairs={{0,4},{8,12},{4,0},{12,8},{1,5},{9,13},{5,1},{13,9},{2,6},{10,14},... | collective-permute-start | bytes 196616 | tf_op jit(solution)/shard_map/ppermute | solution.py:62
  22.5 5.5 %collective-permute-start.6 = (f32[16,8,128]{2,1,0:T(8,128)S(1)}, f32[16,8,128]{2,1,0:T(8,128)S(1)}, u32[]{:S(2)}, u32[]{:S(2)}) collective-permute-start(f32[16,8,128]{2,1,0:T(8,128)S(1)} %get-tuple-element.47), channel_id=1, source_target_pairs={{4,8},{5,9},{6,10},{7,11},{8,4},{9,5},{10,6},{11,7},{0,1},{1,0},{2... | collective-permute-start | bytes 196616 | tf_op jit(solution)/shard_map/ppermute | solution.py:57
  22.5 5.5 %collective-permute-start.7 = (f32[16,4,128]{2,1,0:T(4,128)S(1)}, f32[16,4,128]{2,1,0:T(4,128)S(1)}, u32[]{:S(2)}, u32[]{:S(2)}) collective-permute-start(f32[16,4,128]{2,1,0:T(4,128)S(1)} %get-tuple-element.48), channel_id=1, source_target_pairs={{0,1},{2,3},{1,0},{3,2},{4,5},{6,7},{5,4},{7,6},{8,9},{10,11},{9,8... | collective-permute-start | bytes 98312 | tf_op jit(solution)/shard_map/ppermute | solution.py:62
  23.0 5.0 %collective-permute-start.8 = (f32[16,4,128]{2,1,0:T(4,128)S(1)}, f32[16,4,128]{2,1,0:T(4,128)S(1)}, u32[]{:S(2)}, u32[]{:S(2)}) collective-permute-start(f32[16,4,128]{2,1,0:T(4,128)S(1)} %get-tuple-element.49), channel_id=1, source_target_pairs={{1,2},{2,1},{0,3},{3,0},{5,6},{6,5},{4,7},{7,4},{9,10},{10,9},{8,1... | collective-permute-start | bytes 98312 | tf_op jit(solution)/shard_map/ppermute | solution.py:62
  24.2 3.9 %collective-permute-start.9 = (f32[7,8,128]{2,1,0:T(8,128)S(1)}, f32[7,8,128]{2,1,0:T(8,128)S(1)}, u32[]{:S(2)}, u32[]{:S(2)}) collective-permute-start(f32[7,8,128]{2,1,0:T(8,128)S(1)} %get-tuple-element.50), channel_id=1, source_target_pairs={{0,16},{16,0},{1,17},{17,1},{2,18},{18,2},{3,19},{19,3},{4,20},{20... | collective-permute-start | bytes 86024 | tf_op jit(solution)/shard_map/ppermute | solution.py:522
  32.6 5.0 %collective-permute-start.10 = (f32[16,2,8,128]{3,2,1,0:T(8,128)S(1)}, f32[16,2,8,128]{3,2,1,0:T(8,128)S(1)}, u32[]{:S(2)}, u32[]{:S(2)}) collective-permute-start(f32[16,2,8,128]{3,2,1,0:T(8,128)S(1)} %get-tuple-element.58), channel_id=1, source_target_pairs={{0,16},{16,0},{1,17},{17,1},{2,18},{18,2},{3,19},{19,3},{4,20},{20... | collective-permute-start | bytes 393224 | tf_op jit(solution)/shard_map/ppermute | solution.py:528

commit v4 on v3

--- a/solution.py
+++ b/solution.py
@@ -6,6 +6,7 @@
 from jax.experimental import pallas as pl
 from jax.experimental.pallas import tpu as pltpu
 from jax.sharding import PartitionSpec as P
+
 
 SUBSTEPS = 12
 STEPS = 2
@@ -31,7 +32,7 @@
     return jax.ShapeDtypeStruct(dims, dtype)
 
 
-def call(kernel, name, mib, out_shape, *args, in_specs=None, scratch_shapes=()):
+def call(kernel, mib, out_shape, *args, in_specs=None, scratch_shapes=()):
     return pl.pallas_call(
         kernel,
         out_shape=out_shape,
@@ -39,7 +40,6 @@
         out_specs=[VMEM] * len(out_shape),
         scratch_shapes=scratch_shapes,
         compiler_params=pltpu.CompilerParams(vmem_limit_bytes=mib * 2**20),
-        name=name,
     )(*args)
 
 
@@ -65,12 +65,11 @@
 def exchange(x1, x2, y1, y2):
     (a, rest_a), (b, rest_b) = swaps(lax.axis_size("gx"))
     (c, rest_c), (d, rest_d) = swaps(lax.axis_size("gy"))
-    return (
-        swap(x1, "gx", a, rest_a, "gy"),
-        swap(x2, "gx", b, rest_b, "gy"),
-        swap(y1, "gy", c, rest_c),
-        swap(y2, "gy", d, rest_d),
-    )
+    x1 = swap(x1, "gx", a, rest_a, "gy")
+    x2 = swap(x2, "gx", b, rest_b, "gy")
+    y1 = swap(y1, "gy", c, rest_c)
+    y2 = swap(y2, "gy", d, rest_d)
+    return x1, x2, y1, y2
 
 
 def sides(axis):
@@ -198,9 +197,11 @@
     for t in range(steps + 2 * lag):
         done = t - 2 * lag
         if done >= 0:
-            state[:, cut(done)] += change.pop(done)
+            u = state[:, cut(done)] + change.pop(done)
+            state[:, cut(done)] = u
         if t < steps:
-            u = state[:, cut(t)]
+            if done < 0:
+                u = state[:, cut(t)]
             sp = jnp.maximum(u, jnp.log2(1.0 + jnp.exp2(jnp.minimum(u, 120.0))))
             hi, lo = split(sp)
             both[t] = jnp.dot(
@@ -488,9 +489,9 @@
     faces = [shape_of(ns, *d) for d in face_dims]
     block = shape_of(ns, nx, ny, nz)
     *sent, conc, gamma = call(
-        faces_kernel, "faces", 4,
+        faces_kernel, 4,
         [shape_of(ns + 1, *d) for d in face_dims] + [block, shape_of(1, nx, ny, nz)],
-        concentrations[0], diffusivity[None],
+        *(pltpu.with_memory_space_constraint(a, pltpu.HBM) for a in (concentrations[0], diffusivity[None])),
         in_specs=[HBM] * 2, scratch_shapes=[pltpu.SemaphoreType.DMA((2,))],
     )
     halos = exchange(*sent)
@@ -500,41 +501,39 @@
         vectors, planes = shape_of(3, nx, ny, nz), shape_of(nx, ny, nz)
         noise_dims = 3 * (nx // 2)
         gather, scatter, drift, amp, speed, noise, noise_out, mix_packed, mix_doubled = call(
-            functools.partial(prepare_kernel, ns), "prepare", 4,
+            functools.partial(prepare_kernel, ns), 4,
             table_shapes
             + [vectors, planes, vectors, vectors, shape_of(noise_dims, ny, nz)]
             + [shape_of(nx // 2, ny, nz), planes],
             reactions.T, rates, gamma, velocity, wiener, mix_rate,
         )
-        mine, theirs = call(
-            leave_kernel, "leave", 4, [half, half], conc, *halos, gamma, drift
-        )
+        mine, theirs = call(leave_kernel, 4, [half, half], conc, *halos, gamma, drift)
         theirs = lax.ppermute(theirs, "field", partner)
-        ups, downs = call(coefs_kernel, "coefs", 4, [vectors, vectors], gamma, *halos)
+        ups, downs = call(coefs_kernel, 4, [vectors, vectors], gamma, *halos)
         parts = -(-ns * nx // (nz // 2))
         conc, *sent, side = call(
-            functools.partial(first_kernel, count), "first", 8,
+            functools.partial(first_kernel, count), 8,
             [block] + faces + [shape_of(parts + noise_dims, ny, nz)],
             mine, theirs, gather, scatter, mix_packed, noise_out,
             scratch_shapes=scratch(ns, nx, ny, nz),
         )
+        side = lax.ppermute(side, "field", partner)
         halos = exchange(*sent)
-        side = lax.ppermute(side, "field", partner)
         mine, theirs = call(
-            functools.partial(second_kernel, count), "second", 8, [block, half],
+            functools.partial(second_kernel, count), 8, [block, half],
             conc, *halos, side, ups, downs, amp, speed, noise, gather, scatter, mix_doubled,
             scratch_shapes=scratch(ns, nx, ny, nz),
         )
         theirs = lax.ppermute(theirs, "field", partner)
-        (out,) = call(join_kernel, "join", 4, [block], mine, theirs)
+        (out,) = call(join_kernel, 4, [block], mine, theirs)
         return out[None]
     gather, scatter = call(
-        functools.partial(tables_kernel, ns), "tables", 2, table_shapes, reactions.T, rates
+        functools.partial(tables_kernel, ns), 2, table_shapes, reactions.T, rates
     )
     gamma_halos = halos
     for step_index in range(STEPS):
         (reacted,) = call(
-            functools.partial(step_kernel, step_index), "step", 8, [block],
+            functools.partial(step_kernel, step_index), 8, [block],
             conc, *halos, gamma, *gamma_halos, velocity, wiener, gather, scatter,
             scratch_shapes=scratch(ns, nx, ny, nz),
         )

time: 38.7 us -> 37.9 us (0.979)
  local copies, waits for them, and re-layouts: 2.34 us -> 0.68 us
  Pallas kernels: 10.9 us -> 11.8 us
    unnamed x14 -> x10, local copies, waits for them, and re-layouts: 2.34 us -> 0.68 us
    pallas_call x7, Pallas kernels: 10.9 us -> 11.8 us  [call(): pl.pallas_call(kernel, out_shape=out_shape, in_specs=in_specs or [VMEM] *...]
where the time goes in v4:
time: 37.9 us; the launch traced here: 37.8 us
  starting transfers between devices  13.9 us (37%)
  Pallas kernels  11.8 us (31%)
  waiting for transfers between devices  11.3 us (30%)
  local copies, waits for them, and re-layouts  0.68 us (2%)
    pallas_call x7, Pallas kernels, call(): pl.pallas_call(kernel, out_shape=out_shape, in_specs=in_specs or [VMEM] *...  11.8 us
    ppermute x6, starting transfers between devices, swap(): return lax.ppermute(value, axis, both)  9.31 us
    ppermute x2, waiting for transfers between devices, on_device(): theirs = lax.ppermute(theirs, 'field', partner)  7.5 us
    ppermute x2, starting transfers between devices, on_device(): theirs = lax.ppermute(theirs, 'field', partner)  3.11 us
    ppermute x1, waiting for transfers between devices, on_device(): side = lax.ppermute(side, 'field', partner)  2.24 us
    ppermute x6, waiting for transfers between devices, swap(): return lax.ppermute(value, axis, both)  1.56 us
    ppermute x1, starting transfers between devices, on_device(): side = lax.ppermute(side, 'field', partner)  1.49 us
  transfers between devices with their start and end apart: 11, of which 4 were waited for; matrix products, arithmetic and copies ran while one was open for 0% of the time, Pallas kernels for 1%

profile of v4, /device:TPU:0, one launch (start us, length us, event | category | flops | bytes accessed | tf_op | source)
XLA Modules:
  0.0 37.8 jit_solution(13933562460944153330)
XLA Ops:
  0.0 1.1 %shard_map.73 = (f32[17,8,128]{2,1,0:T(8,128)S(1)}, f32[17,8,128]{2,1,0:T(8,128)S(1)}, f32[17,4,128]{2,1,0:T(4,128)S(1)}, f32[17,4,128]{2,1,0:T(4,128)S(1)}, f32...) custom-call(f32[16,4,8,128]{3,2,1,0:T(8,128)} %bitcast.7, f32[1,4,8,128]{3,2,1,0:T(8,128)} %bitcast.8), custom_call_target="tpu_custom_call" | custom-call | tf_op jit(solution)/shard_map/pallas_call | solution.py:36
  1.1 3.1 %collective-permute-start = (f32[17,8,128]{2,1,0:T(8,128)S(1)}, f32[17,8,128]{2,1,0:T(8,128)S(1)}, u32[]{:S(2)}, u32[]{:S(2)}) collective-permute-start(f32[17,8,128]{2,1,0:T(8,128)S(1)} %get-tuple-element.33), channel_id=1, source_target_pairs={{0,4},{8,12},{4,0},{12,8},{1,5},{9,13},{5,1},{13,9},{2,6},{10,14},... | collective-permute-start | bytes 208904 | tf_op jit(solution)/shard_map/ppermute | solution.py:62
  4.2 0.0 collective-permute-start.1
  4.2 0.5 %collective-permute-start.2 = (f32[17,4,128]{2,1,0:T(4,128)S(1)}, f32[17,4,128]{2,1,0:T(4,128)S(1)}, u32[]{:S(2)}, u32[]{:S(2)}) collective-permute-start(f32[17,4,128]{2,1,0:T(4,128)S(1)} %get-tuple-element.35), channel_id=1, source_target_pairs={{0,1},{2,3},{1,0},{3,2},{4,5},{6,7},{5,4},{7,6},{8,9},{10,11},{9,8... | collective-permute-start | bytes 104456 | tf_op jit(solution)/shard_map/ppermute | solution.py:62
  4.7 1.1 %collective-permute-start.3 = (f32[17,4,128]{2,1,0:T(4,128)S(1)}, f32[17,4,128]{2,1,0:T(4,128)S(1)}, u32[]{:S(2)}, u32[]{:S(2)}) collective-permute-start(f32[17,4,128]{2,1,0:T(4,128)S(1)} %get-tuple-element.36), channel_id=1, source_target_pairs={{1,2},{2,1},{0,3},{3,0},{5,6},{6,5},{4,7},{7,4},{9,10},{10,9},{8,1... | collective-permute-start | bytes 104456 | tf_op jit(solution)/shard_map/ppermute | solution.py:62
  5.9 0.7 %copy-done.3 = s32[64,4]{0,1:T(4,128)S(1)} copy-done((s32[64,4]{0,1:T(4,128)S(1)}, s32[64,4]{0,1:T(4,128)}, u32[]{:S(2)}) %copy-start.3) | copy-done | bytes 1048
  6.5 0.2 shard_map.74
  6.7 1.5 %collective-permute-done.3.y2 = f32[17,4,128]{2,1,0:T(4,128)S(1)} collective-permute-done((f32[17,4,128]{2,1,0:T(4,128)S(1)}, f32[17,4,128]{2,1,0:T(4,128)S(1)}, u32[]{:S(2)}, u32[]{:S(2)}) %collective-permute-start.3) | collective-permute-done | bytes 34848 | tf_op jit(solution)/shard_map/ppermute | solution.py:62
  8.3 0.0 collective-permute-done.x1
  8.3 0.0 collective-permute-done.1.x2
  8.3 0.5 %shard_map.75 = (f32[16,2,8,128]{3,2,1,0:T(8,128)S(1)}, f32[16,2,8,128]{3,2,1,0:T(8,128)S(1)}) custom-call(f32[16,4,8,128]{3,2,1,0:T(8,128)S(1)} %get-tuple-element.32.conc, f32[17,8,128]{2,1,0:T(8,128)S(1)} %collective-permute-done.x1, f32[17,8,128]{2,1,0:T(8,128)S(1)} %collective-permute-done.1.x2, f32[17,4,128]{2,1,0:T(4,128)S(1)} %collective-permute-done.2.y1, ...), custom_call_target="tpu_custom_call" | custom-call | tf_op jit(solution)/shard_map/pallas_call | solution.py:36
  8.8 1.6 %collective-permute-start.4 = (f32[16,2,8,128]{3,2,1,0:T(8,128)S(1)}, f32[16,2,8,128]{3,2,1,0:T(8,128)S(1)}, u32[]{:S(2)}, u32[]{:S(2)}) collective-permute-start(f32[16,2,8,128]{3,2,1,0:T(8,128)S(1)} %get-tuple-element.40), channel_id=1, source_target_pairs={{0,16},{16,0},{1,17},{17,1},{2,18},{18,2},{3,19},{19,3},{4,20},{20... | collective-permute-start | bytes 393224 | tf_op jit(solution)/shard_map/ppermute | solution.py:511
  10.3 4.0 %collective-permute-done.4.theirs = f32[16,2,8,128]{3,2,1,0:T(8,128)S(1)} collective-permute-done((f32[16,2,8,128]{3,2,1,0:T(8,128)S(1)}, f32[16,2,8,128]{3,2,1,0:T(8,128)S(1)}, u32[]{:S(2)}, u32[]{:S(2)}) %collective-permute-start.4) | collective-permute-done | bytes 131104 | tf_op jit(solution)/shard_map/ppermute | solution.py:511
  14.3 4.5 %shard_map.76 = (f32[16,4,8,128]{3,2,1,0:T(8,128)S(1)}, f32[16,8,128]{2,1,0:T(8,128)S(1)}, f32[16,8,128]{2,1,0:T(8,128)S(1)}, f32[16,4,128]{2,1,0:T(4,128)S(1)},...) custom-call(f32[16,2,8,128]{3,2,1,0:T(8,128)S(1)} %get-tuple-element.39.mine, ...), custom_call_target="tpu_custom_call" | custom-call | tf_op jit(solution)/shard_map/pallas_call | solution.py:36
  18.9 2.9 %collective-permute-start.5 = (f32[16,8,128]{2,1,0:T(8,128)S(1)}, f32[16,8,128]{2,1,0:T(8,128)S(1)}, u32[]{:S(2)}, u32[]{:S(2)}) collective-permute-start(f32[16,8,128]{2,1,0:T(8,128)S(1)} %get-tuple-element.46), channel_id=1, source_target_pairs={{0,4},{8,12},{4,0},{12,8},{1,5},{9,13},{5,1},{13,9},{2,6},{10,14},... | collective-permute-start | bytes 196616 | tf_op jit(solution)/shard_map/ppermute | solution.py:62
  21.8 0.5 %collective-permute-start.7 = (f32[16,4,128]{2,1,0:T(4,128)S(1)}, f32[16,4,128]{2,1,0:T(4,128)S(1)}, u32[]{:S(2)}, u32[]{:S(2)}) collective-permute-start(f32[16,4,128]{2,1,0:T(4,128)S(1)} %get-tuple-element.48), channel_id=1, source_target_pairs={{0,1},{2,3},{1,0},{3,2},{4,5},{6,7},{5,4},{7,6},{8,9},{10,11},{9,8... | collective-permute-start | bytes 98312 | tf_op jit(solution)/shard_map/ppermute | solution.py:62
  22.3 1.1 %collective-permute-start.8 = (f32[16,4,128]{2,1,0:T(4,128)S(1)}, f32[16,4,128]{2,1,0:T(4,128)S(1)}, u32[]{:S(2)}, u32[]{:S(2)}) collective-permute-start(f32[16,4,128]{2,1,0:T(4,128)S(1)} %get-tuple-element.49), channel_id=1, source_target_pairs={{1,2},{2,1},{0,3},{3,0},{5,6},{6,5},{4,7},{7,4},{9,10},{10,9},{8,1... | collective-permute-start | bytes 98312 | tf_op jit(solution)/shard_map/ppermute | solution.py:62
  23.4 1.5 %collective-permute-start.9 = (f32[7,8,128]{2,1,0:T(8,128)S(1)}, f32[7,8,128]{2,1,0:T(8,128)S(1)}, u32[]{:S(2)}, u32[]{:S(2)}) collective-permute-start(f32[7,8,128]{2,1,0:T(8,128)S(1)} %get-tuple-element.50), channel_id=1, source_target_pairs={{0,16},{16,0},{1,17},{17,1},{2,18},{18,2},{3,19},{19,3},{4,20},{20... | collective-permute-start | bytes 86024 | tf_op jit(solution)/shard_map/ppermute | solution.py:520
  24.9 0.1 shard_map.77
  25.1 2.2 %collective-permute-done.9.side = f32[7,8,128]{2,1,0:T(8,128)S(1)} collective-permute-done((f32[7,8,128]{2,1,0:T(8,128)S(1)}, f32[7,8,128]{2,1,0:T(8,128)S(1)}, u32[]{:S(2)}, u32[]{:S(2)}) %collective-permute-start.9) | collective-permute-done | bytes 28704 | tf_op jit(solution)/shard_map/ppermute | solution.py:520
  27.3 4.6 %shard_map.78 = (f32[16,4,8,128]{3,2,1,0:T(8,128)S(1)}, f32[16,2,8,128]{3,2,1,0:T(8,128)S(1)}) custom-call(f32[16,4,8,128]{3,2,1,0:T(8,128)S(1)} %get-tuple-element.45.conc, f32[16,8,128]{2,1,0:T(8,128)S(1)} %collective-permute-done.5.x1, f32[16,8,128]{2,1,0:T(8,128)S(1)} %collective-permute-done.6.x2, f32[16,4,128]{2,1,0:T(4,128)S(1)} %collective-permute-done.7.y1, ...), custom_call_target="tpu_custom_call" | custom-call | tf_op jit(solution)/shard_map/pallas_call | solution.py:36
  31.9 1.6 %collective-permute-start.10 = (f32[16,2,8,128]{3,2,1,0:T(8,128)S(1)}, f32[16,2,8,128]{3,2,1,0:T(8,128)S(1)}, u32[]{:S(2)}, u32[]{:S(2)}) collective-permute-start(f32[16,2,8,128]{3,2,1,0:T(8,128)S(1)} %get-tuple-element.58), channel_id=1, source_target_pairs={{0,16},{16,0},{1,17},{17,1},{2,18},{18,2},{3,19},{19,3},{4,20},{20... | collective-permute-start | bytes 393224 | tf_op jit(solution)/shard_map/ppermute | solution.py:527
  33.5 3.5 %collective-permute-done.10.theirs = f32[16,2,8,128]{3,2,1,0:T(8,128)S(1)} collective-permute-done((f32[16,2,8,128]{3,2,1,0:T(8,128)S(1)}, f32[16,2,8,128]{3,2,1,0:T(8,128)S(1)}, u32[]{:S(2)}, u32[]{:S(2)}) %collective-permute-start.10) | collective-permute-done | bytes 131104 | tf_op jit(solution)/shard_map/ppermute | solution.py:527
  37.0 0.8 %shard_map.79 = f32[16,4,8,128]{3,2,1,0:T(8,128)} custom-call(f32[16,4,8,128]{3,2,1,0:T(8,128)S(1)} %get-tuple-element.57.mine, f32[16,2,8,128]{3,2,1,0:T(8,128)S(1)} %collective-permute-done.10.theirs), custom_call_target="tpu_custom_call" | custom-call | tf_op jit(solution)/shard_map/pallas_call | solution.py:36
  (15 shorter events, 0.0 us)
Async XLA Ops:
  0.0 5.8 %copy-start = (f32[2,3,1,4,8,128]{5,4,3,2,1,0:T(8,128)S(1)}, f32[2,3,1,4,8,128]{5,4,3,2,1,0:T(8,128)}, u32[]{:S(2)}) copy-start(f32[2,3,1,4,8,128]{5,4,3,2,1,0:T(8,128)} %wiener.1) | copy-start | bytes 294916
  0.0 5.8 %copy-start.1 = (f32[3,4,8,128]{3,2,1,0:T(8,128)S(1)}, f32[3,4,8,128]{3,2,1,0:T(8,128)}, u32[]{:S(2)}) copy-start(f32[3,4,8,128]{3,2,1,0:T(8,128)} %velocity.1) | copy-start | bytes 147460
  0.0 5.8 %copy-start.2 = (f32[4,8,128]{2,1,0:T(8,128)S(1)}, f32[4,8,128]{2,1,0:T(8,128)}, u32[]{:S(2)}) copy-start(f32[4,8,128]{2,1,0:T(8,128)} %mix_rate.1) | copy-start | bytes 49156
  1.1 7.2 %collective-permute-start = (f32[17,8,128]{2,1,0:T(8,128)S(1)}, f32[17,8,128]{2,1,0:T(8,128)S(1)}, u32[]{:S(2)}, u32[]{:S(2)}) collective-permute-start(f32[17,8,128]{2,1,0:T(8,128)S(1)} %get-tuple-element.33), channel_id=1, source_target_pairs={{0,4},{8,12},{4,0},{12,8},{1,5},{9,13},{5,1},{13,9},{2,6},{10,14},... | collective-permute-start | bytes 208904 | tf_op jit(solution)/shard_map/ppermute | solution.py:62
  4.2 4.1 %collective-permute-start.1 = (f32[17,8,128]{2,1,0:T(8,128)S(1)}, f32[17,8,128]{2,1,0:T(8,128)S(1)}, u32[]{:S(2)}, u32[]{:S(2)}) collective-permute-start(f32[17,8,128]{2,1,0:T(8,128)S(1)} %get-tuple-element.34), channel_id=1, source_target_pairs={{4,8},{5,9},{6,10},{7,11},{8,4},{9,5},{10,6},{11,7},{0,1},{1,0},{2... | collective-permute-start | bytes 208904 | tf_op jit(solution)/shard_map/ppermute | solution.py:57
  4.2 2.5 %collective-permute-start.2 = (f32[17,4,128]{2,1,0:T(4,128)S(1)}, f32[17,4,128]{2,1,0:T(4,128)S(1)}, u32[]{:S(2)}, u32[]{:S(2)}) collective-permute-start(f32[17,4,128]{2,1,0:T(4,128)S(1)} %get-tuple-element.35), channel_id=1, source_target_pairs={{0,1},{2,3},{1,0},{3,2},{4,5},{6,7},{5,4},{7,6},{8,9},{10,11},{9,8... | collective-permute-start | bytes 104456 | tf_op jit(solution)/shard_map/ppermute | solution.py:62
  4.7 3.5 %collective-permute-start.3 = (f32[17,4,128]{2,1,0:T(4,128)S(1)}, f32[17,4,128]{2,1,0:T(4,128)S(1)}, u32[]{:S(2)}, u32[]{:S(2)}) collective-permute-start(f32[17,4,128]{2,1,0:T(4,128)S(1)} %get-tuple-element.36), channel_id=1, source_target_pairs={{1,2},{2,1},{0,3},{3,0},{5,6},{6,5},{4,7},{7,4},{9,10},{10,9},{8,1... | collective-permute-start | bytes 104456 | tf_op jit(solution)/shard_map/ppermute | solution.py:62
  5.8 0.7 %copy-start.3 = (s32[64,4]{0,1:T(4,128)S(1)}, s32[64,4]{0,1:T(4,128)}, u32[]{:S(2)}) copy-start(s32[64,4]{0,1:T(4,128)} %param.13) | copy-start | bytes 3076
  5.8 0.7 %copy-start.4 = (f32[64]{0:T(128)S(1)}, f32[64]{0:T(128)}, u32[]{:S(2)}) copy-start(f32[64]{0:T(128)} %param.12) | copy-start | bytes 772
  8.8 5.6 %collective-permute-start.4 = (f32[16,2,8,128]{3,2,1,0:T(8,128)S(1)}, f32[16,2,8,128]{3,2,1,0:T(8,128)S(1)}, u32[]{:S(2)}, u32[]{:S(2)}) collective-permute-start(f32[16,2,8,128]{3,2,1,0:T(8,128)S(1)} %get-tuple-element.40), channel_id=1, source_target_pairs={{0,16},{16,0},{1,17},{17,1},{2,18},{18,2},{3,19},{19,3},{4,20},{20... | collective-permute-start | bytes 393224 | tf_op jit(solution)/shard_map/ppermute | solution.py:511
  18.9 8.4 %collective-permute-start.5 = (f32[16,8,128]{2,1,0:T(8,128)S(1)}, f32[16,8,128]{2,1,0:T(8,128)S(1)}, u32[]{:S(2)}, u32[]{:S(2)}) collective-permute-start(f32[16,8,128]{2,1,0:T(8,128)S(1)} %get-tuple-element.46), channel_id=1, source_target_pairs={{0,4},{8,12},{4,0},{12,8},{1,5},{9,13},{5,1},{13,9},{2,6},{10,14},... | collective-permute-start | bytes 196616 | tf_op jit(solution)/shard_map/ppermute | solution.py:62
  21.8 5.5 %collective-permute-start.6 = (f32[16,8,128]{2,1,0:T(8,128)S(1)}, f32[16,8,128]{2,1,0:T(8,128)S(1)}, u32[]{:S(2)}, u32[]{:S(2)}) collective-permute-start(f32[16,8,128]{2,1,0:T(8,128)S(1)} %get-tuple-element.47), channel_id=1, source_target_pairs={{4,8},{5,9},{6,10},{7,11},{8,4},{9,5},{10,6},{11,7},{0,1},{1,0},{2... | collective-permute-start | bytes 196616 | tf_op jit(solution)/shard_map/ppermute | solution.py:57
  21.8 5.5 %collective-permute-start.7 = (f32[16,4,128]{2,1,0:T(4,128)S(1)}, f32[16,4,128]{2,1,0:T(4,128)S(1)}, u32[]{:S(2)}, u32[]{:S(2)}) collective-permute-start(f32[16,4,128]{2,1,0:T(4,128)S(1)} %get-tuple-element.48), channel_id=1, source_target_pairs={{0,1},{2,3},{1,0},{3,2},{4,5},{6,7},{5,4},{7,6},{8,9},{10,11},{9,8... | collective-permute-start | bytes 98312 | tf_op jit(solution)/shard_map/ppermute | solution.py:62
  22.3 5.0 %collective-permute-start.8 = (f32[16,4,128]{2,1,0:T(4,128)S(1)}, f32[16,4,128]{2,1,0:T(4,128)S(1)}, u32[]{:S(2)}, u32[]{:S(2)}) collective-permute-start(f32[16,4,128]{2,1,0:T(4,128)S(1)} %get-tuple-element.49), channel_id=1, source_target_pairs={{1,2},{2,1},{0,3},{3,0},{5,6},{6,5},{4,7},{7,4},{9,10},{10,9},{8,1... | collective-permute-start | bytes 98312 | tf_op jit(solution)/shard_map/ppermute | solution.py:62
  23.4 3.9 %collective-permute-start.9 = (f32[7,8,128]{2,1,0:T(8,128)S(1)}, f32[7,8,128]{2,1,0:T(8,128)S(1)}, u32[]{:S(2)}, u32[]{:S(2)}) collective-permute-start(f32[7,8,128]{2,1,0:T(8,128)S(1)} %get-tuple-element.50), channel_id=1, source_target_pairs={{0,16},{16,0},{1,17},{17,1},{2,18},{18,2},{3,19},{19,3},{4,20},{20... | collective-permute-start | bytes 86024 | tf_op jit(solution)/shard_map/ppermute | solution.py:520
  31.9 5.0 %collective-permute-start.10 = (f32[16,2,8,128]{3,2,1,0:T(8,128)S(1)}, f32[16,2,8,128]{3,2,1,0:T(8,128)S(1)}, u32[]{:S(2)}, u32[]{:S(2)}) collective-permute-start(f32[16,2,8,128]{3,2,1,0:T(8,128)S(1)} %get-tuple-element.58), channel_id=1, source_target_pairs={{0,16},{16,0},{1,17},{17,1},{2,18},{18,2},{3,19},{19,3},{4,20},{20... | collective-permute-start | bytes 393224 | tf_op jit(solution)/shard_map/ppermute | solution.py:527

commit v5 on v4

--- a/solution.py
+++ b/solution.py
@@ -14,6 +14,7 @@
 LOG2E = 1.4426950408889634
 LN2 = 0.6931471805599453
 TILE = 256
+DIRECT = 2
 VMEM = pl.BlockSpec(memory_space=pltpu.VMEM)
 HBM = pl.BlockSpec(memory_space=pltpu.HBM)
 
@@ -182,14 +183,28 @@
     return pltpu.roll(p, nz - 1, 1), pltpu.roll(p, 1, 1)
 
 
-def chemistry(state, gather, scatter):
+def second_reactant(sp, index):
+    width = index.shape[1]
+    pieces = []
+    for start in range(0, sp.shape[1], width):
+        picked_rows = None
+        for low in range(0, sp.shape[0], 8):
+            rows = sp[low : low + 8, start : start + width]
+            inside = jnp.logical_and(index >= low, index < low + 8)
+            got = jnp.take_along_axis(rows, jnp.where(inside, index - low, 0), axis=0)
+            picked_rows = got if low == 0 else jnp.where(inside, got, picked_rows)
+        pieces.append(picked_rows)
+    return jnp.concatenate(pieces, axis=1)
+
+
+def chemistry(state, gather, scatter, index):
     ns, cells = state.shape
     tiles = cells // TILE
     table, net = gather[...][:, : 3 * ns], scatter[...]
-    nr = table.shape[0] // 2
+    paired = net.shape[1] // 16 - DIRECT
     steps = SUBSTEPS * tiles
     lag = tiles // 2
-    both, change = {}, {}
+    both, direct, change = {}, {}, {}
 
     def cut(t):
         return slice(t % tiles * TILE, (t % tiles + 1) * TILE)
@@ -209,23 +224,29 @@
                 jnp.concatenate([hi, lo, hi], axis=0),
                 preferred_element_type=jnp.float32,
             )
+            direct[t] = [second_reactant(sp, index[j]) for j in range(DIRECT)]
         ready = t - lag
         if 0 <= ready < steps:
-            pair = both.pop(ready).reshape(nr // 8, 2, 8, TILE)
-            hi, lo = split((pair[:, 0] * pair[:, 1]).reshape(nr, TILE))
+            got = both.pop(ready)
+            pair = got[: 16 * paired].reshape(paired, 2, 8, TILE)
+            rates = [(pair[:, 0] * pair[:, 1]).reshape(8 * paired, TILE)]
+            for j, second in enumerate(direct.pop(ready)):
+                start = 16 * paired + 8 * j
+                rates.append(got[start : start + 8] * second)
+            hi, lo = split(jnp.concatenate(rates, axis=0))
             change[ready] = jnp.dot(
                 net, jnp.concatenate([hi, lo], axis=0), preferred_element_type=jnp.float32
             )
 
 
-def react(rows, state, gather, scatter):
+def react(rows, state, gather, scatter, index):
     ns = state.shape[0]
     nz = rows.shape[1]
     stride = rows.shape[0] // ns
     chunks = state.shape[1] // nz
     for j in range(chunks):
         state[:, j * nz : (j + 1) * nz] = rows[pl.ds(j, ns, stride=stride), :]
-    chemistry(state, gather, scatter)
+    chemistry(state, gather, scatter, index)
     for j in range(chunks):
         rows[pl.ds(j, ns, stride=stride), :] = state[:, j * nz : (j + 1) * nz] * LN2
 
@@ -269,9 +290,10 @@
     send_faces(gamma, 0, x1, x2, y1, y2, ns)
 
 
-def tables_kernel(ns, reactions, rates, gather, scatter):
+def tables_kernel(ns, reactions, rates, gather, scatter, index):
     nr = reactions.shape[1]
     depth = gather.shape[1]
+    paired = nr // 8 - DIRECT
     row = lax.broadcasted_iota(jnp.int32, (depth, nr), 0)
     scalar, part = lax.rem(row, ns), lax.div(row, ns)
     k = rates[...] * (CHEM_STEP * LN2)
@@ -286,18 +308,24 @@
     both = jnp.concatenate(
         [first * weight, second * jnp.where(part < 2, 1.0, 0.0)], axis=1
     ).T
-    for j in range(nr // 8):
+    for j in range(paired):
         block = [both[c + 8 * j : c + 8 * j + 8, :] for c in (0, nr)]
         gather[16 * j : 16 * j + 16, :] = jnp.concatenate(block, axis=0).astype(jnp.bfloat16)
+    gather[16 * paired :, :] = both[8 * paired : nr, :].astype(jnp.bfloat16)
+    partner = jnp.broadcast_to(reactions[1:2, :].astype(jnp.float32), (depth, nr))
+    partner = jnp.concatenate([partner, partner], axis=1).T
+    for j in range(DIRECT):
+        start = 8 * (paired + j)
+        index[j] = partner[start : start + 8, :].astype(jnp.int32)
     net = (third + fourth - first - second)[:ns].astype(jnp.bfloat16)
     scatter[...] = jnp.concatenate([net, net], axis=1)
 
 
 def prepare_kernel(
     ns, reactions, rates, gamma, velocity, wiener, mix_rate,
-    gather, scatter, drift, amp, speed, noise, noise_out, mix_packed, mix_doubled
+    gather, scatter, index, drift, amp, speed, noise, noise_out, mix_packed, mix_doubled
 ):
-    tables_kernel(ns, reactions, rates, gather, scatter)
+    tables_kernel(ns, reactions, rates, gather, scatter, index)
     nx = gamma.shape[1]
     own = kept(gamma.shape[2:])
     for x in range(nx):
@@ -341,7 +369,7 @@
 
 
 def first_kernel(
-    count, mine, theirs, gather, scatter, mix_rate, noise_out,
+    count, mine, theirs, gather, scatter, index, mix_rate, noise_out,
     conc, x1, x2, y1, y2, side, rows, state
 ):
     ns, nx, ny, nz = conc.shape
@@ -358,7 +386,7 @@
         for x in range(half):
             rows[place(s, 0, x), :] = mine[s, x]
             rows[place(s, 1, x), :] = theirs[s, x]
-    react(rows, state, gather, scatter)
+    react(rows, state, gather, scatter, index)
     for x in range(half):
         mixed = mixing(
             (ns, lambda s: (rows[place(s, 0, x), :], rows[place(s, 1, x), :])),
@@ -385,7 +413,7 @@
 
 
 def second_kernel(
-    count, conc, x1, x2, y1, y2, side, ups, downs, amp, speed, noise, gather, scatter, mix_rate,
+    count, conc, x1, x2, y1, y2, side, ups, downs, amp, speed, noise, gather, scatter, index, mix_rate,
     mine, theirs, rows, state
 ):
     ns, nx, ny, nz = conc.shape
@@ -418,7 +446,7 @@
     for s in range(ns):
         for x, moved in enumerate(move(conc, s, coefs, x1, x2, y1, y2, half_z)):
             rows[s * stride + x * ny : s * stride + (x + 1) * ny, :] = moved
-    react(rows, state, gather, scatter)
+    react(rows, state, gather, scatter, index)
 
     def field_pair(x):
         def get(s):
@@ -447,7 +475,7 @@
 
 
 def step_kernel(
-    step, conc, x1, x2, y1, y2, gamma, gx1, gx2, gy1, gy2, velocity, wiener, gather, scatter,
+    step, conc, x1, x2, y1, y2, gamma, gx1, gx2, gy1, gy2, velocity, wiener, gather, scatter, index,
     out, rows, state
 ):
     ns, nx, ny, nz = conc.shape
@@ -462,7 +490,7 @@
     for s in range(ns):
         for x, moved in enumerate(move(conc, s, coefs, x1, x2, y1, y2, whole_z)):
             rows[s * stride + x * ny : s * stride + (x + 1) * ny, :] = moved
-    react(rows, state, gather, scatter)
+    react(rows, state, gather, scatter, index)
     for s in range(ns):
         for x in range(nx):
             out[s, x] = rows[s * stride + x * ny : s * stride + (x + 1) * ny, :]
@@ -483,7 +511,9 @@
     count = lax.axis_size("field")
     rates = rate_constants.reshape(1, nr)
     table_shapes = [
-        shape_of(2 * nr, 128, dtype=jnp.bfloat16), shape_of(ns, 2 * nr, dtype=jnp.bfloat16)
+        shape_of(2 * nr - 8 * DIRECT, 128, dtype=jnp.bfloat16),
+        shape_of(ns, 2 * nr, dtype=jnp.bfloat16),
+        shape_of(DIRECT, 8, 128, dtype=jnp.int32),
     ]
     face_dims = [(ny, nz), (ny, nz), (nx, nz), (nx, nz)]
     faces = [shape_of(ns, *d) for d in face_dims]
@@ -500,7 +530,7 @@
         partner = [(0, 1), (1, 0)]
         vectors, planes = shape_of(3, nx, ny, nz), shape_of(nx, ny, nz)
         noise_dims = 3 * (nx // 2)
-        gather, scatter, drift, amp, speed, noise, noise_out, mix_packed, mix_doubled = call(
+        *tables, drift, amp, speed, noise, noise_out, mix_packed, mix_doubled = call(
             functools.partial(prepare_kernel, ns), 4,
             table_shapes
             + [vectors, planes, vectors, vectors, shape_of(noise_dims, ny, nz)]
@@ -514,27 +544,25 @@
         conc, *sent, side = call(
             functools.partial(first_kernel, count), 8,
             [block] + faces + [shape_of(parts + noise_dims, ny, nz)],
-            mine, theirs, gather, scatter, mix_packed, noise_out,
+            mine, theirs, *tables, mix_packed, noise_out,
             scratch_shapes=scratch(ns, nx, ny, nz),
         )
         side = lax.ppermute(side, "field", partner)
         halos = exchange(*sent)
         mine, theirs = call(
             functools.partial(second_kernel, count), 8, [block, half],
-            conc, *halos, side, ups, downs, amp, speed, noise, gather, scatter, mix_doubled,
+            conc, *halos, side, ups, downs, amp, speed, noise, *tables, mix_doubled,
             scratch_shapes=scratch(ns, nx, ny, nz),
         )
         theirs = lax.ppermute(theirs, "field", partner)
         (out,) = call(join_kernel, 4, [block], mine, theirs)
         return out[None]
-    gather, scatter = call(
-        functools.partial(tables_kernel, ns), 2, table_shapes, reactions.T, rates
-    )
+    tables = call(functools.partial(tables_kernel, ns), 2, table_shapes, reactions.T, rates)
     gamma_halos = halos
     for step_index in range(STEPS):
         (reacted,) = call(
             functools.partial(step_kernel, step_index), 8, [block],
-            conc, *halos, gamma, *gamma_halos, velocity, wiener, gather, scatter,
+            conc, *halos, gamma, *gamma_halos, velocity, wiener, *tables,
             scratch_shapes=scratch(ns, nx, ny, nz),
         )
         first = lax.psum(reacted, "field")

time: 37.9 us -> 37.4 us (0.987)
  Pallas kernels: 11.8 us -> 11.3 us
    pallas_call x7, Pallas kernels: 11.8 us -> 11.3 us  [call(): pl.pallas_call(kernel, out_shape=out_shape, in_specs=in_specs or [VMEM] *...]
where the time goes in v5:
time: 37.4 us; the launch traced here: 37.3 us
  starting transfers between devices  13.9 us (37%)
  Pallas kernels  11.3 us (30%)
  waiting for transfers between devices  11.3 us (30%)
  local copies, waits for them, and re-layouts  0.68 us (2%)
    pallas_call x7, Pallas kernels, call(): pl.pallas_call(kernel, out_shape=out_shape, in_specs=in_specs or [VMEM] *...  11.3 us
    ppermute x6, starting transfers between devices, swap(): return lax.ppermute(value, axis, both)  9.31 us
    ppermute x2, waiting for transfers between devices, on_device(): theirs = lax.ppermute(theirs, 'field', partner)  7.5 us
    ppermute x2, starting transfers between devices, on_device(): theirs = lax.ppermute(theirs, 'field', partner)  3.12 us
    ppermute x1, waiting for transfers between devices, on_device(): side = lax.ppermute(side, 'field', partner)  2.23 us
    ppermute x6, waiting for transfers between devices, swap(): return lax.ppermute(value, axis, both)  1.55 us
    ppermute x1, starting transfers between devices, on_device(): side = lax.ppermute(side, 'field', partner)  1.49 us
  transfers between devices with their start and end apart: 11, of which 4 were waited for; matrix products, arithmetic and copies ran while one was open for 0% of the time, Pallas kernels for 1%

profile of v5, /device:TPU:0, one launch (start us, length us, event | category | flops | bytes accessed | tf_op | source)
XLA Modules:
  0.0 37.3 jit_solution(5603244417828845336)
XLA Ops:
  0.0 1.1 %shard_map.73 = (f32[17,8,128]{2,1,0:T(8,128)S(1)}, f32[17,8,128]{2,1,0:T(8,128)S(1)}, f32[17,4,128]{2,1,0:T(4,128)S(1)}, f32[17,4,128]{2,1,0:T(4,128)S(1)}, f32...) custom-call(f32[16,4,8,128]{3,2,1,0:T(8,128)} %bitcast.7, f32[1,4,8,128]{3,2,1,0:T(8,128)} %bitcast.8), custom_call_target="tpu_custom_call" | custom-call | tf_op jit(solution)/shard_map/pallas_call | solution.py:37
  1.1 3.1 %collective-permute-start = (f32[17,8,128]{2,1,0:T(8,128)S(1)}, f32[17,8,128]{2,1,0:T(8,128)S(1)}, u32[]{:S(2)}, u32[]{:S(2)}) collective-permute-start(f32[17,8,128]{2,1,0:T(8,128)S(1)} %get-tuple-element.34), channel_id=1, source_target_pairs={{0,4},{8,12},{4,0},{12,8},{1,5},{9,13},{5,1},{13,9},{2,6},{10,14},... | collective-permute-start | bytes 208904 | tf_op jit(solution)/shard_map/ppermute | solution.py:63
  4.2 0.0 collective-permute-start.1
  4.2 0.5 %collective-permute-start.2 = (f32[17,4,128]{2,1,0:T(4,128)S(1)}, f32[17,4,128]{2,1,0:T(4,128)S(1)}, u32[]{:S(2)}, u32[]{:S(2)}) collective-permute-start(f32[17,4,128]{2,1,0:T(4,128)S(1)} %get-tuple-element.36), channel_id=1, source_target_pairs={{0,1},{2,3},{1,0},{3,2},{4,5},{6,7},{5,4},{7,6},{8,9},{10,11},{9,8... | collective-permute-start | bytes 104456 | tf_op jit(solution)/shard_map/ppermute | solution.py:63
  4.7 1.1 %collective-permute-start.3 = (f32[17,4,128]{2,1,0:T(4,128)S(1)}, f32[17,4,128]{2,1,0:T(4,128)S(1)}, u32[]{:S(2)}, u32[]{:S(2)}) collective-permute-start(f32[17,4,128]{2,1,0:T(4,128)S(1)} %get-tuple-element.37), channel_id=1, source_target_pairs={{1,2},{2,1},{0,3},{3,0},{5,6},{6,5},{4,7},{7,4},{9,10},{10,9},{8,1... | collective-permute-start | bytes 104456 | tf_op jit(solution)/shard_map/ppermute | solution.py:63
  5.9 0.7 %copy-done.3 = s32[64,4]{0,1:T(4,128)S(1)} copy-done((s32[64,4]{0,1:T(4,128)S(1)}, s32[64,4]{0,1:T(4,128)}, u32[]{:S(2)}) %copy-start.3) | copy-done | bytes 1048
  6.5 0.2 shard_map.74
  6.7 1.5 %collective-permute-done.3.y2 = f32[17,4,128]{2,1,0:T(4,128)S(1)} collective-permute-done((f32[17,4,128]{2,1,0:T(4,128)S(1)}, f32[17,4,128]{2,1,0:T(4,128)S(1)}, u32[]{:S(2)}, u32[]{:S(2)}) %collective-permute-start.3) | collective-permute-done | bytes 34848 | tf_op jit(solution)/shard_map/ppermute | solution.py:63
  8.3 0.0 collective-permute-done.x1
  8.3 0.0 collective-permute-done.1.x2
  8.3 0.5 %shard_map.75 = (f32[16,2,8,128]{3,2,1,0:T(8,128)S(1)}, f32[16,2,8,128]{3,2,1,0:T(8,128)S(1)}) custom-call(f32[16,4,8,128]{3,2,1,0:T(8,128)S(1)} %get-tuple-element.33.conc, f32[17,8,128]{2,1,0:T(8,128)S(1)} %collective-permute-done.x1, f32[17,8,128]{2,1,0:T(8,128)S(1)} %collective-permute-done.1.x2, f32[17,4,128]{2,1,0:T(4,128)S(1)} %collective-permute-done.2.y1, ...), custom_call_target="tpu_custom_call" | custom-call | tf_op jit(solution)/shard_map/pallas_call | solution.py:37
  8.8 1.6 %collective-permute-start.4 = (f32[16,2,8,128]{3,2,1,0:T(8,128)S(1)}, f32[16,2,8,128]{3,2,1,0:T(8,128)S(1)}, u32[]{:S(2)}, u32[]{:S(2)}) collective-permute-start(f32[16,2,8,128]{3,2,1,0:T(8,128)S(1)} %get-tuple-element.41), channel_id=1, source_target_pairs={{0,16},{16,0},{1,17},{17,1},{2,18},{18,2},{3,19},{19,3},{4,20},{20... | collective-permute-start | bytes 393224 | tf_op jit(solution)/shard_map/ppermute | solution.py:541
  10.3 4.0 %collective-permute-done.4.theirs = f32[16,2,8,128]{3,2,1,0:T(8,128)S(1)} collective-permute-done((f32[16,2,8,128]{3,2,1,0:T(8,128)S(1)}, f32[16,2,8,128]{3,2,1,0:T(8,128)S(1)}, u32[]{:S(2)}, u32[]{:S(2)}) %collective-permute-start.4) | collective-permute-done | bytes 131104 | tf_op jit(solution)/shard_map/ppermute | solution.py:541
  14.3 4.3 %shard_map.76 = (f32[16,4,8,128]{3,2,1,0:T(8,128)S(1)}, f32[16,8,128]{2,1,0:T(8,128)S(1)}, f32[16,8,128]{2,1,0:T(8,128)S(1)}, f32[16,4,128]{2,1,0:T(4,128)S(1)},...) custom-call(f32[16,2,8,128]{3,2,1,0:T(8,128)S(1)} %get-tuple-element.40.mine, ...), custom_call_target="tpu_custom_call" | custom-call | tf_op jit(solution)/shard_map/pallas_call | solution.py:37
  18.6 2.9 %collective-permute-start.5 = (f32[16,8,128]{2,1,0:T(8,128)S(1)}, f32[16,8,128]{2,1,0:T(8,128)S(1)}, u32[]{:S(2)}, u32[]{:S(2)}) collective-permute-start(f32[16,8,128]{2,1,0:T(8,128)S(1)} %get-tuple-element.48), channel_id=1, source_target_pairs={{0,4},{8,12},{4,0},{12,8},{1,5},{9,13},{5,1},{13,9},{2,6},{10,14},... | collective-permute-start | bytes 196616 | tf_op jit(solution)/shard_map/ppermute | solution.py:63
  21.5 0.5 %collective-permute-start.7 = (f32[16,4,128]{2,1,0:T(4,128)S(1)}, f32[16,4,128]{2,1,0:T(4,128)S(1)}, u32[]{:S(2)}, u32[]{:S(2)}) collective-permute-start(f32[16,4,128]{2,1,0:T(4,128)S(1)} %get-tuple-element.50), channel_id=1, source_target_pairs={{0,1},{2,3},{1,0},{3,2},{4,5},{6,7},{5,4},{7,6},{8,9},{10,11},{9,8... | collective-permute-start | bytes 98312 | tf_op jit(solution)/shard_map/ppermute | solution.py:63
  22.0 1.1 %collective-permute-start.8 = (f32[16,4,128]{2,1,0:T(4,128)S(1)}, f32[16,4,128]{2,1,0:T(4,128)S(1)}, u32[]{:S(2)}, u32[]{:S(2)}) collective-permute-start(f32[16,4,128]{2,1,0:T(4,128)S(1)} %get-tuple-element.51), channel_id=1, source_target_pairs={{1,2},{2,1},{0,3},{3,0},{5,6},{6,5},{4,7},{7,4},{9,10},{10,9},{8,1... | collective-permute-start | bytes 98312 | tf_op jit(solution)/shard_map/ppermute | solution.py:63
  23.2 1.5 %collective-permute-start.9 = (f32[7,8,128]{2,1,0:T(8,128)S(1)}, f32[7,8,128]{2,1,0:T(8,128)S(1)}, u32[]{:S(2)}, u32[]{:S(2)}) collective-permute-start(f32[7,8,128]{2,1,0:T(8,128)S(1)} %get-tuple-element.52), channel_id=1, source_target_pairs={{0,16},{16,0},{1,17},{17,1},{2,18},{18,2},{3,19},{19,3},{4,20},{20... | collective-permute-start | bytes 86024 | tf_op jit(solution)/shard_map/ppermute | solution.py:550
  24.7 0.1 shard_map.77
  24.8 2.2 %collective-permute-done.9.side = f32[7,8,128]{2,1,0:T(8,128)S(1)} collective-permute-done((f32[7,8,128]{2,1,0:T(8,128)S(1)}, f32[7,8,128]{2,1,0:T(8,128)S(1)}, u32[]{:S(2)}, u32[]{:S(2)}) %collective-permute-start.9) | collective-permute-done | bytes 28704 | tf_op jit(solution)/shard_map/ppermute | solution.py:550
  27.1 4.4 %shard_map.78 = (f32[16,4,8,128]{3,2,1,0:T(8,128)S(1)}, f32[16,2,8,128]{3,2,1,0:T(8,128)S(1)}) custom-call(f32[16,4,8,128]{3,2,1,0:T(8,128)S(1)} %get-tuple-element.47.conc, f32[16,8,128]{2,1,0:T(8,128)S(1)} %collective-permute-done.5.x1, f32[16,8,128]{2,1,0:T(8,128)S(1)} %collective-permute-done.6.x2, f32[16,4,128]{2,1,0:T(4,128)S(1)} %collective-permute-done.7.y1, ...), custom_call_target="tpu_custom_call" | custom-call | tf_op jit(solution)/shard_map/pallas_call | solution.py:37
  31.4 1.6 %collective-permute-start.10 = (f32[16,2,8,128]{3,2,1,0:T(8,128)S(1)}, f32[16,2,8,128]{3,2,1,0:T(8,128)S(1)}, u32[]{:S(2)}, u32[]{:S(2)}) collective-permute-start(f32[16,2,8,128]{3,2,1,0:T(8,128)S(1)} %get-tuple-element.60), channel_id=1, source_target_pairs={{0,16},{16,0},{1,17},{17,1},{2,18},{18,2},{3,19},{19,3},{4,20},{20... | collective-permute-start | bytes 393224 | tf_op jit(solution)/shard_map/ppermute | solution.py:557
  33.0 3.5 %collective-permute-done.10.theirs = f32[16,2,8,128]{3,2,1,0:T(8,128)S(1)} collective-permute-done((f32[16,2,8,128]{3,2,1,0:T(8,128)S(1)}, f32[16,2,8,128]{3,2,1,0:T(8,128)S(1)}, u32[]{:S(2)}, u32[]{:S(2)}) %collective-permute-start.10) | collective-permute-done | bytes 131104 | tf_op jit(solution)/shard_map/ppermute | solution.py:557
  36.5 0.8 %shard_map.79 = f32[16,4,8,128]{3,2,1,0:T(8,128)} custom-call(f32[16,4,8,128]{3,2,1,0:T(8,128)S(1)} %get-tuple-element.59.mine, f32[16,2,8,128]{3,2,1,0:T(8,128)S(1)} %collective-permute-done.10.theirs), custom_call_target="tpu_custom_call" | custom-call | tf_op jit(solution)/shard_map/pallas_call | solution.py:37
  (15 shorter events, 0.0 us)
Async XLA Ops:
  0.0 5.8 %copy-start = (f32[2,3,1,4,8,128]{5,4,3,2,1,0:T(8,128)S(1)}, f32[2,3,1,4,8,128]{5,4,3,2,1,0:T(8,128)}, u32[]{:S(2)}) copy-start(f32[2,3,1,4,8,128]{5,4,3,2,1,0:T(8,128)} %wiener.1) | copy-start | bytes 294916
  0.0 5.8 %copy-start.1 = (f32[3,4,8,128]{3,2,1,0:T(8,128)S(1)}, f32[3,4,8,128]{3,2,1,0:T(8,128)}, u32[]{:S(2)}) copy-start(f32[3,4,8,128]{3,2,1,0:T(8,128)} %velocity.1) | copy-start | bytes 147460
  0.0 5.8 %copy-start.2 = (f32[4,8,128]{2,1,0:T(8,128)S(1)}, f32[4,8,128]{2,1,0:T(8,128)}, u32[]{:S(2)}) copy-start(f32[4,8,128]{2,1,0:T(8,128)} %mix_rate.1) | copy-start | bytes 49156
  1.1 7.2 %collective-permute-start = (f32[17,8,128]{2,1,0:T(8,128)S(1)}, f32[17,8,128]{2,1,0:T(8,128)S(1)}, u32[]{:S(2)}, u32[]{:S(2)}) collective-permute-start(f32[17,8,128]{2,1,0:T(8,128)S(1)} %get-tuple-element.34), channel_id=1, source_target_pairs={{0,4},{8,12},{4,0},{12,8},{1,5},{9,13},{5,1},{13,9},{2,6},{10,14},... | collective-permute-start | bytes 208904 | tf_op jit(solution)/shard_map/ppermute | solution.py:63
  4.2 4.1 %collective-permute-start.1 = (f32[17,8,128]{2,1,0:T(8,128)S(1)}, f32[17,8,128]{2,1,0:T(8,128)S(1)}, u32[]{:S(2)}, u32[]{:S(2)}) collective-permute-start(f32[17,8,128]{2,1,0:T(8,128)S(1)} %get-tuple-element.35), channel_id=1, source_target_pairs={{4,8},{5,9},{6,10},{7,11},{8,4},{9,5},{10,6},{11,7},{0,1},{1,0},{2... | collective-permute-start | bytes 208904 | tf_op jit(solution)/shard_map/ppermute | solution.py:58
  4.2 2.5 %collective-permute-start.2 = (f32[17,4,128]{2,1,0:T(4,128)S(1)}, f32[17,4,128]{2,1,0:T(4,128)S(1)}, u32[]{:S(2)}, u32[]{:S(2)}) collective-permute-start(f32[17,4,128]{2,1,0:T(4,128)S(1)} %get-tuple-element.36), channel_id=1, source_target_pairs={{0,1},{2,3},{1,0},{3,2},{4,5},{6,7},{5,4},{7,6},{8,9},{10,11},{9,8... | collective-permute-start | bytes 104456 | tf_op jit(solution)/shard_map/ppermute | solution.py:63
  4.7 3.5 %collective-permute-start.3 = (f32[17,4,128]{2,1,0:T(4,128)S(1)}, f32[17,4,128]{2,1,0:T(4,128)S(1)}, u32[]{:S(2)}, u32[]{:S(2)}) collective-permute-start(f32[17,4,128]{2,1,0:T(4,128)S(1)} %get-tuple-element.37), channel_id=1, source_target_pairs={{1,2},{2,1},{0,3},{3,0},{5,6},{6,5},{4,7},{7,4},{9,10},{10,9},{8,1... | collective-permute-start | bytes 104456 | tf_op jit(solution)/shard_map/ppermute | solution.py:63
  5.8 0.7 %copy-start.3 = (s32[64,4]{0,1:T(4,128)S(1)}, s32[64,4]{0,1:T(4,128)}, u32[]{:S(2)}) copy-start(s32[64,4]{0,1:T(4,128)} %param.13) | copy-start | bytes 3076
  5.8 0.7 %copy-start.4 = (f32[64]{0:T(128)S(1)}, f32[64]{0:T(128)}, u32[]{:S(2)}) copy-start(f32[64]{0:T(128)} %param.12) | copy-start | bytes 772
  8.8 5.6 %collective-permute-start.4 = (f32[16,2,8,128]{3,2,1,0:T(8,128)S(1)}, f32[16,2,8,128]{3,2,1,0:T(8,128)S(1)}, u32[]{:S(2)}, u32[]{:S(2)}) collective-permute-start(f32[16,2,8,128]{3,2,1,0:T(8,128)S(1)} %get-tuple-element.41), channel_id=1, source_target_pairs={{0,16},{16,0},{1,17},{17,1},{2,18},{18,2},{3,19},{19,3},{4,20},{20... | collective-permute-start | bytes 393224 | tf_op jit(solution)/shard_map/ppermute | solution.py:541
  18.6 8.4 %collective-permute-start.5 = (f32[16,8,128]{2,1,0:T(8,128)S(1)}, f32[16,8,128]{2,1,0:T(8,128)S(1)}, u32[]{:S(2)}, u32[]{:S(2)}) collective-permute-start(f32[16,8,128]{2,1,0:T(8,128)S(1)} %get-tuple-element.48), channel_id=1, source_target_pairs={{0,4},{8,12},{4,0},{12,8},{1,5},{9,13},{5,1},{13,9},{2,6},{10,14},... | collective-permute-start | bytes 196616 | tf_op jit(solution)/shard_map/ppermute | solution.py:63
  21.5 5.5 %collective-permute-start.6 = (f32[16,8,128]{2,1,0:T(8,128)S(1)}, f32[16,8,128]{2,1,0:T(8,128)S(1)}, u32[]{:S(2)}, u32[]{:S(2)}) collective-permute-start(f32[16,8,128]{2,1,0:T(8,128)S(1)} %get-tuple-element.49), channel_id=1, source_target_pairs={{4,8},{5,9},{6,10},{7,11},{8,4},{9,5},{10,6},{11,7},{0,1},{1,0},{2... | collective-permute-start | bytes 196616 | tf_op jit(solution)/shard_map/ppermute | solution.py:58
  21.5 5.5 %collective-permute-start.7 = (f32[16,4,128]{2,1,0:T(4,128)S(1)}, f32[16,4,128]{2,1,0:T(4,128)S(1)}, u32[]{:S(2)}, u32[]{:S(2)}) collective-permute-start(f32[16,4,128]{2,1,0:T(4,128)S(1)} %get-tuple-element.50), channel_id=1, source_target_pairs={{0,1},{2,3},{1,0},{3,2},{4,5},{6,7},{5,4},{7,6},{8,9},{10,11},{9,8... | collective-permute-start | bytes 98312 | tf_op jit(solution)/shard_map/ppermute | solution.py:63
  22.0 5.0 %collective-permute-start.8 = (f32[16,4,128]{2,1,0:T(4,128)S(1)}, f32[16,4,128]{2,1,0:T(4,128)S(1)}, u32[]{:S(2)}, u32[]{:S(2)}) collective-permute-start(f32[16,4,128]{2,1,0:T(4,128)S(1)} %get-tuple-element.51), channel_id=1, source_target_pairs={{1,2},{2,1},{0,3},{3,0},{5,6},{6,5},{4,7},{7,4},{9,10},{10,9},{8,1... | collective-permute-start | bytes 98312 | tf_op jit(solution)/shard_map/ppermute | solution.py:63
  23.2 3.9 %collective-permute-start.9 = (f32[7,8,128]{2,1,0:T(8,128)S(1)}, f32[7,8,128]{2,1,0:T(8,128)S(1)}, u32[]{:S(2)}, u32[]{:S(2)}) collective-permute-start(f32[7,8,128]{2,1,0:T(8,128)S(1)} %get-tuple-element.52), channel_id=1, source_target_pairs={{0,16},{16,0},{1,17},{17,1},{2,18},{18,2},{3,19},{19,3},{4,20},{20... | collective-permute-start | bytes 86024 | tf_op jit(solution)/shard_map/ppermute | solution.py:550
  31.4 5.0 %collective-permute-start.10 = (f32[16,2,8,128]{3,2,1,0:T(8,128)S(1)}, f32[16,2,8,128]{3,2,1,0:T(8,128)S(1)}, u32[]{:S(2)}, u32[]{:S(2)}) collective-permute-start(f32[16,2,8,128]{3,2,1,0:T(8,128)S(1)} %get-tuple-element.60), channel_id=1, source_target_pairs={{0,16},{16,0},{1,17},{17,1},{2,18},{18,2},{3,19},{19,3},{4,20},{20... | collective-permute-start | bytes 393224 | tf_op jit(solution)/shard_map/ppermute | solution.py:557
